TPU v7x, 32 devices: a whole 2x2x4 slice. The times are simulated.
32 devices in a mesh: lon: 8 (over y, x, core), lat: 4 (over z).
Axes of the slice: x: 2, y: 2, z: 4, core: 2. Of those that a mesh axis runs over, the one named last changes fastest.
Arguments:
- normed: bfloat16 [8, 96, 192, 192], P(None, 'lat', 'lon'), may hold values from -6 to 6
- cotangent: bfloat16 [8, 96, 192, 192], P(None, 'lat', 'lon'), may hold values from -6 to 6
- weight_qkv: bfloat16 [192, 576], replicated, may hold values from -0.4375 to 0.4375
- weight_proj: bfloat16 [192, 192], replicated, may hold values from -0.4375 to 0.4375
- bias_table: bfloat16 [64, 6, 20736], P('lat'), may hold values from -6 to 390
Outputs:
- input_grad: bfloat16 [8, 96, 192, 192], P(None, 'lat', 'lon')
- qkv_grad: float32 [192, 576], replicated
- proj_grad: float32 [192, 192], replicated
- bias_grad: float32 [64, 6, 20736], P('lat')
All inputs are finite; a program needn't handle non-finite values.
Results may differ from a plain program's by a relative error of at most 0.019.
Values may be sent and summed in bfloat16 or wider, within the bound.
A program may use at most 192 MiB of HBM per device.

v0:
```python
import functools
import math

import jax
import jax.numpy as jnp
from jax import lax
from jax.experimental import pallas as pl
from jax.experimental.pallas import tpu as pltpu
from jax.sharding import PartitionSpec as P

HEADS = 6
WIN_Z = 2
WIN_LAT = 6
WIN_LON = 12
WTOK = 144
LANES = 128
TAIL = WTOK - LANES
HALO = 8
CHUNKS = 1
UNROLL = 6
LOG2E = math.log2(math.e)
F32 = jnp.float32
BF16 = jnp.bfloat16


def ring_permute(block, axis, distance):
    size = lax.axis_size(axis)
    return lax.ppermute(block, axis, [((i - distance) % size, i) for i in range(size)])


def line_permute(block, axis, distance):
    size = lax.axis_size(axis)
    route = [(i - distance, i) for i in range(size) if 0 <= i - distance < size]
    return lax.ppermute(block, axis, route)


def mm(a, b, ca=1, cb=0):
    return lax.dot_general(a, b, (((ca,), (cb,)), ((), ())), preferred_element_type=F32)


def kernel(
    first_row,
    lat_windows,
    level_windows,
    lon_windows,
    last_ref,
    perm_ref,
    xa_ref,
    xb_ref,
    ca_ref,
    cb_ref,
    wqkv_ref,
    wproj_ref,
    bias_ref,
    gframe_ref,
    gqkv_ref,
    gproj_ref,
    gbias_ref,
    qm_s,
    mm_s,
    p_s,
    ds_s,
):
    step = pl.program_id(0)
    a = lax.rem(step, level_windows)
    b = step // level_windows + first_row
    channels = wqkv_ref.shape[0]
    head_dim = channels // HEADS
    scale = head_dim ** -0.5
    half = WIN_LAT * xa_ref.shape[2]

    @pl.when(step == 0)
    def _():
        gqkv_ref[...] = jnp.zeros_like(gqkv_ref)
        gproj_ref[...] = jnp.zeros_like(gproj_ref)

    perm = perm_ref[...]
    x_raw = jnp.concatenate(
        [xa_ref[...].reshape(half, channels), xb_ref[...].reshape(half, channels)], axis=0
    )
    c_raw = jnp.concatenate(
        [ca_ref[...].reshape(half, channels), cb_ref[...].reshape(half, channels)], axis=0
    )
    x = mm(perm, x_raw).astype(BF16)
    c = mm(perm, c_raw).astype(BF16)
    proj = mm(x, wqkv_ref[...]).astype(BF16)
    mgrad = mm(c, wproj_ref[...], 1, 1).astype(BF16)

    wrap_here = a == level_windows - 1
    dead_here = (b == lat_windows - 1) & (last_ref[0] == 1)
    per_level = WTOK // WIN_Z

    def classes(shape, dim):
        token = lax.broadcasted_iota(jnp.int32, shape, dim)
        upper = token >= per_level
        inner = jnp.where(upper, token - per_level, token)
        wrapped = jnp.where(upper & wrap_here, 2, 0)
        dead = jnp.where((inner >= per_level // 2) & dead_here, 1, 0)
        return wrapped + dead

    same = classes((WTOK, WTOK), 0) == classes((WTOK, WTOK), 1)
    mask_add = jnp.where(same, 0.0, -1e30)
    lane_head = lax.broadcasted_iota(jnp.int32, (1, channels), 1) // head_dim
    zero = jnp.zeros((), BF16)

    parts = []
    for w in range(lon_windows):
        rows = slice(w * WTOK, (w + 1) * WTOK)
        parts.append(
            (
                proj[rows, :channels],
                proj[rows, channels : 2 * channels],
                proj[rows, 2 * channels :],
                mgrad[rows],
            )
        )
    mixed = [jnp.zeros((WTOK, channels), F32) for _ in range(lon_windows)]
    dq = [jnp.zeros((WTOK, channels), F32) for _ in range(lon_windows)]
    for h in range(HEADS):
        hot = (lane_head == h).astype(BF16)
        hrows = slice(h * WTOK, (h + 1) * WTOK)
        shift = bias_ref[0, hrows, :].astype(F32) * LOG2E + mask_add
        gb = None
        for w in range(lon_windows):
            q, k, v, m = parts[w]
            qm = q * hot
            mg = m * hot
            qm_s[w, hrows, :] = qm
            mm_s[w, hrows, :] = mg
            s = mm(qm, k, 1, 1) * (scale * LOG2E) + shift
            dp = mm(mg, v, 1, 1)
            e = jnp.exp2(s - jnp.max(s, axis=1, keepdims=True))
            p = e * (1.0 / jnp.sum(e, axis=1, keepdims=True))
            delta = jnp.sum(p * dp, axis=1, keepdims=True)
            ds = p * (dp - delta)
            pb = p.astype(BF16)
            dsb = ds.astype(BF16)
            p_s[w, hrows, :] = pb
            ds_s[w, hrows, :] = dsb
            gb = ds if gb is None else gb + ds
            mixed[w] = mixed[w] + mm(pb, v * hot)
            dq[w] = dq[w] + mm(dsb, k * hot)
        gb = gb.astype(BF16)
        gbias_ref[0, hrows, :] = gb[:, :LANES]
        gbias_ref[0, HEADS * WTOK :, h * TAIL : (h + 1) * TAIL] = gb[:, LANES:]
    cols = []
    for w in range(lon_windows):
        dk = mm(ds_s[w], qm_s[w], 0, 0) * scale
        dv = mm(p_s[w], mm_s[w], 0, 0)
        cols.append(
            jnp.concatenate(
                [(dq[w] * scale).astype(BF16), dk.astype(BF16), dv.astype(BF16)], axis=1
            )
        )
    cols = jnp.concatenate(cols, axis=0)
    mixed_b = jnp.concatenate([t.astype(BF16) for t in mixed], axis=0)
    gproj_ref[...] += mm(mixed_b, c, 0, 0)
    gqkv_ref[...] += mm(x, cols, 0, 0)
    gin = mm(cols, wqkv_ref[...], 1, 1).astype(BF16)
    gout = mm(perm, gin, 0, 0).astype(BF16)
    gframe_ref[...] = gout.reshape(gframe_ref.shape)


def reduce_kernel(
    n, lats, gb_ref, wg_ref, out_ref, wout_ref, pair_s, send_s, recv_s, w1_s, w2_s,
    pair_sem, cross_sem, back_sem, fwd_sem, w1_sem, w2_sem, w3_sem,
):
    chips = n // 2
    me = lax.axis_index("lon")
    lat = lax.axis_index("lat")
    core = lax.rem(me, 2)
    chip = me // 2
    other = 1 - core
    partner = chip * 2 + other
    types = gb_ref.shape[0]
    share = types // n

    def piece(which, where):
        return pl.ds((which * chips + where) * share, share)

    def copy(src, dst, sems, out_at, in_at, device):
        return pltpu.make_async_remote_copy(
            src_ref=src,
            dst_ref=dst,
            send_sem=sems.at[0, out_at],
            recv_sem=sems.at[1, in_at],
            device_id=device,
            device_id_type=pl.DeviceIdType.MESH,
        )

    barrier = pltpu.get_barrier_semaphore()
    for o in range(1, n):
        pl.semaphore_signal(
            barrier, inc=1, device_id={"lon": lax.rem(me + o, n)},
            device_id_type=pl.DeviceIdType.MESH,
        )
    for o in range(1, lats):
        pl.semaphore_signal(
            barrier, inc=1, device_id={"lat": lax.rem(lat + o, lats)},
            device_id_type=pl.DeviceIdType.MESH,
        )
    pl.semaphore_wait(barrier, n + lats - 2)

    order = [(o, lax.rem(chip + o, chips)) for o in list(range(1, chips)) + [0]]
    sends = []
    first = []
    for o in range(1, n):
        p = lax.rem(me + o, n)
        cp = copy(wg_ref.at[p], w1_s.at[me], w1_sem, p, me, {"lon": p})
        cp.start()
        sends.append(cp)
    for o, j in order:
        cp = copy(gb_ref.at[piece(other, j)], pair_s.at[o], pair_sem, o, o, {"lon": partner})
        cp.start()
        first.append(cp)
    sends += first

    w1_s[pl.ds(me, 1)] = wg_ref[pl.ds(me, 1)]
    for o in range(1, n):
        p = lax.rem(me + o, n)
        copy(wg_ref.at[p], w1_s.at[p], w1_sem, p, p, {"lon": p}).wait_recv()
    w2_s[pl.ds(lat, 1)] = jnp.sum(w1_s[...].astype(F32), axis=0, keepdims=True).astype(BF16)
    for o in range(1, lats):
        p = lax.rem(lat + o, lats)
        cp = copy(w2_s.at[lat], w2_s.at[lat], w2_sem, p, lat, {"lat": p})
        cp.start()
        sends.append(cp)

    for cp, (o, j) in zip(first, order):
        cp.wait_recv()

        def add(i, _, o=o, j=j):
            mine = gb_ref[(core * chips + j) * share + i].astype(F32)
            total = (mine + pair_s[o, i].astype(F32)).astype(BF16)
            if o:
                send_s[o, i] = total
            else:
                recv_s[chip, i] = total
            return 0

        lax.fori_loop(0, share, add, 0)
        if o:
            cp2 = copy(
                send_s.at[o], recv_s.at[chip], cross_sem, o, chip, {"lon": j * 2 + core}
            )
            cp2.start()
            sends.append(cp2)

    for o in range(1, lats):
        p = lax.rem(lat + o, lats)
        copy(w2_s.at[p], w2_s.at[p], w2_sem, p, p, {"lat": p}).wait_recv()
    wout_ref[pl.ds(me, 1)] = jnp.sum(w2_s[...].astype(F32), axis=0, keepdims=True).astype(BF16)
    for o in range(1, n):
        p = lax.rem(me + o, n)
        cp = copy(wout_ref.at[me], wout_ref.at[me], w3_sem, p, me, {"lon": p})
        cp.start()
        sends.append(cp)

    for o in range(1, chips):
        j = lax.rem(chip + o, chips)
        copy(send_s.at[o], recv_s.at[j], cross_sem, o, j, {"lon": j * 2 + core}).wait_recv()

    def total(i, _):
        acc = recv_s[0, i].astype(F32)
        for j in range(1, chips):
            acc = acc + recv_s[j, i].astype(F32)
        out_ref[(core * chips + chip) * share + i] = acc.astype(BF16)
        return 0

    lax.fori_loop(0, share, total, 0)
    own = out_ref.at[piece(core, chip)]
    for o in range(1, chips):
        j = lax.rem(chip + o, chips)
        cp = copy(own, own, back_sem, j, chip, {"lon": j * 2 + core})
        cp.start()
        sends.append(cp)
    cp = copy(own, own, fwd_sem, chip, chip, {"lon": partner})
    cp.start()
    sends.append(cp)
    for o in range(1, chips):
        j = lax.rem(chip + o, chips)
        part = out_ref.at[piece(core, j)]
        copy(part, part, back_sem, j, j, {"lon": j * 2 + core}).wait_recv()
        cp = copy(part, part, fwd_sem, j, j, {"lon": partner})
        cp.start()
        sends.append(cp)
    for j in range(chips):
        part = out_ref.at[piece(other, j)]
        copy(part, part, fwd_sem, j, j, {"lon": partner}).wait_recv()
    for o in range(1, n):
        p = lax.rem(me + o, n)
        copy(wout_ref.at[p], wout_ref.at[p], w3_sem, p, p, {"lon": p}).wait_recv()
    for cp in sends:
        cp.wait_send()


def reduce_all(gbias, weights):
    n, lats = lax.axis_size("lon"), lax.axis_size("lat")
    chips = n // 2
    types, packed, lanes = gbias.shape
    rows, width = weights.shape
    share = types // n
    weights = weights.reshape(n, rows // n, width)
    vm = pl.BlockSpec(memory_space=pltpu.VMEM)
    sem = lambda k: pltpu.SemaphoreType.DMA((2, k))
    block = pltpu.VMEM((chips, share, packed, lanes), BF16)
    out, wout = pl.pallas_call(
        functools.partial(reduce_kernel, n, lats),
        in_specs=[vm, vm],
        out_specs=[vm, vm],
        out_shape=[
            jax.ShapeDtypeStruct(gbias.shape, BF16),
            jax.ShapeDtypeStruct(weights.shape, BF16),
        ],
        scratch_shapes=[
            block,
            block,
            block,
            pltpu.VMEM((n, rows // n, width), BF16),
            pltpu.VMEM((lats, rows // n, width), BF16),
            sem(chips),
            sem(chips),
            sem(chips),
            sem(chips),
            sem(n),
            sem(lats),
            sem(n),
        ],
        compiler_params=pltpu.CompilerParams(
            collective_id=0, has_side_effects=True, vmem_limit_bytes=40 * 2**20
        ),
        cost_estimate=pl.CostEstimate(
            flops=30_000_000_000, bytes_accessed=60_000_000, transcendentals=0
        ),
    )(gbias, weights)
    return out, wout.reshape(rows, width)


def unpack_kernel(packed_ref, out_ref, main_s, tail_s):
    stack = HEADS * WTOK
    main_s[...] = packed_ref[0, :stack].astype(F32)
    tails = packed_ref[0, stack:].astype(F32)
    for h in range(HEADS):
        turned = tails if h == 0 else pltpu.roll(tails, LANES - h * TAIL, 1)
        tail_s[h * WTOK : (h + 1) * WTOK] = turned
    group = LANES // TAIL
    lane = lax.broadcasted_iota(jnp.int32, (HEADS, LANES), 1)

    def body(m, _):
        before_main = before_tail = None
        for r in range(group + 1):
            tile = None
            if r < group:
                at = pl.ds(m * group + r, HEADS, stride=WTOK)
                here_main, here_tail = main_s[at, :], tail_s[at, :]
                if r:
                    here_main = pltpu.roll(here_main, TAIL * r, 1)
                    here_tail = pltpu.roll(here_tail, TAIL * r, 1)
                tile = here_main
            if r:
                ended = before_tail
                if r > 1:
                    ended = jnp.where(lane < TAIL * (r - 1), before_main, before_tail)
                tile = ended if r == group else jnp.where(lane < TAIL * r, ended, tile)
            start = pl.multiple_of(m * (group * WTOK) + r * LANES, LANES)
            out_ref[0, :, pl.ds(start, LANES)] = tile
            if r < group:
                before_main, before_tail = here_main, here_tail
        return 0

    def several(i, _):
        for u in range(UNROLL):
            body(i * UNROLL + u, 0)
        return 0

    lax.fori_loop(0, WTOK // group // UNROLL, several, 0)


def unpack(packed):
    kinds, rows, lanes = packed.shape
    stack = HEADS * WTOK
    return pl.pallas_call(
        unpack_kernel,
        grid=(kinds,),
        in_specs=[pl.BlockSpec((1, rows, lanes), lambda i: (i, 0, 0))],
        out_specs=pl.BlockSpec((1, HEADS, WTOK * WTOK), lambda i: (i, 0, 0)),
        out_shape=jax.ShapeDtypeStruct((kinds, HEADS, WTOK * WTOK), F32),
        scratch_shapes=[pltpu.VMEM((stack, LANES), F32), pltpu.VMEM((stack, LANES), F32)],
        cost_estimate=pl.CostEstimate(
            flops=10_000_000_000, bytes_accessed=15_000_000, transcendentals=0
        ),
    )(packed)


def window_call(chunk, last, perm, frame_in, frame_cot, weight_qkv, weight_proj, bias):
    levels, height, wide, channels = frame_in.shape
    level_windows = levels // WIN_Z
    lat_windows = height // WIN_LAT
    lon_windows = perm.shape[0] // WTOK
    rows_here = lat_windows // CHUNKS
    first = chunk * rows_here
    kinds = rows_here * level_windows

    def at(step, up):
        z = lax.rem(WIN_Z * lax.rem(step, level_windows) + up, levels)
        return z, step // level_windows + first, 0, 0

    tok = (1, WIN_LAT, wide, channels)
    low = pl.BlockSpec(tok, lambda i: at(i, 1))
    high = pl.BlockSpec(tok, lambda i: at(i, 2))
    whole = lambda arr: pl.BlockSpec(arr.shape, lambda i: (0,) * arr.ndim)
    const = lambda shape: pl.BlockSpec(shape, lambda i: (0,) * len(shape))
    stack = HEADS * WTOK
    packed = stack + WTOK
    return pl.pallas_call(
        functools.partial(kernel, first, lat_windows, level_windows, lon_windows),
        grid=(kinds,),
        in_specs=[
            pl.BlockSpec(memory_space=pltpu.SMEM),
            whole(perm),
            low,
            high,
            low,
            high,
            whole(weight_qkv),
            whole(weight_proj),
            pl.BlockSpec((1, stack, WTOK), lambda i: (i + first * level_windows, 0, 0)),
        ],
        out_specs=[
            pl.BlockSpec(
                (WIN_Z, WIN_LAT, wide, channels),
                lambda i: (lax.rem(i, level_windows), i // level_windows, 0, 0),
            ),
            const((channels, 3 * channels)),
            const((channels, channels)),
            pl.BlockSpec((1, packed, LANES), lambda i: (i, 0, 0)),
        ],
        out_shape=[
            jax.ShapeDtypeStruct((levels, rows_here * WIN_LAT, wide, channels), BF16),
            jax.ShapeDtypeStruct((channels, 3 * channels), F32),
            jax.ShapeDtypeStruct((channels, channels), F32),
            jax.ShapeDtypeStruct((kinds, packed, LANES), BF16),
        ],
        scratch_shapes=[
            pltpu.VMEM((lon_windows, stack, channels), BF16),
            pltpu.VMEM((lon_windows, stack, channels), BF16),
            pltpu.VMEM((lon_windows, stack, WTOK), BF16),
            pltpu.VMEM((lon_windows, stack, WTOK), BF16),
        ],
        compiler_params=pltpu.CompilerParams(
            dimension_semantics=("arbitrary",), vmem_limit_bytes=48 * 2**20
        ),
        cost_estimate=pl.CostEstimate(
            flops=kinds * 1_500_000_000, bytes_accessed=kinds * 2_000_000, transcendentals=0
        ),
    )(
        last, perm, frame_in, frame_in, frame_cot, frame_cot, weight_qkv, weight_proj, bias
    )


def local(normed, cotangent, weight_qkv, weight_proj, bias_table):
    levels, height, breadth, channels = normed.shape
    lat_shift = WIN_LAT // 2
    lon_shift = WIN_LON // 2
    lon_windows = breadth // WIN_LON
    wide = breadth + HALO
    across = ring_permute((normed[:, :, :HALO], cotangent[:, :, :HALO]), "lon", -1)
    wide_in = jnp.concatenate([normed, across[0]], axis=2)
    wide_cot = jnp.concatenate([cotangent, across[1]], axis=2)
    upward = line_permute((wide_in[:, :lat_shift], wide_cot[:, :lat_shift]), "lat", -1)
    frame_in = jnp.concatenate([wide_in[:, lat_shift:], upward[0]], axis=1)
    frame_cot = jnp.concatenate([wide_cot[:, lat_shift:], upward[1]], axis=1)
    last = (lax.axis_index("lat") == lax.axis_size("lat") - 1).astype(jnp.int32).reshape(1)
    bias = bias_table.reshape(bias_table.shape[0], HEADS * WTOK, WTOK)

    rows = jnp.arange(lon_windows * WTOK, dtype=jnp.int32)
    token = rows % WTOK
    per_level = WIN_LAT * WIN_LON
    source = (
        token // per_level * (WIN_LAT * wide)
        + token % per_level // WIN_LON * wide
        + rows // WTOK * WIN_LON
        + token % WIN_LON
        + lon_shift
    )
    columns = jnp.arange(WIN_Z * WIN_LAT * wide, dtype=jnp.int32)
    perm = (source[:, None] == columns[None, :]).astype(BF16)

    gframe, gqkv, gproj, gbias = window_call(
        0, last, perm, frame_in, frame_cot, weight_qkv, weight_proj, bias
    )
    weights = jnp.concatenate([gqkv, gproj], axis=1).astype(BF16)
    packed, weights = reduce_all(gbias, weights)
    weights = weights.astype(F32)

    gwide = jnp.roll(gframe, WIN_Z // 2, axis=0)
    side = ring_permute(gwide[:, :, breadth:], "lon", 1)
    seam = jnp.concatenate(
        [gwide[:, :, :HALO] + side, gwide[:, :, HALO:breadth]], axis=2
    )
    down = line_permute(seam[:, height - lat_shift :], "lat", 1)
    input_grad = jnp.concatenate([down, seam[:, : height - lat_shift]], axis=1)

    bias_grad = unpack(packed)
    return input_grad, weights[:, : 3 * channels], weights[:, 3 * channels :], bias_grad


def solution(mesh):
    in_specs = (
        P(None, "lat", "lon", None),
        P(None, "lat", "lon", None),
        P(),
        P(),
        P("lat", None, None),
    )
    out_specs = (P(None, "lat", "lon", None), P(), P(), P("lat", None, None))
    return jax.shard_map(local, mesh=mesh, in_specs=in_specs, out_specs=out_specs, check_vma=False)
```

profile of v0, /device:TPU:0, one launch (start us, length us, event | category | flops | bytes accessed | tf_op | source)
XLA Modules:
  0.0 256.1 jit_solution(760066687205548809)
XLA Ops:
  0.6 0.0 copy-start.6
  0.6 1.3 slice.47
  2.0 0.0 copy-start.7
  2.0 3.4 %collective-permute-start = (bf16[8,24,8,192]{3,2,1,0:T(8,128)(2,1)S(1)}, bf16[8,24,8,192]{3,2,1,0:T(8,128)(2,1)S(1)}, u32[]{:S(2)}, u32[]{:S(2)}) collective-permute-start(bf16[8,24,8,192]{3,2,1,0:T(8,128)(2,1)S(1)} %slice.47), channel_id=1, source_target_pairs={{4,0},{8,4},{12,8},{16,12},{20,16},{24,20},{28,24},{0,28},{5,1},{9... | collective-permute-start | bytes 1769480 | tf_op jit(solution)/shard_map/ppermute | solution.py:28
  5.4 1.2 slice.50
  6.6 0.7 collective-permute-start.2
  7.4 0.0 copy-done.6
  7.4 0.3 constant_dynamic-update-slice_fusion.1
  7.7 0.0 copy-done.7
  7.7 0.3 constant_dynamic-update-slice_fusion.3
  8.0 6.9 %collective-permute-done = bf16[8,24,8,192]{3,2,1,0:T(8,128)(2,1)S(1)} collective-permute-done((bf16[8,24,8,192]{3,2,1,0:T(8,128)(2,1)S(1)}, bf16[8,24,8,192]{3,2,1,0:T(8,128)(2,1)S(1)}, u32[]{:S(2)}, u32[]{:S(2)}) %collective-permute-start) | collective-permute-done | bytes 589856 | tf_op jit(solution)/shard_map/ppermute | solution.py:28
  14.9 0.1 constant_dynamic-update-slice_fusion
  15.0 0.0 copy-start.5
  15.0 0.8 slice.63
  15.9 1.3 collective-permute-start.1
  17.2 6.2 %collective-permute-done.2 = bf16[8,24,8,192]{3,2,1,0:T(8,128)(2,1)S(1)} collective-permute-done((bf16[8,24,8,192]{3,2,1,0:T(8,128)(2,1)S(1)}, bf16[8,24,8,192]{3,2,1,0:T(8,128)(2,1)S(1)}, u32[]{:S(2)}, u32[]{:S(2)}) %collective-permute-start.2) | collective-permute-done | bytes 589856 | tf_op jit(solution)/shard_map/ppermute | solution.py:28
  23.3 0.1 constant_dynamic-update-slice_fusion.2
  23.4 0.8 slice.65
  24.2 0.0 copy-done.5
  24.2 1.3 collective-permute-start.3
  25.5 0.1 fusion.4.perm_ref
  25.6 5.6 %copy.11 = bf16[16,6,20736]{2,1,0:T(8,128)(2,1)} copy(bf16[16,6,20736]{2,0,1:T(8,128)(2,1)} %param.9) | data formatting | bytes 7962624 | tf_op args[4]
  31.3 13.8 %reshape.76.bias_ref = bf16[16,864,144]{2,1,0:T(8,128)(2,1)} reshape(bf16[16,6,20736]{2,1,0:T(8,128)(2,1)} %copy.11) | data formatting | bytes 7962624 | tf_op jit(solution)/shard_map/reshape | solution.py:474
  45.1 2.0 slice.62
  47.2 0.3 slice.64
  47.4 0.0 collective-permute-done.1
  47.4 3.2 %pad_maximum_fusion.xa_ref.xb_ref = bf16[8,24,32,192]{3,2,1,0:T(8,128)(2,1)} fusion(bf16[8,3,32,192]{3,2,1,0:T(8,128)(2,1)} %collective-permute-done.1, bf16[8,21,32,192]{3,2,1,0:T(8,128)(2,1)S(1)} %slice.62), kind=kLoop, calls=%fused_computation.3 | loop fusion | flops 1179648 | bytes 4718592 | tf_op jit(solution)/shard_map/concatenate | solution.py:471
  50.6 0.0 copy-start
  50.6 0.0 copy-start.1
  50.6 0.0 collective-permute-done.3
  50.6 3.3 %pad_maximum_fusion.1.ca_ref.cb_ref = bf16[8,24,32,192]{3,2,1,0:T(8,128)(2,1)} fusion(bf16[8,3,32,192]{3,2,1,0:T(8,128)(2,1)} %collective-permute-done.3, bf16[8,21,32,192]{3,2,1,0:T(8,128)(2,1)S(1)} %slice.64), kind=kLoop, calls=%fused_computation.4 | loop fusion | flops 1179648 | bytes 4718592 | tf_op jit(solution)/shard_map/concatenate | solution.py:472
  53.9 0.0 copy-done
  53.9 0.0 copy-done.1
  53.9 98.8 %shard_map.84 = (bf16[8,24,32,192]{3,2,1,0:T(8,128)(2,1)S(1)}, f32[192,576]{1,0:T(8,128)S(1)}, f32[192,192]{1,0:T(8,128)S(1)}, bf16[16,1008,128]{2,1,0:T(8,128)(2,1)}) custom-call(s32[1]{0:T(128)} %bitcast.last_ref, bf16[288,384]{1,0:T(8,128)(2,1)S(1)} %fusion.4.perm_ref, bf16[8,24,32,192]{3,2,1,0:T(8,128)(2,1)} %pad_maximum_fusion.xa_ref.xb_ref, ...), custom_call_target="tpu_custom_call" | custom-call | flops 24000000000 | bytes 32000000 | tf_op jit(solution)/shard_map/pallas_call | solution.py:415
  152.7 0.3 slice.54
  153.0 0.0 copy-start.3
  153.1 1.1 pad_maximum_fusion.3
  154.2 0.3 collective-permute-start.4
  154.5 0.1 pad_maximum_fusion.4.wg_ref
  154.6 0.9 copy-done.3
  155.5 66.6 %shard_map.85 = (bf16[16,1008,128]{2,1,0:T(8,128)(2,1)S(1)}, bf16[8,24,768]{2,1,0:T(8,128)(2,1)S(1)}) custom-call(bf16[16,1008,128]{2,1,0:T(8,128)(2,1)S(1)} %copy-done.3, bf16[8,24,768]{2,1,0:T(8,128)(2,1)S(1)} %pad_maximum_fusion.4.wg_ref), custom_call_target="tpu_custom_call" | custom-call | flops 30000001024 | bytes 60000000 | tf_op jit(solution)/shard_map/pallas_call | solution.py:307
  222.1 0.0 copy-start.2
  222.1 2.0 copy-done.2
  224.1 16.0 %shard_map.86 = f32[16,6,20736]{2,1,0:T(8,128)} custom-call(bf16[16,1008,128]{2,1,0:T(8,128)(2,1)} %copy-done.2), custom_call_target="tpu_custom_call" | custom-call | flops 10000000000 | bytes 15000000 | tf_op jit(solution)/shard_map/pallas_call | solution.py:382
  240.1 0.0 collective-permute-done.4
  240.1 0.0 copy-start.4
  240.1 1.6 maximum_add_fusion
  241.7 0.6 fusion.3
  242.3 4.5 %collective-permute-start.5 = (bf16[8,3,24,192]{3,2,1,0:T(8,128)(2,1)S(1)}, bf16[8,3,24,192]{3,2,1,0:T(8,128)(2,1)S(1)}, u32[]{:S(2)}, u32[]{:S(2)}) collective-permute-start(bf16[8,3,24,192]{3,2,1,0:T(8,128)(2,1)S(1)} %slice.66), channel_id=1, source_target_pairs={{0,1},{1,2},{2,3},{4,5},{5,6},{6,7},{8,9},{9,10},{10,11},{12,13},{... | collective-permute-start | bytes 663560 | tf_op jit(solution)/shard_map/ppermute | solution.py:34
  246.8 0.1 bitcast_convert_fusion
  246.9 0.8 slice.69
  247.7 0.8 slice.68
  248.5 0.0 copy-done.4
  248.5 5.7 %copy.12 = f32[16,6,20736]{2,0,1:T(8,128)} copy(f32[16,6,20736]{2,1,0:T(8,128)S(1)} %copy-done.4) | data formatting | bytes 15925248
  254.2 0.1 slice.67
  254.3 0.0 collective-permute-done.5
  254.3 1.8 pad_maximum_fusion.2
  (5 shorter events, 0.1 us)
Async XLA Ops:
  0.6 6.7 %copy-start.6 = (bf16[8,24,24,192]{3,2,1,0:T(8,128)(2,1)S(1)}, bf16[8,24,24,192]{3,2,1,0:T(8,128)(2,1)}, u32[]{:S(2)}) copy-start(bf16[8,24,24,192]{3,2,1,0:T(8,128)(2,1)} %param.5) | copy-start | bytes 5308420
  2.0 5.7 %copy-start.7 = (bf16[8,24,24,192]{3,2,1,0:T(8,128)(2,1)S(1)}, bf16[8,24,24,192]{3,2,1,0:T(8,128)(2,1)}, u32[]{:S(2)}) copy-start(bf16[8,24,24,192]{3,2,1,0:T(8,128)(2,1)} %param.6) | copy-start | bytes 5308420
  2.0 12.9 %collective-permute-start = (bf16[8,24,8,192]{3,2,1,0:T(8,128)(2,1)S(1)}, bf16[8,24,8,192]{3,2,1,0:T(8,128)(2,1)S(1)}, u32[]{:S(2)}, u32[]{:S(2)}) collective-permute-start(bf16[8,24,8,192]{3,2,1,0:T(8,128)(2,1)S(1)} %slice.47), channel_id=1, source_target_pairs={{4,0},{8,4},{12,8},{16,12},{20,16},{24,20},{28,24},{0,28},{5,1},{9... | collective-permute-start | bytes 1769480 | tf_op jit(solution)/shard_map/ppermute | solution.py:28
  6.6 16.7 %collective-permute-start.2 = (bf16[8,24,8,192]{3,2,1,0:T(8,128)(2,1)S(1)}, bf16[8,24,8,192]{3,2,1,0:T(8,128)(2,1)S(1)}, u32[]{:S(2)}, u32[]{:S(2)}) collective-permute-start(bf16[8,24,8,192]{3,2,1,0:T(8,128)(2,1)S(1)} %slice.50), channel_id=1, source_target_pairs={{4,0},{8,4},{12,8},{16,12},{20,16},{24,20},{28,24},{0,28},{5,1},{9... | collective-permute-start | bytes 1769480 | tf_op jit(solution)/shard_map/ppermute | solution.py:28
  15.0 9.2 %copy-start.5 = (bf16[8,24,32,192]{3,2,1,0:T(8,128)(2,1)}, bf16[8,24,32,192]{3,2,1,0:T(8,128)(2,1)S(1)}, u32[]{:S(2)}) copy-start(bf16[8,24,32,192]{3,2,1,0:T(8,128)(2,1)S(1)} %constant_dynamic-update-slice_fusion) | copy-start | bytes 7077892
  15.9 31.6 %collective-permute-start.1 = (bf16[8,3,32,192]{3,2,1,0:T(8,128)(2,1)}, bf16[8,3,32,192]{3,2,1,0:T(8,128)(2,1)}, u32[]{:S(2)}, u32[]{:S(2)}) collective-permute-start(bf16[8,3,32,192]{3,2,1,0:T(8,128)(2,1)} %slice.63), channel_id=1, source_target_pairs={{1,0},{2,1},{3,2},{5,4},{6,5},{7,6},{9,8},{10,9},{11,10},{13,12},{... | collective-permute-start | bytes 884744 | tf_op jit(solution)/shard_map/ppermute | solution.py:34
  24.2 26.4 %collective-permute-start.3 = (bf16[8,3,32,192]{3,2,1,0:T(8,128)(2,1)}, bf16[8,3,32,192]{3,2,1,0:T(8,128)(2,1)}, u32[]{:S(2)}, u32[]{:S(2)}) collective-permute-start(bf16[8,3,32,192]{3,2,1,0:T(8,128)(2,1)} %slice.65), channel_id=1, source_target_pairs={{1,0},{2,1},{3,2},{5,4},{6,5},{7,6},{9,8},{10,9},{11,10},{13,12},{... | collective-permute-start | bytes 884744 | tf_op jit(solution)/shard_map/ppermute | solution.py:34
  50.6 3.3 %copy-start = (bf16[192,576]{1,0:T(8,128)(2,1)S(1)}, bf16[192,576]{1,0:T(8,128)(2,1)}, u32[]{:S(2)}) copy-start(bf16[192,576]{1,0:T(8,128)(2,1)} %wqkv_ref.1) | copy-start | bytes 663556
  50.6 3.3 %copy-start.1 = (bf16[192,192]{1,0:T(8,128)(2,1)S(1)}, bf16[192,192]{1,0:T(8,128)(2,1)}, u32[]{:S(2)}) copy-start(bf16[192,192]{1,0:T(8,128)(2,1)} %wproj_ref.1) | copy-start | bytes 221188
  153.0 2.5 copy-start.3
  154.2 85.9 %collective-permute-start.4 = (bf16[8,24,8,192]{3,2,1,0:T(8,128)(2,1)}, bf16[8,24,8,192]{3,2,1,0:T(8,128)(2,1)}, u32[]{:S(2)}, u32[]{:S(2)}) collective-permute-start(bf16[8,24,8,192]{3,2,1,0:T(8,128)(2,1)} %pad_maximum_fusion.3), channel_id=1, source_target_pairs={{28,0},{0,4},{4,8},{8,12},{12,16},{16,20},{20,24},{24,28},{29,1},{... | collective-permute-start | bytes 1769480 | tf_op jit(solution)/shard_map/ppermute | solution.py:28
  222.1 2.0 copy-start.2
  240.1 8.4 %copy-start.4 = (f32[16,6,20736]{2,1,0:T(8,128)S(1)}, f32[16,6,20736]{2,1,0:T(8,128)}, u32[]{:S(2)}) copy-start(f32[16,6,20736]{2,1,0:T(8,128)} %shard_map.86) | copy-start | bytes 23887876
  242.3 12.1 %collective-permute-start.5 = (bf16[8,3,24,192]{3,2,1,0:T(8,128)(2,1)S(1)}, bf16[8,3,24,192]{3,2,1,0:T(8,128)(2,1)S(1)}, u32[]{:S(2)}, u32[]{:S(2)}) collective-permute-start(bf16[8,3,24,192]{3,2,1,0:T(8,128)(2,1)S(1)} %slice.66), channel_id=1, source_target_pairs={{0,1},{1,2},{2,3},{4,5},{5,6},{6,7},{8,9},{9,10},{10,11},{12,13},{... | collective-permute-start | bytes 663560 | tf_op jit(solution)/shard_map/ppermute | solution.py:34
where the time goes:
time: 257 us; the launch traced here: 256 us
  Pallas kernels  181 us (70%)
  local copies, waits for them, and re-layouts  37.4 us (15%)
  waiting for transfers between devices  13.1 us (5%)
  other arithmetic  11.8 us (5%)
  starting transfers between devices  11.5 us (4%)
    pallas_call x1, Pallas kernels, window_call(): pl.pallas_call(functools.partial(kernel, first, lat_windows, level_window...  98.8 us
    pallas_call x1, Pallas kernels, reduce_all(): pl.pallas_call(functools.partial(reduce_kernel, n, lats), in_specs=[vm, v...  66.6 us
    pallas_call x1, Pallas kernels, unpack(): pl.pallas_call(unpack_kernel, grid=(kinds,), in_specs=[pl.BlockSpec((1, r...  16 us
    unnamed x20, local copies, waits for them, and re-layouts  14.8 us
    reshape x1, local copies, waits for them, and re-layouts, local(): bias = bias_table.reshape(bias_table.shape[0], HEADS * WTOK, WTOK)  13.8 us
    ppermute x3, waiting for transfers between devices, ring_permute(): lax.ppermute(block, axis, [((i - distance) % size, i) for i in range(size)])  13.1 us
    ppermute x3, starting transfers between devices, line_permute(): return lax.ppermute(block, axis, route)  7.11 us
  transfers between devices with their start and end apart: 6, of which 2 were waited for; matrix products, arithmetic and copies ran while one was open for 14% of the time, Pallas kernels for 32%

commit v1 on v0

v1 whole, which is shorter than its diff:
```python
import functools
import math

import jax
import jax.numpy as jnp
from jax import lax
from jax.experimental import pallas as pl
from jax.experimental.pallas import tpu as pltpu
from jax.sharding import PartitionSpec as P

HEADS = 6
WIN_Z = 2
WIN_LAT = 6
WIN_LON = 12
WTOK = 144
LANES = 128
TAIL = WTOK - LANES
HALO = 8
PACKED = 1024
UNROLL = 6
LOG2E = math.log2(math.e)
F32 = jnp.float32
BF16 = jnp.bfloat16


def ring_permute(block, axis, distance):
    size = lax.axis_size(axis)
    return lax.ppermute(block, axis, [((i - distance) % size, i) for i in range(size)])


def line_permute(block, axis, distance):
    size = lax.axis_size(axis)
    route = [(i - distance, i) for i in range(size) if 0 <= i - distance < size]
    return lax.ppermute(block, axis, route)


def mm(a, b, ca=1, cb=0):
    return lax.dot_general(a, b, (((ca,), (cb,)), ((), ())), preferred_element_type=F32)


class Exchange:
    def __init__(self, n, kinds, bufs, sems):
        self.n, self.kinds = n, kinds
        self.chips = n // 2
        self.gb, self.pair, self.sum, self.cross, self.out, self.hbm = bufs
        self.pair_sem, self.cross_sem, self.back_sem, self.fwd_sem, self.store_sem = sems
        me = lax.axis_index("lon")
        self.me = me
        self.core = lax.rem(me, 2)
        self.chip = me // 2
        self.other = 1 - self.core
        self.partner = self.chip * 2 + self.other
        self.half = PACKED // 2
        self.part = self.half // self.chips

    def remote(self, src, dst, send, recv, device):
        return pltpu.make_async_remote_copy(
            src_ref=src, dst_ref=dst, send_sem=send, recv_sem=recv,
            device_id={"lon": device}, device_id_type=pl.DeviceIdType.MESH,
        )

    def peer(self, o):
        return lax.rem(self.chip + o, self.chips)

    def rows(self, core, chip):
        return pl.ds(core * self.half + chip * self.part, self.part)

    def pair_copy(self, t):
        src = self.gb.at[t, pl.ds(self.other * self.half, self.half)]
        return self.remote(
            src, self.pair.at[t], self.pair_sem.at[0, t], self.pair_sem.at[1, t], self.partner
        )

    def cross_copy(self, t, o, arriving):
        j = self.peer(o)
        src = self.sum.at[t, pl.ds(j * self.part, self.part)]
        slot = j if arriving else self.chip
        return self.remote(
            src, self.cross.at[t, slot], self.cross_sem.at[0, t, j],
            self.cross_sem.at[1, t, slot], j * 2 + self.core,
        )

    def back_copy(self, t, o, arriving):
        j = self.peer(o)
        slot = j if arriving else self.chip
        part = self.out.at[t, self.rows(self.core, slot)]
        return self.remote(
            part, part, self.back_sem.at[0, t, j], self.back_sem.at[1, t, slot],
            j * 2 + self.core,
        )

    def fwd_copy(self, t, j, arriving):
        part = self.out.at[t, self.rows(self.other if arriving else self.core, j)]
        return self.remote(
            part, part, self.fwd_sem.at[0, t, j], self.fwd_sem.at[1, t, j], self.partner
        )

    def store(self, t):
        return pltpu.make_async_copy(self.out.at[t], self.hbm.at[t], self.store_sem.at[t])

    def stage_pair(self, t):
        self.pair_copy(t).wait_recv()
        mine = self.gb[t, pl.ds(self.core * self.half, self.half)].astype(F32)
        total = (mine + self.pair[t].astype(F32)).astype(BF16)
        self.sum[t] = total
        for o in range(1, self.chips):
            self.cross_copy(t, o, False).start()

    def stage_cross(self, t):
        for o in range(1, self.chips):
            self.cross_copy(t, o, True).wait_recv()
        acc = self.sum[t, pl.ds(self.chip * self.part, self.part)].astype(F32)
        for o in range(1, self.chips):
            acc = acc + self.cross[t, self.peer(o)].astype(F32)
        self.out[t, self.rows(self.core, self.chip)] = acc.astype(BF16)
        for o in range(1, self.chips):
            self.back_copy(t, o, False).start()
        self.fwd_copy(t, self.chip, False).start()

    def stage_back(self, t):
        for o in range(1, self.chips):
            self.back_copy(t, o, True).wait_recv()
            self.fwd_copy(t, self.peer(o), False).start()

    def stage_fwd(self, t):
        for j in range(self.chips):
            self.fwd_copy(t, j, True).wait_recv()
        self.store(t).start()

    def stages(self):
        return [self.stage_pair, self.stage_cross, self.stage_back, self.stage_fwd]

    def behind(self, step):
        for d, stage in enumerate(self.stages()):
            t = step - 1 - d
            if isinstance(t, int):
                if 0 <= t < self.kinds:
                    stage(t)
            else:
                pl.when(t >= 0)(functools.partial(stage, t))

    def drain(self):
        def body(t, _):
            self.pair_copy(t).wait_send()
            for o in range(1, self.chips):
                self.cross_copy(t, o, False).wait_send()
                self.back_copy(t, o, False).wait_send()
            for j in range(self.chips):
                self.fwd_copy(t, j, False).wait_send()
            self.store(t).wait()
            return 0

        lax.fori_loop(0, self.kinds, body, 0)


def enter(n, lats):
    me, lat = lax.axis_index("lon"), lax.axis_index("lat")
    barrier = pltpu.get_barrier_semaphore()
    for o in range(1, n):
        pl.semaphore_signal(
            barrier, inc=1, device_id={"lon": lax.rem(me + o, n)},
            device_id_type=pl.DeviceIdType.MESH,
        )
    for o in range(1, lats):
        pl.semaphore_signal(
            barrier, inc=1, device_id={"lat": lax.rem(lat + o, lats)},
            device_id_type=pl.DeviceIdType.MESH,
        )
    pl.semaphore_wait(barrier, n + lats - 2)


class WeightSum:
    def __init__(self, n, lats, wg, w1, w2, wout, sems):
        self.n, self.lats = n, lats
        self.wg, self.w1, self.w2, self.wout = wg, w1, w2, wout
        self.s1, self.s2, self.s3 = sems
        self.me, self.lat = lax.axis_index("lon"), lax.axis_index("lat")

    def remote(self, src, dst, sems, out_at, in_at, device):
        return pltpu.make_async_remote_copy(
            src_ref=src, dst_ref=dst, send_sem=sems.at[0, out_at], recv_sem=sems.at[1, in_at],
            device_id=device, device_id_type=pl.DeviceIdType.MESH,
        )

    def first(self, o, arriving):
        p = lax.rem(self.me + o, self.n)
        slot = p if arriving else self.me
        return self.remote(self.wg.at[p], self.w1.at[slot], self.s1, p, slot, {"lon": p})

    def second(self, o, arriving):
        p = lax.rem(self.lat + o, self.lats)
        slot = p if arriving else self.lat
        return self.remote(self.w2.at[slot], self.w2.at[slot], self.s2, p, slot, {"lat": p})

    def third(self, o, arriving):
        p = lax.rem(self.me + o, self.n)
        slot = p if arriving else self.me
        return self.remote(self.wout.at[slot], self.wout.at[slot], self.s3, p, slot, {"lon": p})

    def start(self):
        for o in range(1, self.n):
            self.first(o, False).start()
        self.w1[pl.ds(self.me, 1)] = self.wg[pl.ds(self.me, 1)]

    def step_one(self):
        for o in range(1, self.n):
            self.first(o, True).wait_recv()
        total = jnp.sum(self.w1[...].astype(F32), axis=0, keepdims=True)
        self.w2[pl.ds(self.lat, 1)] = total.astype(BF16)
        for o in range(1, self.lats):
            self.second(o, False).start()

    def step_two(self):
        for o in range(1, self.lats):
            self.second(o, True).wait_recv()
        total = jnp.sum(self.w2[...].astype(F32), axis=0, keepdims=True)
        self.wout[pl.ds(self.me, 1)] = total.astype(BF16)
        for o in range(1, self.n):
            self.third(o, False).start()

    def finish(self):
        for o in range(1, self.n):
            self.third(o, True).wait_recv()
        for o in range(1, self.n):
            self.first(o, False).wait_send()
            self.third(o, False).wait_send()
        for o in range(1, self.lats):
            self.second(o, False).wait_send()


def kernel(
    n,
    lats,
    kinds,
    lat_windows,
    level_windows,
    lon_windows,
    last_ref,
    perm_ref,
    xa_ref,
    xb_ref,
    ca_ref,
    cb_ref,
    wqkv_ref,
    wproj_ref,
    bias_ref,
    gframe_ref,
    wout_ref,
    gbias_hbm,
    qm_s,
    mm_s,
    p_s,
    ds_s,
    gqkv_ref,
    gproj_ref,
    gbias_ref,
    pair_s,
    sum_s,
    cross_s,
    red_s,
    wg_s,
    w1_s,
    w2_s,
    w3_s,
    pair_sem,
    cross_sem,
    back_sem,
    fwd_sem,
    store_sem,
    w1_sem,
    w2_sem,
    w3_sem,
):
    step = pl.program_id(0)
    a = lax.rem(step, level_windows)
    b = step // level_windows
    channels = wqkv_ref.shape[0]
    head_dim = channels // HEADS
    scale = head_dim ** -0.5
    half = WIN_LAT * xa_ref.shape[2]

    @pl.when(step == 0)
    def _():
        gqkv_ref[...] = jnp.zeros_like(gqkv_ref)
        gproj_ref[...] = jnp.zeros_like(gproj_ref)
        gbias_ref[:, HEADS * WTOK :, :] = jnp.zeros((kinds, PACKED - HEADS * WTOK, LANES), BF16)
        enter(n, lats)

    ex = Exchange(
        n, kinds,
        (gbias_ref, pair_s, sum_s, cross_s, red_s, gbias_hbm),
        (pair_sem, cross_sem, back_sem, fwd_sem, store_sem),
    )
    ex.behind(step)

    perm = perm_ref[...]
    x_raw = jnp.concatenate(
        [xa_ref[...].reshape(half, channels), xb_ref[...].reshape(half, channels)], axis=0
    )
    c_raw = jnp.concatenate(
        [ca_ref[...].reshape(half, channels), cb_ref[...].reshape(half, channels)], axis=0
    )
    x = mm(perm, x_raw).astype(BF16)
    c = mm(perm, c_raw).astype(BF16)
    proj = mm(x, wqkv_ref[...]).astype(BF16)
    mgrad = mm(c, wproj_ref[...], 1, 1).astype(BF16)

    wrap_here = a == level_windows - 1
    dead_here = (b == lat_windows - 1) & (last_ref[0] == 1)
    per_level = WTOK // WIN_Z

    def classes(shape, dim):
        token = lax.broadcasted_iota(jnp.int32, shape, dim)
        upper = token >= per_level
        inner = jnp.where(upper, token - per_level, token)
        wrapped = jnp.where(upper & wrap_here, 2, 0)
        dead = jnp.where((inner >= per_level // 2) & dead_here, 1, 0)
        return wrapped + dead

    same = classes((WTOK, WTOK), 0) == classes((WTOK, WTOK), 1)
    mask_add = jnp.where(same, 0.0, -1e30)
    lane_head = lax.broadcasted_iota(jnp.int32, (1, channels), 1) // head_dim
    zero = jnp.zeros((), BF16)

    parts = []
    for w in range(lon_windows):
        rows = slice(w * WTOK, (w + 1) * WTOK)
        parts.append(
            (
                proj[rows, :channels],
                proj[rows, channels : 2 * channels],
                proj[rows, 2 * channels :],
                mgrad[rows],
            )
        )
    mixed = [jnp.zeros((WTOK, channels), F32) for _ in range(lon_windows)]
    dq = [jnp.zeros((WTOK, channels), F32) for _ in range(lon_windows)]
    for h in range(HEADS):
        hot = (lane_head == h).astype(BF16)
        hrows = slice(h * WTOK, (h + 1) * WTOK)
        shift = bias_ref[0, hrows, :].astype(F32) * LOG2E + mask_add
        gb = None
        for w in range(lon_windows):
            q, k, v, m = parts[w]
            qm = q * hot
            mg = m * hot
            qm_s[w, hrows, :] = qm
            mm_s[w, hrows, :] = mg
            s = mm(qm, k, 1, 1) * (scale * LOG2E) + shift
            dp = mm(mg, v, 1, 1)
            e = jnp.exp2(s - jnp.max(s, axis=1, keepdims=True))
            p = e * (1.0 / jnp.sum(e, axis=1, keepdims=True))
            delta = jnp.sum(p * dp, axis=1, keepdims=True)
            ds = p * (dp - delta)
            pb = p.astype(BF16)
            dsb = ds.astype(BF16)
            p_s[w, hrows, :] = pb
            ds_s[w, hrows, :] = dsb
            gb = ds if gb is None else gb + ds
            mixed[w] = mixed[w] + mm(pb, v * hot)
            dq[w] = dq[w] + mm(dsb, k * hot)
        gb = gb.astype(BF16)
        gbias_ref[step, hrows, :] = gb[:, :LANES]
        gbias_ref[step, HEADS * WTOK : HEADS * WTOK + WTOK, h * TAIL : (h + 1) * TAIL] = gb[:, LANES:]
    cols = []
    for w in range(lon_windows):
        dk = mm(ds_s[w], qm_s[w], 0, 0) * scale
        dv = mm(p_s[w], mm_s[w], 0, 0)
        cols.append(
            jnp.concatenate(
                [(dq[w] * scale).astype(BF16), dk.astype(BF16), dv.astype(BF16)], axis=1
            )
        )
    cols = jnp.concatenate(cols, axis=0)
    mixed_b = jnp.concatenate([t.astype(BF16) for t in mixed], axis=0)
    gproj_ref[...] += mm(mixed_b, c, 0, 0)
    gqkv_ref[...] += mm(x, cols, 0, 0)
    gin = mm(cols, wqkv_ref[...], 1, 1).astype(BF16)
    gout = mm(perm, gin, 0, 0).astype(BF16)
    gframe_ref[...] = gout.reshape(gframe_ref.shape)
    ex.pair_copy(step).start()

    @pl.when(step == kinds - 1)
    def _():
        share = channels // n
        for i in range(n):
            rows = slice(i * share, (i + 1) * share)
            wg_s[i, :, : 3 * channels] = gqkv_ref[rows].astype(BF16)
            wg_s[i, :, 3 * channels :] = gproj_ref[rows].astype(BF16)
        ws = WeightSum(n, lats, wg_s, w1_s, w2_s, w3_s, (w1_sem, w2_sem, w3_sem))
        ws.start()
        ex.behind(kinds)
        ws.step_one()
        ex.behind(kinds + 1)
        ws.step_two()
        ex.behind(kinds + 2)
        ex.behind(kinds + 3)
        ws.finish()
        wout_ref[...] = w3_s[...]
        ex.drain()


def unpack_kernel(packed_ref, out_ref, main_s, tail_s):
    stack = HEADS * WTOK
    main_s[...] = packed_ref[0, :stack].astype(F32)
    tails = packed_ref[0, stack : stack + WTOK].astype(F32)
    for h in range(HEADS):
        turned = tails if h == 0 else pltpu.roll(tails, LANES - h * TAIL, 1)
        tail_s[h * WTOK : (h + 1) * WTOK] = turned
    group = LANES // TAIL
    lane = lax.broadcasted_iota(jnp.int32, (HEADS, LANES), 1)

    def body(m, _):
        before_main = before_tail = None
        for r in range(group + 1):
            tile = None
            if r < group:
                at = pl.ds(m * group + r, HEADS, stride=WTOK)
                here_main, here_tail = main_s[at, :], tail_s[at, :]
                if r:
                    here_main = pltpu.roll(here_main, TAIL * r, 1)
                    here_tail = pltpu.roll(here_tail, TAIL * r, 1)
                tile = here_main
            if r:
                ended = before_tail
                if r > 1:
                    ended = jnp.where(lane < TAIL * (r - 1), before_main, before_tail)
                tile = ended if r == group else jnp.where(lane < TAIL * r, ended, tile)
            start = pl.multiple_of(m * (group * WTOK) + r * LANES, LANES)
            out_ref[0, :, pl.ds(start, LANES)] = tile
            if r < group:
                before_main, before_tail = here_main, here_tail
        return 0

    def several(i, _):
        for u in range(UNROLL):
            body(i * UNROLL + u, 0)
        return 0

    lax.fori_loop(0, WTOK // group // UNROLL, several, 0)


def unpack(packed):
    kinds, rows, lanes = packed.shape
    stack = HEADS * WTOK
    return pl.pallas_call(
        unpack_kernel,
        grid=(kinds,),
        in_specs=[pl.BlockSpec((1, rows, lanes), lambda i: (i, 0, 0))],
        out_specs=pl.BlockSpec((1, HEADS, WTOK * WTOK), lambda i: (i, 0, 0)),
        out_shape=jax.ShapeDtypeStruct((kinds, HEADS, WTOK * WTOK), F32),
        scratch_shapes=[pltpu.VMEM((stack, LANES), F32), pltpu.VMEM((stack, LANES), F32)],
        cost_estimate=pl.CostEstimate(
            flops=10_000_000_000, bytes_accessed=15_000_000, transcendentals=0
        ),
    )(packed)


def window_call(last, perm, frame_in, frame_cot, weight_qkv, weight_proj, bias):
    levels, height, wide, channels = frame_in.shape
    level_windows = levels // WIN_Z
    lat_windows = height // WIN_LAT
    lon_windows = perm.shape[0] // WTOK
    kinds = lat_windows * level_windows
    n, lats = lax.axis_size("lon"), lax.axis_size("lat")
    chips = n // 2

    def at(step, up):
        z = lax.rem(WIN_Z * lax.rem(step, level_windows) + up, levels)
        return z, step // level_windows, 0, 0

    tok = (1, WIN_LAT, wide, channels)
    low = pl.BlockSpec(tok, lambda i: at(i, 1))
    high = pl.BlockSpec(tok, lambda i: at(i, 2))
    whole = lambda arr: pl.BlockSpec(arr.shape, lambda i: (0,) * arr.ndim)
    const = lambda shape: pl.BlockSpec(shape, lambda i: (0,) * len(shape))
    stack = HEADS * WTOK
    share = channels // n
    sem = lambda *k: pltpu.SemaphoreType.DMA((2,) + k)
    return pl.pallas_call(
        functools.partial(kernel, n, lats, kinds, lat_windows, level_windows, lon_windows),
        grid=(kinds,),
        in_specs=[
            pl.BlockSpec(memory_space=pltpu.SMEM),
            whole(perm),
            low,
            high,
            low,
            high,
            whole(weight_qkv),
            whole(weight_proj),
            pl.BlockSpec((1, stack, WTOK), lambda i: (i, 0, 0)),
        ],
        out_specs=[
            pl.BlockSpec(
                (WIN_Z, WIN_LAT, wide, channels),
                lambda i: (lax.rem(i, level_windows), i // level_windows, 0, 0),
            ),
            const((n, share, 4 * channels)),
            pl.BlockSpec(memory_space=pl.ANY),
        ],
        out_shape=[
            jax.ShapeDtypeStruct((levels, height, wide, channels), BF16),
            jax.ShapeDtypeStruct((n, share, 4 * channels), BF16),
            jax.ShapeDtypeStruct((kinds, PACKED, LANES), BF16),
        ],
        scratch_shapes=[
            pltpu.VMEM((lon_windows, stack, channels), BF16),
            pltpu.VMEM((lon_windows, stack, channels), BF16),
            pltpu.VMEM((lon_windows, stack, WTOK), BF16),
            pltpu.VMEM((lon_windows, stack, WTOK), BF16),
            pltpu.VMEM((channels, 3 * channels), F32),
            pltpu.VMEM((channels, channels), F32),
            pltpu.VMEM((kinds, PACKED, LANES), BF16),
            pltpu.VMEM((kinds, PACKED // 2, LANES), BF16),
            pltpu.VMEM((kinds, PACKED // 2, LANES), BF16),
            pltpu.VMEM((kinds, chips, PACKED // n, LANES), BF16),
            pltpu.VMEM((kinds, PACKED, LANES), BF16),
            pltpu.VMEM((n, share, 4 * channels), BF16),
            pltpu.VMEM((n, share, 4 * channels), BF16),
            pltpu.VMEM((lats, share, 4 * channels), BF16),
            pltpu.VMEM((n, share, 4 * channels), BF16),
            sem(kinds),
            sem(kinds, chips),
            sem(kinds, chips),
            sem(kinds, chips),
            pltpu.SemaphoreType.DMA((kinds,)),
            sem(n),
            sem(lats),
            sem(n),
        ],
        compiler_params=pltpu.CompilerParams(
            dimension_semantics=("arbitrary",),
            vmem_limit_bytes=56 * 2**20,
            collective_id=0,
            has_side_effects=True,
        ),
        cost_estimate=pl.CostEstimate(
            flops=kinds * 1_500_000_000, bytes_accessed=kinds * 2_000_000, transcendentals=0
        ),
    )(
        last, perm, frame_in, frame_in, frame_cot, frame_cot, weight_qkv, weight_proj, bias
    )


def local(normed, cotangent, weight_qkv, weight_proj, bias_table):
    levels, height, breadth, channels = normed.shape
    lat_shift = WIN_LAT // 2
    lon_shift = WIN_LON // 2
    lon_windows = breadth // WIN_LON
    wide = breadth + HALO
    across = ring_permute((normed[:, :, :HALO], cotangent[:, :, :HALO]), "lon", -1)
    wide_in = jnp.concatenate([normed, across[0]], axis=2)
    wide_cot = jnp.concatenate([cotangent, across[1]], axis=2)
    upward = line_permute((wide_in[:, :lat_shift], wide_cot[:, :lat_shift]), "lat", -1)
    frame_in = jnp.concatenate([wide_in[:, lat_shift:], upward[0]], axis=1)
    frame_cot = jnp.concatenate([wide_cot[:, lat_shift:], upward[1]], axis=1)
    last = (lax.axis_index("lat") == lax.axis_size("lat") - 1).astype(jnp.int32).reshape(1)
    bias = bias_table.reshape(bias_table.shape[0], HEADS * WTOK, WTOK)

    rows = jnp.arange(lon_windows * WTOK, dtype=jnp.int32)
    token = rows % WTOK
    per_level = WIN_LAT * WIN_LON
    source = (
        token // per_level * (WIN_LAT * wide)
        + token % per_level // WIN_LON * wide
        + rows // WTOK * WIN_LON
        + token % WIN_LON
        + lon_shift
    )
    columns = jnp.arange(WIN_Z * WIN_LAT * wide, dtype=jnp.int32)
    perm = (source[:, None] == columns[None, :]).astype(BF16)

    gframe, weights, packed = window_call(
        last, perm, frame_in, frame_cot, weight_qkv, weight_proj, bias
    )
    weights = weights.reshape(channels, 4 * channels).astype(F32)

    gwide = jnp.roll(gframe, WIN_Z // 2, axis=0)
    side = ring_permute(gwide[:, :, breadth:], "lon", 1)
    seam = jnp.concatenate(
        [gwide[:, :, :HALO] + side, gwide[:, :, HALO:breadth]], axis=2
    )
    down = line_permute(seam[:, height - lat_shift :], "lat", 1)
    input_grad = jnp.concatenate([down, seam[:, : height - lat_shift]], axis=1)

    bias_grad = unpack(packed)
    return input_grad, weights[:, : 3 * channels], weights[:, 3 * channels :], bias_grad


def solution(mesh):
    in_specs = (
        P(None, "lat", "lon", None),
        P(None, "lat", "lon", None),
        P(),
        P(),
        P("lat", None, None),
    )
    out_specs = (P(None, "lat", "lon", None), P(), P(), P("lat", None, None))
    return jax.shard_map(local, mesh=mesh, in_specs=in_specs, out_specs=out_specs, check_vma=False)
```

time: 257 us -> 232 us (0.903)
  Pallas kernels: 181 us -> 158 us
    pallas_call x2 -> x1, Pallas kernels: 165 us -> 142 us  [window_call(): pl.pallas_call(functools.partial(kernel, n, lats, kinds, lat_windows, lev...]
    slice x2, local copies, waits for them, and re-layouts: 0.35 us -> 3.12 us  [local(): gwide = jnp.roll(gframe, WIN_Z // 2, axis=0)]
    unnamed x20 -> x14, local copies, waits for them, and re-layouts: 14.8 us -> 12.5 us
  transfers between devices with their start and end apart: 6 -> 6, of which waited for: 2 -> 2; matrix products, arithmetic and copies ran while one was open for 14% -> 16% of each run, Pallas kernels for 32% -> 7%
where the time goes in v1:
time: 232 us; the launch traced here: 231 us
  Pallas kernels  158 us (68%)
  local copies, waits for them, and re-layouts  37.9 us (16%)
  waiting for transfers between devices  12.5 us (5%)
  other arithmetic  11.3 us (5%)
  starting transfers between devices  10.6 us (5%)
    pallas_call x1, Pallas kernels, window_call(): pl.pallas_call(functools.partial(kernel, n, lats, kinds, lat_windows, lev...  142 us
    pallas_call x1, Pallas kernels, unpack(): pl.pallas_call(unpack_kernel, grid=(kinds,), in_specs=[pl.BlockSpec((1, r...  15.9 us
    reshape x1, local copies, waits for them, and re-layouts, local(): bias = bias_table.reshape(bias_table.shape[0], HEADS * WTOK, WTOK)  13.8 us
    unnamed x14, local copies, waits for them, and re-layouts  12.5 us
    ppermute x3, waiting for transfers between devices, ring_permute(): lax.ppermute(block, axis, [((i - distance) % size, i) for i in range(size)])  12.5 us
    ppermute x3, starting transfers between devices, line_permute(): return lax.ppermute(block, axis, route)  6.1 us
  transfers between devices with their start and end apart: 6, of which 2 were waited for; matrix products, arithmetic and copies ran while one was open for 16% of the time, Pallas kernels for 7%

profile of v1, /device:TPU:0, one launch (start us, length us, event | category | flops | bytes accessed | tf_op | source)
XLA Modules:
  0.0 230.9 jit_solution(13682771467101704389)
XLA Ops:
  0.6 0.0 copy-start.2
  0.6 1.3 slice.47
  2.0 3.4 %collective-permute-start = (bf16[8,24,8,192]{3,2,1,0:T(8,128)(2,1)S(1)}, bf16[8,24,8,192]{3,2,1,0:T(8,128)(2,1)S(1)}, u32[]{:S(2)}, u32[]{:S(2)}) collective-permute-start(bf16[8,24,8,192]{3,2,1,0:T(8,128)(2,1)S(1)} %slice.47), channel_id=1, source_target_pairs={{4,0},{8,4},{12,8},{16,12},{20,16},{24,20},{28,24},{0,28},{5,1},{9... | collective-permute-start | bytes 1769480 | tf_op jit(solution)/shard_map/ppermute | solution.py:28
  5.4 1.2 slice.50
  6.6 0.0 copy-start.3
  6.6 0.7 collective-permute-start.2
  7.4 0.0 copy-done.2
  7.4 0.3 constant_dynamic-update-slice_fusion.1
  7.7 0.6 copy-done.3
  8.2 0.3 constant_dynamic-update-slice_fusion.3
  8.6 6.3 %collective-permute-done = bf16[8,24,8,192]{3,2,1,0:T(8,128)(2,1)S(1)} collective-permute-done((bf16[8,24,8,192]{3,2,1,0:T(8,128)(2,1)S(1)}, bf16[8,24,8,192]{3,2,1,0:T(8,128)(2,1)S(1)}, u32[]{:S(2)}, u32[]{:S(2)}) %collective-permute-start) | collective-permute-done | bytes 589856 | tf_op jit(solution)/shard_map/ppermute | solution.py:28
  14.9 0.1 constant_dynamic-update-slice_fusion
  15.0 0.0 copy-start.1
  15.0 0.9 slice.63
  15.9 1.3 collective-permute-start.1
  17.2 6.1 %collective-permute-done.2 = bf16[8,24,8,192]{3,2,1,0:T(8,128)(2,1)S(1)} collective-permute-done((bf16[8,24,8,192]{3,2,1,0:T(8,128)(2,1)S(1)}, bf16[8,24,8,192]{3,2,1,0:T(8,128)(2,1)S(1)}, u32[]{:S(2)}, u32[]{:S(2)}) %collective-permute-start.2) | collective-permute-done | bytes 589856 | tf_op jit(solution)/shard_map/ppermute | solution.py:28
  23.3 0.1 constant_dynamic-update-slice_fusion.2
  23.4 0.0 copy-done.1
  23.4 0.8 slice.65
  24.2 1.3 collective-permute-start.3
  25.5 0.8 fusion.4.perm_ref
  26.3 5.6 %copy.11 = bf16[16,6,20736]{2,1,0:T(8,128)(2,1)} copy(bf16[16,6,20736]{2,0,1:T(8,128)(2,1)} %param.9) | data formatting | bytes 7962624 | tf_op args[4]
  32.0 13.8 %reshape.71.bias_ref = bf16[16,864,144]{2,1,0:T(8,128)(2,1)} reshape(bf16[16,6,20736]{2,1,0:T(8,128)(2,1)} %copy.11) | data formatting | bytes 7962624 | tf_op jit(solution)/shard_map/reshape | solution.py:559
  45.8 2.0 slice.62
  47.9 0.3 slice.64
  48.1 0.0 collective-permute-done.1
  48.1 2.1 pad_maximum_fusion.xa_ref.xb_ref
  50.3 0.0 collective-permute-done.3
  50.3 3.2 %pad_maximum_fusion.1.ca_ref.cb_ref = bf16[8,24,32,192]{3,2,1,0:T(8,128)(2,1)} fusion(bf16[8,3,32,192]{3,2,1,0:T(8,128)(2,1)} %collective-permute-done.3, bf16[8,21,32,192]{3,2,1,0:T(8,128)(2,1)S(1)} %slice.64), kind=kLoop, calls=%fused_computation.4 | loop fusion | flops 1179648 | bytes 4718592 | tf_op jit(solution)/shard_map/concatenate | solution.py:557
  53.5 141.9 %shard_map.84 = (bf16[8,24,32,192]{3,2,1,0:T(8,128)(2,1)}, bf16[8,24,768]{2,1,0:T(8,128)(2,1)}, bf16[16,1024,128]{2,1,0:T(8,128)(2,1)}) custom-call(s32[1]{0:T(128)} %bitcast.last_ref, bf16[288,384]{1,0:T(8,128)(2,1)} %fusion.4.perm_ref, bf16[8,24,32,192]{3,2,1,0:T(8,128)(2,1)} %pad_maximum_fusion.xa_ref.xb_ref, ...), custom_call_target="tpu_custom_call" | custom-call | flops 24000000000 | bytes 32000000 | tf_op jit(solution)/shard_map/pallas_call | solution.py:480
  195.3 1.0 slice.53
  196.3 2.1 slice.54
  198.4 1.1 pad_maximum_fusion.3
  199.6 0.3 collective-permute-start.4
  199.9 15.9 %shard_map.85 = f32[16,6,20736]{2,1,0:T(8,128)} custom-call(bf16[16,1024,128]{2,1,0:T(8,128)(2,1)} %get-tuple-element.9.packed_ref), custom_call_target="tpu_custom_call" | custom-call | flops 10000000000 | bytes 15000000 | tf_op jit(solution)/shard_map/pallas_call | solution.py:446
  215.8 0.0 collective-permute-done.4
  215.8 0.0 copy-start
  215.8 1.6 maximum_add_fusion
  217.4 0.0 copy-start.4
  217.4 0.6 fusion.3
  218.0 3.5 %collective-permute-start.5 = (bf16[8,3,24,192]{3,2,1,0:T(8,128)(2,1)S(1)}, bf16[8,3,24,192]{3,2,1,0:T(8,128)(2,1)S(1)}, u32[]{:S(2)}, u32[]{:S(2)}) collective-permute-start(bf16[8,3,24,192]{3,2,1,0:T(8,128)(2,1)S(1)} %slice.66), channel_id=1, source_target_pairs={{0,1},{1,2},{2,3},{4,5},{5,6},{6,7},{8,9},{9,10},{10,11},{12,13},{... | collective-permute-start | bytes 663560 | tf_op jit(solution)/shard_map/ppermute | solution.py:34
  221.6 0.0 copy-done.4
  221.6 0.1 bitcast_convert_fusion
  221.6 0.8 slice.69
  222.4 0.8 slice.68
  223.2 0.0 copy-done
  223.2 5.7 %copy.12 = f32[16,6,20736]{2,0,1:T(8,128)} copy(f32[16,6,20736]{2,1,0:T(8,128)S(1)} %copy-done) | data formatting | bytes 15925248
  228.9 0.1 slice.67
  229.1 0.0 collective-permute-done.5
  229.1 1.8 pad_maximum_fusion.2
  (2 shorter events, 0.1 us)
Async XLA Ops:
  0.6 6.7 %copy-start.2 = (bf16[8,24,24,192]{3,2,1,0:T(8,128)(2,1)S(1)}, bf16[8,24,24,192]{3,2,1,0:T(8,128)(2,1)}, u32[]{:S(2)}) copy-start(bf16[8,24,24,192]{3,2,1,0:T(8,128)(2,1)} %param.5) | copy-start | bytes 5308420
  2.0 12.9 %collective-permute-start = (bf16[8,24,8,192]{3,2,1,0:T(8,128)(2,1)S(1)}, bf16[8,24,8,192]{3,2,1,0:T(8,128)(2,1)S(1)}, u32[]{:S(2)}, u32[]{:S(2)}) collective-permute-start(bf16[8,24,8,192]{3,2,1,0:T(8,128)(2,1)S(1)} %slice.47), channel_id=1, source_target_pairs={{4,0},{8,4},{12,8},{16,12},{20,16},{24,20},{28,24},{0,28},{5,1},{9... | collective-permute-start | bytes 1769480 | tf_op jit(solution)/shard_map/ppermute | solution.py:28
  6.6 1.7 copy-start.3
  6.6 16.7 %collective-permute-start.2 = (bf16[8,24,8,192]{3,2,1,0:T(8,128)(2,1)S(1)}, bf16[8,24,8,192]{3,2,1,0:T(8,128)(2,1)S(1)}, u32[]{:S(2)}, u32[]{:S(2)}) collective-permute-start(bf16[8,24,8,192]{3,2,1,0:T(8,128)(2,1)S(1)} %slice.50), channel_id=1, source_target_pairs={{4,0},{8,4},{12,8},{16,12},{20,16},{24,20},{28,24},{0,28},{5,1},{9... | collective-permute-start | bytes 1769480 | tf_op jit(solution)/shard_map/ppermute | solution.py:28
  15.0 8.4 %copy-start.1 = (bf16[8,24,32,192]{3,2,1,0:T(8,128)(2,1)}, bf16[8,24,32,192]{3,2,1,0:T(8,128)(2,1)S(1)}, u32[]{:S(2)}) copy-start(bf16[8,24,32,192]{3,2,1,0:T(8,128)(2,1)S(1)} %constant_dynamic-update-slice_fusion) | copy-start | bytes 7077892
  15.9 32.2 %collective-permute-start.1 = (bf16[8,3,32,192]{3,2,1,0:T(8,128)(2,1)}, bf16[8,3,32,192]{3,2,1,0:T(8,128)(2,1)S(1)}, u32[]{:S(2)}, u32[]{:S(2)}) collective-permute-start(bf16[8,3,32,192]{3,2,1,0:T(8,128)(2,1)} %slice.63), channel_id=1, source_target_pairs={{1,0},{2,1},{3,2},{5,4},{6,5},{7,6},{9,8},{10,9},{11,10},{13,12},{... | collective-permute-start | bytes 884744 | tf_op jit(solution)/shard_map/ppermute | solution.py:34
  24.2 26.0 %collective-permute-start.3 = (bf16[8,3,32,192]{3,2,1,0:T(8,128)(2,1)}, bf16[8,3,32,192]{3,2,1,0:T(8,128)(2,1)}, u32[]{:S(2)}, u32[]{:S(2)}) collective-permute-start(bf16[8,3,32,192]{3,2,1,0:T(8,128)(2,1)} %slice.65), channel_id=1, source_target_pairs={{1,0},{2,1},{3,2},{5,4},{6,5},{7,6},{9,8},{10,9},{11,10},{13,12},{... | collective-permute-start | bytes 884744 | tf_op jit(solution)/shard_map/ppermute | solution.py:34
  199.6 16.3 %collective-permute-start.4 = (bf16[8,24,8,192]{3,2,1,0:T(8,128)(2,1)}, bf16[8,24,8,192]{3,2,1,0:T(8,128)(2,1)}, u32[]{:S(2)}, u32[]{:S(2)}) collective-permute-start(bf16[8,24,8,192]{3,2,1,0:T(8,128)(2,1)} %pad_maximum_fusion.3), channel_id=1, source_target_pairs={{28,0},{0,4},{4,8},{8,12},{12,16},{16,20},{20,24},{24,28},{29,1},{... | collective-permute-start | bytes 1769480 | tf_op jit(solution)/shard_map/ppermute | solution.py:28
  215.8 7.4 %copy-start = (f32[16,6,20736]{2,1,0:T(8,128)S(1)}, f32[16,6,20736]{2,1,0:T(8,128)}, u32[]{:S(2)}) copy-start(f32[16,6,20736]{2,1,0:T(8,128)} %shard_map.85) | copy-start | bytes 23887876
  217.4 4.2 %copy-start.4 = (bf16[8,24,768]{2,1,0:T(8,128)(2,1)S(1)}, bf16[8,24,768]{2,1,0:T(8,128)(2,1)}, u32[]{:S(2)}) copy-start(bf16[8,24,768]{2,1,0:T(8,128)(2,1)} %get-tuple-element.8) | copy-start | bytes 884740
  218.0 11.1 %collective-permute-start.5 = (bf16[8,3,24,192]{3,2,1,0:T(8,128)(2,1)S(1)}, bf16[8,3,24,192]{3,2,1,0:T(8,128)(2,1)S(1)}, u32[]{:S(2)}, u32[]{:S(2)}) collective-permute-start(bf16[8,3,24,192]{3,2,1,0:T(8,128)(2,1)S(1)} %slice.66), channel_id=1, source_target_pairs={{0,1},{1,2},{2,3},{4,5},{5,6},{6,7},{8,9},{9,10},{10,11},{12,13},{... | collective-permute-start | bytes 663560 | tf_op jit(solution)/shard_map/ppermute | solution.py:34

commit v2 on v1

--- a/solution.py
+++ b/solution.py
@@ -17,21 +17,12 @@
 TAIL = WTOK - LANES
 HALO = 8
 PACKED = 1024
+LAGS = (1, 3, 5, 6)
+GRAD_LAG = 2
 UNROLL = 6
 LOG2E = math.log2(math.e)
 F32 = jnp.float32
 BF16 = jnp.bfloat16
-
-
-def ring_permute(block, axis, distance):
-    size = lax.axis_size(axis)
-    return lax.ppermute(block, axis, [((i - distance) % size, i) for i in range(size)])
-
-
-def line_permute(block, axis, distance):
-    size = lax.axis_size(axis)
-    route = [(i - distance, i) for i in range(size) if 0 <= i - distance < size]
-    return lax.ppermute(block, axis, route)
 
 
 def mm(a, b, ca=1, cb=0):
@@ -131,8 +122,8 @@
         return [self.stage_pair, self.stage_cross, self.stage_back, self.stage_fwd]
 
     def behind(self, step):
-        for d, stage in enumerate(self.stages()):
-            t = step - 1 - d
+        for lag, stage in zip(LAGS, self.stages()):
+            t = step - lag
             if isinstance(t, int):
                 if 0 <= t < self.kinds:
                     stage(t)
@@ -153,6 +144,194 @@
         lax.fori_loop(0, self.kinds, body, 0)
 
 
+class Halo:
+    def __init__(self, n, lats, levels, level_windows, lat_windows, refs, sems):
+        self.n, self.lats = n, lats
+        self.levels, self.level_windows, self.lat_windows = levels, level_windows, lat_windows
+        self.given, self.east, self.south, self.gl, self.gh, self.wh, self.nh, self.out = refs
+        self.east_sem, self.south_sem, self.wh_sem, self.nh_sem, self.out_sem = sems
+        self.me, self.lat = lax.axis_index("lon"), lax.axis_index("lat")
+        self.shift = WIN_LAT // 2
+        self.height = lat_windows * WIN_LAT
+
+    def remote(self, src, dst, sems, at, lat, lon):
+        device = {"lat": self.lat + lat, "lon": lax.rem(self.me + lon + self.n, self.n)}
+        return pltpu.make_async_remote_copy(
+            src_ref=src, dst_ref=dst, send_sem=sems.at[(0,) + at], recv_sem=sems.at[(1,) + at],
+            device_id=device, device_id_type=pl.DeviceIdType.MESH,
+        )
+
+    def east_copy(self, i, z, piece):
+        short = piece >= self.lat_windows - 1
+        count = self.shift if short else WIN_LAT
+        corner = piece == self.lat_windows
+        src_row = 0 if corner else self.shift + piece * WIN_LAT
+        dst_row = self.height - self.shift if corner else piece * WIN_LAT
+        src = self.given[i].at[z, pl.ds(src_row, count), pl.ds(0, HALO), :]
+        dst = self.east.at[i, z, pl.ds(dst_row, count)]
+        return self.remote(src, dst, self.east_sem, (i, piece, z), -1 if corner else 0, -1)
+
+    def south_copy(self, i, z):
+        src = self.given[i].at[z, pl.ds(0, self.shift)]
+        return self.remote(src, self.south.at[i, z], self.south_sem, (i, z), -1, 0)
+
+    def send(self):
+        def level(piece, y, _):
+            z = lax.rem(y + 1, self.levels)
+            for i in range(2):
+                self.east_copy(i, z, piece).start()
+            return 0
+
+        def below(y, _):
+            z = lax.rem(y + 1, self.levels)
+            for i in range(2):
+                self.south_copy(i, z).start()
+                self.east_copy(i, z, self.lat_windows).start()
+            return 0
+
+        for piece in range(self.lat_windows):
+            lax.fori_loop(0, self.levels, functools.partial(level, piece), 0)
+
+        @pl.when(self.lat > 0)
+        def _():
+            lax.fori_loop(0, self.levels, below, 0)
+
+        @pl.when(self.lat == self.lats - 1)
+        def _():
+            self.south[...] = jnp.zeros_like(self.south)
+            shape = self.east.shape
+            rows = pl.ds(self.height - self.shift, self.shift)
+            self.east[:, :, rows] = jnp.zeros(shape[:2] + (self.shift,) + shape[3:], BF16)
+
+        @pl.when(self.lat == 0)
+        def _():
+            self.nh[...] = jnp.zeros_like(self.nh)
+            shape = self.wh.shape
+            self.wh[:, : self.shift] = jnp.zeros((shape[0], self.shift) + shape[2:], BF16)
+
+    def pair(self, a):
+        return [lax.rem(WIN_Z * a + 1 + u, self.levels) for u in range(WIN_Z)]
+
+    def arrive(self, a, b):
+        last = self.lat_windows - 1
+        for z in self.pair(a):
+            for i in range(2):
+                for piece in range(self.lat_windows):
+                    @pl.when(b == piece)
+                    def _(i=i, z=z, piece=piece):
+                        self.east_copy(i, z, piece).wait_recv()
+
+                @pl.when((b == last) & (self.lat < self.lats - 1))
+                def _(i=i, z=z):
+                    self.south_copy(i, z).wait_recv()
+                    self.east_copy(i, z, self.lat_windows).wait_recv()
+
+    def back_copy(self, z, piece):
+        short = piece >= self.lat_windows - 1
+        count = self.shift if short else WIN_LAT
+        corner = piece == self.lat_windows
+        src_row = self.height - self.shift if corner else piece * WIN_LAT
+        dst_row = 0 if corner else self.shift + piece * WIN_LAT
+        return self.remote(
+            self.gh.at[z, pl.ds(src_row, count)], self.wh.at[z, pl.ds(dst_row, count)],
+            self.wh_sem, (piece, z), 1 if corner else 0, 1,
+        )
+
+    def down_copy(self, z):
+        src = self.gl.at[z, pl.ds(self.height, self.shift)]
+        return self.remote(src, self.nh.at[z], self.nh_sem, (z,), 1, 0)
+
+    def give(self, a, b):
+        last = self.lat_windows - 1
+        for z in self.pair(a):
+            for piece in range(self.lat_windows):
+                @pl.when(b == piece)
+                def _(z=z, piece=piece):
+                    self.back_copy(z, piece).start()
+
+            @pl.when((b == last) & (self.lat < self.lats - 1))
+            def _(z=z):
+                self.back_copy(z, self.lat_windows).start()
+                self.down_copy(z).start()
+
+    def store(self, z, piece):
+        short = piece >= self.lat_windows - 1
+        count = self.shift if short else WIN_LAT
+        if piece == self.lat_windows:
+            return pltpu.make_async_copy(
+                self.nh.at[z], self.out.at[z, pl.ds(0, count)], self.out_sem.at[piece, z]
+            )
+        rows = pl.ds(self.shift + piece * WIN_LAT, count)
+        return pltpu.make_async_copy(
+            self.gl.at[z, rows], self.out.at[z, rows], self.out_sem.at[piece, z]
+        )
+
+    def finish_piece(self, z, piece):
+        short = piece >= self.lat_windows - 1
+        count = self.shift if short else WIN_LAT
+        if piece == self.lat_windows:
+            @pl.when(self.lat > 0)
+            def _():
+                self.back_copy(z, piece).wait_recv()
+                self.down_copy(z).wait_recv()
+
+            seam = self.nh[z, :, :HALO].astype(F32) + self.wh[z, :count].astype(F32)
+            self.nh[z, :, :HALO] = seam.astype(BF16)
+        else:
+            self.back_copy(z, piece).wait_recv()
+            rows = pl.ds(self.shift + piece * WIN_LAT, count)
+            seam = self.gl[z, rows, :HALO].astype(F32) + self.wh[z, rows].astype(F32)
+            self.gl[z, rows, :HALO] = seam.astype(BF16)
+        self.store(z, piece).start()
+
+    def finish(self, a, b):
+        for z in self.pair(a):
+            for piece in range(self.lat_windows):
+                @pl.when(b == piece)
+                def _(z=z, piece=piece):
+                    self.finish_piece(z, piece)
+
+    def end(self):
+        def top(z, _):
+            self.finish_piece(z, self.lat_windows)
+            return 0
+
+        def level(piece, z, _):
+            for i in range(2):
+                self.east_copy(i, z, piece).wait_send()
+            self.back_copy(z, piece).wait_send()
+            self.store(z, piece).wait()
+            return 0
+
+        def near(z, _):
+            self.store(z, self.lat_windows).wait()
+            return 0
+
+        def up(z, _):
+            for i in range(2):
+                self.south_copy(i, z).wait_send()
+                self.east_copy(i, z, self.lat_windows).wait_send()
+            return 0
+
+        def down(z, _):
+            self.back_copy(z, self.lat_windows).wait_send()
+            self.down_copy(z).wait_send()
+            return 0
+
+        lax.fori_loop(0, self.levels, top, 0)
+        for piece in range(self.lat_windows):
+            lax.fori_loop(0, self.levels, functools.partial(level, piece), 0)
+        lax.fori_loop(0, self.levels, near, 0)
+
+        @pl.when(self.lat > 0)
+        def _():
+            lax.fori_loop(0, self.levels, up, 0)
+
+        @pl.when(self.lat < self.lats - 1)
+        def _():
+            lax.fori_loop(0, self.levels, down, 0)
+
+
 def enter(n, lats):
     me, lat = lax.axis_index("lon"), lax.axis_index("lat")
     barrier = pltpu.get_barrier_semaphore()
@@ -166,7 +345,13 @@
             barrier, inc=1, device_id={"lat": lax.rem(lat + o, lats)},
             device_id_type=pl.DeviceIdType.MESH,
         )
-    pl.semaphore_wait(barrier, n + lats - 2)
+    for o in (-1, 1):
+        pl.semaphore_signal(
+            barrier, inc=1,
+            device_id={"lat": lax.rem(lat + o + lats, lats), "lon": lax.rem(me + o + n, n)},
+            device_id_type=pl.DeviceIdType.MESH,
+        )
+    pl.semaphore_wait(barrier, n + lats)
 
 
 class WeightSum:
@@ -228,6 +413,24 @@
             self.second(o, False).wait_send()
 
 
+def flip(mains, under, right, corner):
+    lane = lax.broadcasted_iota(jnp.int32, (TAIL, LANES), 1) // TAIL
+    spare = jnp.zeros((LANES - HEADS * TAIL, LANES), F32)
+    mains_t = [block.T for block in mains]
+    right_t = jnp.concatenate(under + [spare], axis=0).T
+    turned = right.T
+    under_t = [turned[h * TAIL : (h + 1) * TAIL] for h in range(HEADS)]
+    pad = jnp.zeros((LANES - TAIL, LANES), F32)
+    turned = jnp.concatenate([corner, pad], axis=0).T
+    corner_t = jnp.zeros((TAIL, LANES), F32)
+    for h in range(HEADS):
+        piece = turned[h * TAIL : (h + 1) * TAIL]
+        if h:
+            piece = pltpu.roll(piece, h * TAIL, 1)
+        corner_t = jnp.where(lane == h, piece, corner_t)
+    return mains_t, under_t, right_t, corner_t
+
+
 def kernel(
     n,
     lats,
@@ -235,25 +438,40 @@
     lat_windows,
     level_windows,
     lon_windows,
-    last_ref,
     perm_ref,
-    xa_ref,
-    xb_ref,
-    ca_ref,
-    cb_ref,
+    back_ref,
+    x0_ref,
+    x1_ref,
+    x2_ref,
+    x3_ref,
+    c0_ref,
+    c1_ref,
+    c2_ref,
+    c3_ref,
+    x_hbm,
+    c_hbm,
     wqkv_ref,
+    wback_ref,
     wproj_ref,
     bias_ref,
-    gframe_ref,
+    side_ref,
     wout_ref,
     gbias_hbm,
-    qm_s,
-    mm_s,
+    grad_hbm,
+    q_s,
+    m_s,
+    qt_s,
+    mt_s,
+    kt_s,
+    vt_s,
     p_s,
     ds_s,
-    gqkv_ref,
-    gproj_ref,
-    gbias_ref,
+    shift_s,
+    mix_s,
+    dqt_s,
+    gqkv_s,
+    gproj_s,
+    gbias_s,
     pair_s,
     sum_s,
     cross_s,
@@ -262,6 +480,13 @@
     w1_s,
     w2_s,
     w3_s,
+    east_s,
+    south_s,
+    gl_s,
+    gh_s,
+    wh_s,
+    nh_s,
+    below_s,
     pair_sem,
     cross_sem,
     back_sem,
@@ -270,114 +495,212 @@
     w1_sem,
     w2_sem,
     w3_sem,
+    east_sem,
+    south_sem,
+    wh_sem,
+    nh_sem,
+    out_sem,
 ):
     step = pl.program_id(0)
     a = lax.rem(step, level_windows)
     b = step // level_windows
-    channels = wqkv_ref.shape[0]
+    channels = wqkv_ref.shape[1]
     head_dim = channels // HEADS
     scale = head_dim ** -0.5
-    half = WIN_LAT * xa_ref.shape[2]
+    levels = x_hbm.shape[0]
+    shift = WIN_LAT // 2
+    breadth = x0_ref.shape[2]
+    tails = HEADS * LANES
+    stack = HEADS * WTOK
 
     @pl.when(step == 0)
     def _():
-        gqkv_ref[...] = jnp.zeros_like(gqkv_ref)
-        gproj_ref[...] = jnp.zeros_like(gproj_ref)
-        gbias_ref[:, HEADS * WTOK :, :] = jnp.zeros((kinds, PACKED - HEADS * WTOK, LANES), BF16)
+        for ref in (gqkv_s, gproj_s, q_s, m_s, qt_s, mt_s):
+            ref[...] = jnp.zeros_like(ref)
+        gbias_s[:, stack + WTOK :, :] = jnp.zeros((kinds, PACKED - stack - WTOK, LANES), BF16)
         enter(n, lats)
 
-    ex = Exchange(
-        n, kinds,
-        (gbias_ref, pair_s, sum_s, cross_s, red_s, gbias_hbm),
-        (pair_sem, cross_sem, back_sem, fwd_sem, store_sem),
+    halo = Halo(
+        n, lats, levels, level_windows, lat_windows,
+        ((x_hbm, c_hbm), east_s, south_s, gl_s, gh_s, wh_s, nh_s, grad_hbm),
+        (east_sem, south_sem, wh_sem, nh_sem, out_sem),
     )
-    ex.behind(step)
+    pl.when(step == 0)(halo.send)
+    halo.arrive(a, b)
 
     perm = perm_ref[...]
-    x_raw = jnp.concatenate(
-        [xa_ref[...].reshape(half, channels), xb_ref[...].reshape(half, channels)], axis=0
-    )
-    c_raw = jnp.concatenate(
-        [ca_ref[...].reshape(half, channels), cb_ref[...].reshape(half, channels)], axis=0
-    )
+    bottom = b == lat_windows - 1
+
+    def raw(which, refs):
+        flat = lambda t: t.reshape(-1, channels)
+        parts = []
+        for u, z in enumerate(halo.pair(a)):
+            @pl.when(bottom)
+            def _(u=u, z=z):
+                below_s[which, u] = south_s[which, z]
+
+            @pl.when(jnp.logical_not(bottom))
+            def _(u=u):
+                below_s[which, u] = refs[2 * u + 1][0]
+
+            parts += [flat(refs[2 * u][0]), flat(below_s[which, u])]
+        for z in halo.pair(a):
+            parts.append(flat(east_s[which, z, pl.ds(b * WIN_LAT, WIN_LAT)]))
+        return jnp.concatenate(parts, axis=0)
+
+    x_raw = raw(0, (x0_ref, x1_ref, x2_ref, x3_ref))
+    c_raw = raw(1, (c0_ref, c1_ref, c2_ref, c3_ref))
     x = mm(perm, x_raw).astype(BF16)
     c = mm(perm, c_raw).astype(BF16)
-    proj = mm(x, wqkv_ref[...]).astype(BF16)
-    mgrad = mm(c, wproj_ref[...], 1, 1).astype(BF16)
+    q = (mm(x, wqkv_ref[0]) * (scale * LOG2E)).astype(BF16)
+    k = mm(x, wqkv_ref[1]).astype(BF16)
+    v = mm(x, wqkv_ref[2]).astype(BF16)
+    m = mm(c, wproj_ref[...]).astype(BF16)
 
     wrap_here = a == level_windows - 1
-    dead_here = (b == lat_windows - 1) & (last_ref[0] == 1)
+    dead_here = bottom & (lax.axis_index("lat") == lats - 1)
     per_level = WTOK // WIN_Z
 
-    def classes(shape, dim):
-        token = lax.broadcasted_iota(jnp.int32, shape, dim)
+    def classes(token):
         upper = token >= per_level
         inner = jnp.where(upper, token - per_level, token)
         wrapped = jnp.where(upper & wrap_here, 2, 0)
         dead = jnp.where((inner >= per_level // 2) & dead_here, 1, 0)
         return wrapped + dead
 
-    same = classes((WTOK, WTOK), 0) == classes((WTOK, WTOK), 1)
-    mask_add = jnp.where(same, 0.0, -1e30)
-    lane_head = lax.broadcasted_iota(jnp.int32, (1, channels), 1) // head_dim
-    zero = jnp.zeros((), BF16)
-
-    parts = []
+    lane = lax.broadcasted_iota(jnp.int32, (1, LANES), 1)
+    key_class = classes(lax.broadcasted_iota(jnp.int32, (WTOK, LANES), 0))
+    mask_main = jnp.where(key_class == classes(lane), 0.0, -1e30)
+    mask_tail = jnp.where(key_class == classes(LANES + lax.rem(lane, TAIL)), 0.0, -1e30)
+
+    table = lambda lo, rows: bias_ref[0, lo : lo + rows, :].astype(F32) * LOG2E
+    mains_t, under_t, right_t, corner_t = flip(
+        [table(h * WTOK, LANES) for h in range(HEADS)],
+        [table(h * WTOK + LANES, TAIL) for h in range(HEADS)],
+        side_ref[0, :LANES, :].astype(F32) * LOG2E,
+        side_ref[0, LANES:, :].astype(F32) * LOG2E,
+    )
+    for h in range(HEADS):
+        cols = slice(h * LANES, (h + 1) * LANES)
+        shift_s[:LANES, cols] = mains_t[h] + mask_main[:LANES]
+        shift_s[LANES:, cols] = under_t[h] + mask_main[LANES:]
+    shift_s[:LANES, tails:] = right_t + mask_tail[:LANES]
+    shift_s[LANES:, tails:] = corner_t + mask_tail[LANES:]
+
+    whole = lon_windows * LANES
+    main = lambda w: slice(w * LANES, (w + 1) * LANES)
+    tail = lambda w: slice(whole + w * TAIL, whole + (w + 1) * TAIL)
+    window = lambda t, w: jnp.concatenate([t[main(w)], t[tail(w)]], axis=0)
+    keys = [window(k, w) for w in range(lon_windows)]
+    values = [window(v, w) for w in range(lon_windows)]
     for w in range(lon_windows):
-        rows = slice(w * WTOK, (w + 1) * WTOK)
-        parts.append(
-            (
-                proj[rows, :channels],
-                proj[rows, channels : 2 * channels],
-                proj[rows, 2 * channels :],
-                mgrad[rows],
-            )
-        )
-    mixed = [jnp.zeros((WTOK, channels), F32) for _ in range(lon_windows)]
-    dq = [jnp.zeros((WTOK, channels), F32) for _ in range(lon_windows)]
+        for flat, wide_s, turned_s in ((q, q_s, qt_s), (m, m_s, mt_s)):
+            turned = flat[main(w)].T
+            for h in range(HEADS):
+                cs = slice(h * head_dim, (h + 1) * head_dim)
+                wide_s[w, h * LANES : (h + 1) * LANES, cs] = flat[main(w), cs]
+                wide_s[w, tails + h * TAIL : tails + (h + 1) * TAIL, cs] = flat[tail(w), cs]
+                turned_s[w, cs, h * LANES : (h + 1) * LANES] = turned[cs]
+            turned_s[w, :, tails:] = wide_s[w, tails:, :].T
+        kt_s[w] = keys[w].T
+        vt_s[w] = values[w].T
+
+    tiles = HEADS + 1
+    gb = []
+    for j in range(0, tiles, 2):
+        cols = slice(j * LANES, min(j + 2, tiles) * LANES)
+        total = [None, None]
+        for w in range(lon_windows):
+            s2 = mm(keys[w], qt_s[w, :, cols])
+            dp2 = mm(values[w], mt_s[w, :, cols])
+            for i in range(min(2, tiles - j)):
+                here = slice(i * LANES, (i + 1) * LANES)
+                at = slice((j + i) * LANES, (j + i + 1) * LANES)
+                s = s2[:, here] + shift_s[:, at]
+                dp = dp2[:, here]
+                e = jnp.exp2(s - jnp.max(s, axis=0, keepdims=True))
+                r = 1.0 / jnp.sum(e, axis=0, keepdims=True)
+                p = e * r
+                delta = jnp.sum(p * dp, axis=0, keepdims=True)
+                ds = p * (dp - delta)
+                p_s[w, :, at] = p.astype(BF16)
+                ds_s[w, :, at] = ds.astype(BF16)
+                total[i] = ds if total[i] is None else total[i] + ds
+        gb += total[: min(2, tiles - j)]
+
+    tail_lane = lax.broadcasted_iota(jnp.int32, (head_dim, LANES), 1) // TAIL
+    for turned_s, from_s, to_s, factor in ((vt_s, p_s, mix_s, None), (kt_s, ds_s, dqt_s, scale)):
+        far = [None] * HEADS
+        for w in range(lon_windows):
+            for j in range(0, HEADS, 2):
+                rows = slice(j * head_dim, (j + 2) * head_dim)
+                out = mm(turned_s[w, rows, :], from_s[w, :, j * LANES : (j + 2) * LANES])
+                if factor is not None:
+                    out = out * factor
+                for i in range(2):
+                    cs = slice((j + i) * head_dim, (j + i + 1) * head_dim)
+                    piece = out[i * head_dim : (i + 1) * head_dim, i * LANES : (i + 1) * LANES]
+                    to_s[cs, main(w)] = piece.astype(BF16)
+            out = mm(turned_s[w], from_s[w, :, tails:])
+            if factor is not None:
+                out = out * factor
+            for h in range(HEADS):
+                piece = out[h * head_dim : (h + 1) * head_dim]
+                turn = (w - h) * TAIL % LANES
+                if turn:
+                    piece = pltpu.roll(piece, turn, 1)
+                far[h] = jnp.where(tail_lane == w, piece, 0.0 if far[h] is None else far[h])
+        for h in range(HEADS):
+            cs = slice(h * head_dim, (h + 1) * head_dim)
+            to_s[cs, whole:] = far[h].astype(BF16)
+
+    dk, dv = [], []
+    for w in range(lon_windows):
+        dk.append((mm(ds_s[w], q_s[w]) * (1.0 / LOG2E)).astype(BF16))
+        dv.append(mm(p_s[w], m_s[w]).astype(BF16))
+    order = lambda ts: jnp.concatenate([t[:LANES] for t in ts] + [t[LANES:] for t in ts], axis=0)
+    tokens = lon_windows * WTOK
+    dq = dqt_s[...].T[:tokens]
+    cols = [dq, order(dk), order(dv)]
+    xt = x.T
+    for i in range(3):
+        gqkv_s[i] += mm(xt, cols[i])
+    gproj_s[...] += mm(mix_s[:, :tokens], c)
+    gin = mm(cols[0], wback_ref[0]) + mm(cols[1], wback_ref[1]) + mm(cols[2], wback_ref[2])
+    gout = mm(back_ref[...], gin.astype(BF16)).astype(BF16)
+    near, far = WIN_LAT * breadth, WIN_LAT * HALO
+    for u, z in enumerate(halo.pair(a)):
+        rows = pl.ds(shift + b * WIN_LAT, WIN_LAT)
+        own = gout[u * near : (u + 1) * near]
+        gl_s[z, rows] = own.reshape(WIN_LAT, breadth, channels)
+        strip = gout[WIN_Z * near + u * far : WIN_Z * near + (u + 1) * far]
+        gh_s[z, pl.ds(b * WIN_LAT, WIN_LAT)] = strip.reshape(WIN_LAT, HALO, channels)
+    halo.give(a, b)
+    late = step - GRAD_LAG
+
+    @pl.when(late >= 0)
+    def _():
+        halo.finish(lax.rem(late, level_windows), late // level_windows)
+
+
+    mains_t, under_t, right_t, corner_t = flip(
+        [gb[h][:LANES] for h in range(HEADS)],
+        [gb[h][LANES:] for h in range(HEADS)],
+        gb[HEADS][:LANES],
+        gb[HEADS][LANES:],
+    )
     for h in range(HEADS):
-        hot = (lane_head == h).astype(BF16)
-        hrows = slice(h * WTOK, (h + 1) * WTOK)
-        shift = bias_ref[0, hrows, :].astype(F32) * LOG2E + mask_add
-        gb = None
-        for w in range(lon_windows):
-            q, k, v, m = parts[w]
-            qm = q * hot
-            mg = m * hot
-            qm_s[w, hrows, :] = qm
-            mm_s[w, hrows, :] = mg
-            s = mm(qm, k, 1, 1) * (scale * LOG2E) + shift
-            dp = mm(mg, v, 1, 1)
-            e = jnp.exp2(s - jnp.max(s, axis=1, keepdims=True))
-            p = e * (1.0 / jnp.sum(e, axis=1, keepdims=True))
-            delta = jnp.sum(p * dp, axis=1, keepdims=True)
-            ds = p * (dp - delta)
-            pb = p.astype(BF16)
-            dsb = ds.astype(BF16)
-            p_s[w, hrows, :] = pb
-            ds_s[w, hrows, :] = dsb
-            gb = ds if gb is None else gb + ds
-            mixed[w] = mixed[w] + mm(pb, v * hot)
-            dq[w] = dq[w] + mm(dsb, k * hot)
-        gb = gb.astype(BF16)
-        gbias_ref[step, hrows, :] = gb[:, :LANES]
-        gbias_ref[step, HEADS * WTOK : HEADS * WTOK + WTOK, h * TAIL : (h + 1) * TAIL] = gb[:, LANES:]
-    cols = []
-    for w in range(lon_windows):
-        dk = mm(ds_s[w], qm_s[w], 0, 0) * scale
-        dv = mm(p_s[w], mm_s[w], 0, 0)
-        cols.append(
-            jnp.concatenate(
-                [(dq[w] * scale).astype(BF16), dk.astype(BF16), dv.astype(BF16)], axis=1
-            )
-        )
-    cols = jnp.concatenate(cols, axis=0)
-    mixed_b = jnp.concatenate([t.astype(BF16) for t in mixed], axis=0)
-    gproj_ref[...] += mm(mixed_b, c, 0, 0)
-    gqkv_ref[...] += mm(x, cols, 0, 0)
-    gin = mm(cols, wqkv_ref[...], 1, 1).astype(BF16)
-    gout = mm(perm, gin, 0, 0).astype(BF16)
-    gframe_ref[...] = gout.reshape(gframe_ref.shape)
+        gbias_s[step, h * WTOK : h * WTOK + LANES, :] = mains_t[h].astype(BF16)
+        gbias_s[step, h * WTOK + LANES : (h + 1) * WTOK, :] = under_t[h].astype(BF16)
+    gbias_s[step, stack : stack + LANES, :] = right_t.astype(BF16)
+    gbias_s[step, stack + LANES : stack + WTOK, :] = corner_t.astype(BF16)
+
+    ex = Exchange(
+        n, kinds,
+        (gbias_s, pair_s, sum_s, cross_s, red_s, gbias_hbm),
+        (pair_sem, cross_sem, back_sem, fwd_sem, store_sem),
+    )
+    ex.behind(step)
     ex.pair_copy(step).start()
 
     @pl.when(step == kinds - 1)
@@ -385,19 +708,82 @@
         share = channels // n
         for i in range(n):
             rows = slice(i * share, (i + 1) * share)
-            wg_s[i, :, : 3 * channels] = gqkv_ref[rows].astype(BF16)
-            wg_s[i, :, 3 * channels :] = gproj_ref[rows].astype(BF16)
+            for j in range(3):
+                wg_s[i, j * share : (j + 1) * share, :] = gqkv_s[j, rows].astype(BF16)
+            wg_s[i, 3 * share :, :] = gproj_s[rows].astype(BF16)
         ws = WeightSum(n, lats, wg_s, w1_s, w2_s, w3_s, (w1_sem, w2_sem, w3_sem))
         ws.start()
         ex.behind(kinds)
+        for late in range(kinds - GRAD_LAG, kinds):
+            halo.finish(late % level_windows, late // level_windows)
+        ex.behind(kinds + 1)
         ws.step_one()
-        ex.behind(kinds + 1)
-        ws.step_two()
         ex.behind(kinds + 2)
         ex.behind(kinds + 3)
+        ws.step_two()
+        ex.behind(kinds + 4)
+        ex.behind(kinds + 5)
         ws.finish()
         wout_ref[...] = w3_s[...]
         ex.drain()
+        halo.end()
+
+
+def pack_kernel(table_ref, main_ref, tail_ref, main_s, tail_s):
+    h = pl.program_id(0)
+    kinds = table_ref.shape[1]
+    group = LANES // TAIL
+    lane = lax.broadcasted_iota(jnp.int32, (kinds, LANES), 1)
+
+    def body(m, _):
+        tiles = []
+        for r in range(group + 1):
+            start = pl.multiple_of(m * (group * WTOK) + r * LANES, LANES)
+            tiles.append(table_ref[0, :, pl.ds(start, LANES)].astype(F32))
+        for r in range(group):
+            turn = (LANES - TAIL * r) % LANES
+            left = pltpu.roll(tiles[r], turn, 1) if r else tiles[r]
+            right = pltpu.roll(tiles[r + 1], turn, 1) if r else tiles[r + 1]
+            whole = jnp.where(lane < LANES - TAIL * r, left, right) if r else left
+            at = m * group + r
+            main_s[pl.ds(at, kinds, stride=WTOK), :] = whole
+            tail_s[pl.ds(at, kinds, stride=WTOK), :] = right
+        return 0
+
+    lax.fori_loop(0, WTOK // group, body, 0)
+    wide = lax.broadcasted_iota(jnp.int32, (WTOK, LANES), 1) // TAIL
+
+    def out(t, _):
+        at = pl.ds(pl.multiple_of(t * WTOK, WTOK), WTOK)
+        main_ref[t, 0] = main_s[at, :].astype(BF16)
+        turned = pltpu.roll(tail_s[at, :], h * TAIL, 1)
+        before = jnp.where(h == 0, 0.0, tail_ref[t].astype(F32))
+        tail_ref[t] = jnp.where(wide == h, turned, before).astype(BF16)
+        return 0
+
+    lax.fori_loop(0, kinds, out, 0)
+
+
+def pack(table):
+    heads, kinds, flat = table.shape
+    main, tail = pl.pallas_call(
+        pack_kernel,
+        grid=(heads,),
+        in_specs=[pl.BlockSpec((1, kinds, flat), lambda i: (i, 0, 0))],
+        out_specs=[
+            pl.BlockSpec((kinds, 1, WTOK, LANES), lambda i: (0, i, 0, 0)),
+            pl.BlockSpec((kinds, WTOK, LANES), lambda i: (0, 0, 0)),
+        ],
+        out_shape=[
+            jax.ShapeDtypeStruct((kinds, heads, WTOK, LANES), BF16),
+            jax.ShapeDtypeStruct((kinds, WTOK, LANES), BF16),
+        ],
+        scratch_shapes=[pltpu.VMEM((kinds * WTOK, LANES), F32)] * 2,
+        cost_estimate=pl.CostEstimate(
+            flops=10_000_000_000, bytes_accessed=10_000_000, transcendentals=0
+        ),
+    )(table)
+    return main, tail
 
 
 def unpack_kernel(packed_ref, out_ref, main_s, tail_s):
@@ -456,70 +842,86 @@
     )(packed)
 
 
-def window_call(last, perm, frame_in, frame_cot, weight_qkv, weight_proj, bias):
-    levels, height, wide, channels = frame_in.shape
+def window_call(perm, back, normed, cotangent, wqkv, wback, wproj, bias, side):
+    levels, height, breadth, channels = normed.shape
     level_windows = levels // WIN_Z
     lat_windows = height // WIN_LAT
     lon_windows = perm.shape[0] // WTOK
     kinds = lat_windows * level_windows
     n, lats = lax.axis_size("lon"), lax.axis_size("lat")
     chips = n // 2
-
-    def at(step, up):
-        z = lax.rem(WIN_Z * lax.rem(step, level_windows) + up, levels)
-        return z, step // level_windows, 0, 0
-
-    tok = (1, WIN_LAT, wide, channels)
-    low = pl.BlockSpec(tok, lambda i: at(i, 1))
-    high = pl.BlockSpec(tok, lambda i: at(i, 2))
+    shift = WIN_LAT // 2
+    rows = height // shift
+
+    def tokens(up, lower):
+        def at(i):
+            z = lax.rem(WIN_Z * lax.rem(i, level_windows) + 1 + up, levels)
+            row = 1 + 2 * (i // level_windows) + lower
+            return z, jnp.minimum(row, rows - 1), 0, 0
+
+        return pl.BlockSpec((1, shift, breadth, channels), at)
+
+    blocks = [tokens(up, lower) for up in range(WIN_Z) for lower in range(2)]
     whole = lambda arr: pl.BlockSpec(arr.shape, lambda i: (0,) * arr.ndim)
     const = lambda shape: pl.BlockSpec(shape, lambda i: (0,) * len(shape))
+    anywhere = pl.BlockSpec(memory_space=pl.ANY)
     stack = HEADS * WTOK
-    share = channels // n
+    padded = (HEADS + 1) * LANES
+    turned = (lon_windows + 1) * LANES
+    wgrad = (4 * channels // n, channels)
     sem = lambda *k: pltpu.SemaphoreType.DMA((2,) + k)
     return pl.pallas_call(
         functools.partial(kernel, n, lats, kinds, lat_windows, level_windows, lon_windows),
         grid=(kinds,),
         in_specs=[
-            pl.BlockSpec(memory_space=pltpu.SMEM),
             whole(perm),
-            low,
-            high,
-            low,
-            high,
-            whole(weight_qkv),
-            whole(weight_proj),
-            pl.BlockSpec((1, stack, WTOK), lambda i: (i, 0, 0)),
+            whole(back),
+            *blocks,
+            *blocks,
+            anywhere,
+            anywhere,
+            whole(wqkv),
+            whole(wback),
+            whole(wproj),
+            pl.BlockSpec((1, stack, LANES), lambda i: (i, 0, 0)),
+            pl.BlockSpec((1, WTOK, LANES), lambda i: (i, 0, 0)),
         ],
-        out_specs=[
-            pl.BlockSpec(
-                (WIN_Z, WIN_LAT, wide, channels),
-                lambda i: (lax.rem(i, level_windows), i // level_windows, 0, 0),
-            ),
-            const((n, share, 4 * channels)),
-            pl.BlockSpec(memory_space=pl.ANY),
-        ],
+        out_specs=[const((n,) + wgrad), anywhere, anywhere],
         out_shape=[
-            jax.ShapeDtypeStruct((levels, height, wide, channels), BF16),
-            jax.ShapeDtypeStruct((n, share, 4 * channels), BF16),
+            jax.ShapeDtypeStruct((n,) + wgrad, BF16),
             jax.ShapeDtypeStruct((kinds, PACKED, LANES), BF16),
+            jax.ShapeDtypeStruct(normed.shape, BF16),
         ],
         scratch_shapes=[
-            pltpu.VMEM((lon_windows, stack, channels), BF16),
-            pltpu.VMEM((lon_windows, stack, channels), BF16),
-            pltpu.VMEM((lon_windows, stack, WTOK), BF16),
-            pltpu.VMEM((lon_windows, stack, WTOK), BF16),
-            pltpu.VMEM((channels, 3 * channels), F32),
+            pltpu.VMEM((lon_windows, padded, channels), BF16),
+            pltpu.VMEM((lon_windows, padded, channels), BF16),
+            pltpu.VMEM((lon_windows, channels, padded), BF16),
+            pltpu.VMEM((lon_windows, channels, padded), BF16),
+            pltpu.VMEM((lon_windows, channels, WTOK), BF16),
+            pltpu.VMEM((lon_windows, channels, WTOK), BF16),
+            pltpu.VMEM((lon_windows, WTOK, padded), BF16),
+            pltpu.VMEM((lon_windows, WTOK, padded), BF16),
+            pltpu.VMEM((WTOK, padded), F32),
+            pltpu.VMEM((channels, turned), BF16),
+            pltpu.VMEM((channels, turned), BF16),
+            pltpu.VMEM((3, channels, channels), F32),
             pltpu.VMEM((channels, channels), F32),
             pltpu.VMEM((kinds, PACKED, LANES), BF16),
             pltpu.VMEM((kinds, PACKED // 2, LANES), BF16),
             pltpu.VMEM((kinds, PACKED // 2, LANES), BF16),
             pltpu.VMEM((kinds, chips, PACKED // n, LANES), BF16),
             pltpu.VMEM((kinds, PACKED, LANES), BF16),
-            pltpu.VMEM((n, share, 4 * channels), BF16),
-            pltpu.VMEM((n, share, 4 * channels), BF16),
-            pltpu.VMEM((lats, share, 4 * channels), BF16),
-            pltpu.VMEM((n, share, 4 * channels), BF16),
+            pltpu.VMEM((n,) + wgrad, BF16),
+            pltpu.VMEM((n,) + wgrad, BF16),
+            pltpu.VMEM((lats,) + wgrad, BF16),
+            pltpu.VMEM((n,) + wgrad, BF16),
+            pltpu.VMEM((2, levels, height, HALO, channels), BF16),
+            pltpu.VMEM((2, levels, shift, breadth, channels), BF16),
+            pltpu.VMEM((levels, height + shift, breadth, channels), BF16),
+            pltpu.VMEM((levels, height, HALO, channels), BF16),
+            pltpu.VMEM((levels, height, HALO, channels), BF16),
+            pltpu.VMEM((levels, shift, breadth, channels), BF16),
+            pltpu.VMEM((2, WIN_Z, shift, breadth, channels), BF16),
             sem(kinds),
             sem(kinds, chips),
             sem(kinds, chips),
@@ -528,6 +930,11 @@
             sem(n),
             sem(lats),
             sem(n),
+            sem(2, lat_windows + 1, levels),
+            sem(2, levels),
+            sem(lat_windows + 1, levels),
+            sem(levels),
+            pltpu.SemaphoreType.DMA((lat_windows + 1, levels)),
         ],
         compiler_params=pltpu.CompilerParams(
             dimension_semantics=("arbitrary",),
@@ -539,50 +946,45 @@
             flops=kinds * 1_500_000_000, bytes_accessed=kinds * 2_000_000, transcendentals=0
         ),
     )(
-        last, perm, frame_in, frame_in, frame_cot, frame_cot, weight_qkv, weight_proj, bias
+        perm, back, *[normed] * 4, *[cotangent] * 4, normed, cotangent,
+        wqkv, wback, wproj, bias, side,
     )
 
 
 def local(normed, cotangent, weight_qkv, weight_proj, bias_table):
     levels, height, breadth, channels = normed.shape
-    lat_shift = WIN_LAT // 2
     lon_shift = WIN_LON // 2
     lon_windows = breadth // WIN_LON
-    wide = breadth + HALO
-    across = ring_permute((normed[:, :, :HALO], cotangent[:, :, :HALO]), "lon", -1)
-    wide_in = jnp.concatenate([normed, across[0]], axis=2)
-    wide_cot = jnp.concatenate([cotangent, across[1]], axis=2)
-    upward = line_permute((wide_in[:, :lat_shift], wide_cot[:, :lat_shift]), "lat", -1)
-    frame_in = jnp.concatenate([wide_in[:, lat_shift:], upward[0]], axis=1)
-    frame_cot = jnp.concatenate([wide_cot[:, lat_shift:], upward[1]], axis=1)
-    last = (lax.axis_index("lat") == lax.axis_size("lat") - 1).astype(jnp.int32).reshape(1)
-    bias = bias_table.reshape(bias_table.shape[0], HEADS * WTOK, WTOK)
+    bias, side = pack(jnp.swapaxes(bias_table, 0, 1))
+    bias = bias.reshape(bias.shape[0], HEADS * WTOK, LANES)
+    wqkv = jnp.stack(jnp.split(weight_qkv, 3, axis=1))
+    wback = jnp.swapaxes(wqkv, 1, 2)
+    wproj = weight_proj.T
 
     rows = jnp.arange(lon_windows * WTOK, dtype=jnp.int32)
-    token = rows % WTOK
+    mains = lon_windows * LANES
+    is_main = rows < mains
+    window = jnp.where(is_main, rows // LANES, (rows - mains) // TAIL)
+    token = jnp.where(is_main, rows % LANES, LANES + (rows - mains) % TAIL)
     per_level = WIN_LAT * WIN_LON
-    source = (
-        token // per_level * (WIN_LAT * wide)
-        + token % per_level // WIN_LON * wide
-        + rows // WTOK * WIN_LON
-        + token % WIN_LON
-        + lon_shift
+    level = token // per_level
+    row = token % per_level // WIN_LON
+    place = window * WIN_LON + token % WIN_LON + lon_shift
+    near, far = WIN_LAT * breadth, WIN_LAT * HALO
+    source = jnp.where(
+        place < breadth,
+        level * near + row * breadth + place,
+        WIN_Z * near + level * far + row * HALO + place - breadth,
     )
-    columns = jnp.arange(WIN_Z * WIN_LAT * wide, dtype=jnp.int32)
+    columns = jnp.arange(WIN_Z * (near + far), dtype=jnp.int32)
     perm = (source[:, None] == columns[None, :]).astype(BF16)
 
-    gframe, weights, packed = window_call(
-        last, perm, frame_in, frame_cot, weight_qkv, weight_proj, bias
+    weights, packed, input_grad = window_call(
+        perm, perm.T, normed, cotangent, wqkv, wback, wproj, bias, side
     )
-    weights = weights.reshape(channels, 4 * channels).astype(F32)
-
-    gwide = jnp.roll(gframe, WIN_Z // 2, axis=0)
-    side = ring_permute(gwide[:, :, breadth:], "lon", 1)
-    seam = jnp.concatenate(
-        [gwide[:, :, :HALO] + side, gwide[:, :, HALO:breadth]], axis=2
-    )
-    down = line_permute(seam[:, height - lat_shift :], "lat", 1)
-    input_grad = jnp.concatenate([down, seam[:, : height - lat_shift]], axis=1)
+    n = lax.axis_size("lon")
+    weights = weights.reshape(n, 4, channels // n, channels).astype(F32)
+    weights = weights.transpose(0, 2, 1, 3).reshape(channels, 4 * channels)
 
     bias_grad = unpack(packed)
     return input_grad, weights[:, : 3 * channels], weights[:, 3 * channels :], bias_grad

time: 232 us -> 169 us (0.73)
  local copies, waits for them, and re-layouts: 37.9 us -> 17.7 us
  waiting for transfers between devices: 12.5 us -> 0 us
  Pallas kernels: 158 us -> 146 us
  starting transfers between devices: 10.6 us -> 0 us
  other arithmetic: 11.3 us -> 3.48 us
    pallas_call x1, Pallas kernels: 142 us -> 107 us  [window_call(): pl.pallas_call(functools.partial(kernel, n, lats, kinds, lat_windows, lev...]
    pallas_call x0 -> x1, Pallas kernels: none -> 23.4 us  [pack(): pl.pallas_call(pack_kernel, grid=(heads,), in_specs=[pl.BlockSpec((1, kin...]
    reshape x1 -> x2, local copies, waits for them, and re-layouts: 13.8 us -> 0.79 us  [local(): weights = weights.transpose(0, 2, 1, 3).reshape(channels, 4 * channels)]
    ppermute x6 -> x0, waiting for transfers between devices: 12.5 us -> none  [the longest x3 12.5 us: ring_permute(): lax.ppermute(block, axis, [((i - distance) % size, i) for i in range(size)])]
    ppermute x6 -> x0, starting transfers between devices: 10.6 us -> none  [the longest x3 6.1 us: line_permute(): return lax.ppermute(block, axis, route)]
    slice x10 -> x0, local copies, waits for them, and re-layouts: 9.75 us -> none  [the longest x2 3.12 us: local(): gwide = jnp.roll(gframe, WIN_Z // 2, axis=0)]
    concatenate x4 -> x0, other arithmetic: 7.7 us -> none  [the longest x1 3.19 us: local(): frame_cot = jnp.concatenate([wide_cot[:, lat_shift:], upward[1]], axis=1)]
    unnamed x14 -> x8, local copies, waits for them, and re-layouts: 12.5 us -> 13.3 us
  transfers between devices with their start and end apart: 6 -> 0, of which waited for: 2 -> 0; matrix products, arithmetic and copies ran while one was open for 16% -> 0% of each run, Pallas kernels for 7% -> 0%
where the time goes in v2:
time: 169 us; the launch traced here: 168 us
  Pallas kernels  146 us (86%)
  local copies, waits for them, and re-layouts  17.7 us (10%)
  other arithmetic  3.48 us (2%)
    pallas_call x1, Pallas kernels, window_call(): pl.pallas_call(functools.partial(kernel, n, lats, kinds, lat_windows, lev...  107 us
    pallas_call x1, Pallas kernels, pack(): pl.pallas_call(pack_kernel, grid=(heads,), in_specs=[pl.BlockSpec((1, kin...  23.4 us
    pallas_call x1, Pallas kernels, unpack(): pl.pallas_call(unpack_kernel, grid=(kinds,), in_specs=[pl.BlockSpec((1, r...  15.9 us
    unnamed x8, local copies, waits for them, and re-layouts  13.3 us

profile of v2, /device:TPU:0, one launch (start us, length us, event | category | flops | bytes accessed | tf_op | source)
XLA Modules:
  0.0 168.0 jit_solution(10517971280025241954)
XLA Ops:
  0.7 1.6 copy.12
  2.3 0.8 fusion.1.perm_ref
  3.1 0.8 fusion.back_ref
  3.9 1.1 fusion.25
  5.0 0.1 copy.16
  5.1 0.1 copy.17
  5.2 0.1 copy.18
  5.3 0.8 fusion.24
  6.1 0.9 copy.13.wqkv_ref
  7.0 23.4 %shard_map.84 = (bf16[16,6,144,128]{3,2,1,0:T(8,128)(2,1)}, bf16[16,144,128]{2,1,0:T(8,128)(2,1)}) custom-call(bf16[6,16,20736]{2,1,0:T(8,128)(2,1)} %bitcast.17), custom_call_target="tpu_custom_call" | custom-call | flops 10000000000 | bytes 10000000 | tf_op jit(solution)/shard_map/pallas_call | solution.py:769
  30.4 106.8 %shard_map.85 = (bf16[8,96,192]{2,1,0:T(8,128)(2,1)}, bf16[16,1024,128]{2,1,0:T(8,128)(2,1)}, bf16[8,24,24,192]{3,2,1,0:T(8,128)(2,1)}) custom-call(bf16[288,384]{1,0:T(8,128)(2,1)} %fusion.1.perm_ref, bf16[384,288]{1,0:T(8,128)(2,1)} %fusion.back_ref, bf16[8,24,24,192]{3,2,1,0:T(8,128)(2,1)} %x_hbm.1, bf16[8,24,24,192]{3,2,1,0:T(8,128)(2,1)} %x_hbm.1, ...), custom_call_target="tpu_custom_call" | custom-call | flops 24000000000 | bytes 32000000 | tf_op jit(solution)/shard_map/pallas_call | solution.py:873
  137.3 1.1 convert_bitcast_fusion
  138.3 0.3 copy.14
  138.7 0.5 reshape.118
  139.2 0.8 slice.9
  139.9 0.8 slice.8
  140.8 15.9 %shard_map.86 = f32[16,6,20736]{2,1,0:T(8,128)} custom-call(bf16[16,1024,128]{2,1,0:T(8,128)(2,1)} %get-tuple-element.13.packed_ref), custom_call_target="tpu_custom_call" | custom-call | flops 10000000000 | bytes 15000000 | tf_op jit(solution)/shard_map/pallas_call | solution.py:832
  156.7 0.0 copy-start
  156.7 10.0 %copy.15 = f32[16,6,20736]{2,0,1:T(8,128)} copy(f32[16,6,20736]{2,1,0:T(8,128)} %shard_map.86) | data formatting | bytes 15925248
  166.6 0.0 copy-done
  166.6 1.4 copy.20
  (1 shorter events, 0.0 us)
Async XLA Ops:
  156.7 10.0 %copy-start = (bf16[8,24,24,192]{3,2,1,0:T(8,128)(2,1)S(1)}, bf16[8,24,24,192]{3,2,1,0:T(8,128)(2,1)}, u32[]{:S(2)}) copy-start(bf16[8,24,24,192]{3,2,1,0:T(8,128)(2,1)} %get-tuple-element.27) | copy-start | bytes 5308420

commit v3 on v2

v3 whole, which is shorter than its diff:
```python
import functools
import math

import jax
import jax.numpy as jnp
import numpy as np
from jax import lax
from jax.experimental import pallas as pl
from jax.experimental.pallas import tpu as pltpu
from jax.sharding import PartitionSpec as P

HEADS = 6
WIN_Z = 2
WIN_LAT = 6
WIN_LON = 12
WTOK = 144
LANES = 128
TAIL = WTOK - LANES
HALO = 8
PACKED = 1024
GRAD_LAG = 2
LAGS = (1, 3, 5, 7, 9, 10)
UNROLL = 3
ODD = WTOK + 1
LOG2E = math.log2(math.e)
F32 = jnp.float32
BF16 = jnp.bfloat16


def mm(a, b, ca=1, cb=0):
    return lax.dot_general(a, b, (((ca,), (cb,)), ((), ())), preferred_element_type=F32)


class Exchange:
    def __init__(self, n, kinds, bufs, sems):
        self.n, self.kinds = n, kinds
        self.chips = n // 2
        self.gb, self.pair, self.sum, self.cross, self.out, self.hbm = bufs
        self.pair_sem, self.cross_sem, self.back_sem, self.fwd_sem, self.store_sem = sems
        me = lax.axis_index("lon")
        self.me = me
        self.core = lax.rem(me, 2)
        self.chip = me // 2
        self.other = 1 - self.core
        self.partner = self.chip * 2 + self.other
        self.half = PACKED // 2
        self.part = self.half // self.chips

    def remote(self, src, dst, send, recv, device):
        return pltpu.make_async_remote_copy(
            src_ref=src, dst_ref=dst, send_sem=send, recv_sem=recv,
            device_id={"lon": device}, device_id_type=pl.DeviceIdType.MESH,
        )

    def peer(self, o):
        return lax.rem(self.chip + o, self.chips)

    def rows(self, core, chip):
        return pl.ds(core * self.half + chip * self.part, self.part)

    def pair_copy(self, t):
        src = self.gb.at[t, pl.ds(self.other * self.half, self.half)]
        return self.remote(
            src, self.pair.at[t], self.pair_sem.at[0, t], self.pair_sem.at[1, t], self.partner
        )

    def cross_copy(self, t, o, arriving):
        j = self.peer(o)
        src = self.sum.at[t, pl.ds(j * self.part, self.part)]
        slot = j if arriving else self.chip
        return self.remote(
            src, self.cross.at[t, slot], self.cross_sem.at[0, t, j],
            self.cross_sem.at[1, t, slot], j * 2 + self.core,
        )

    def back_copy(self, t, o, arriving):
        j = self.peer(o)
        slot = j if arriving else self.chip
        part = self.out.at[t, self.rows(self.core, slot)]
        return self.remote(
            part, part, self.back_sem.at[0, t, j], self.back_sem.at[1, t, slot],
            j * 2 + self.core,
        )

    def fwd_copy(self, t, arriving):
        core = self.other if arriving else self.core
        part = self.out.at[t, pl.ds(core * self.half, self.half)]
        return self.remote(
            part, part, self.fwd_sem.at[0, t], self.fwd_sem.at[1, t], self.partner
        )

    def store(self, t):
        return pltpu.make_async_copy(self.out.at[t], self.hbm.at[t], self.store_sem.at[t])

    def stage_pair(self, t):
        self.pair_copy(t).wait_recv()
        mine = self.gb[t, pl.ds(self.core * self.half, self.half)].astype(F32)
        total = (mine + self.pair[t].astype(F32)).astype(BF16)
        self.sum[t] = total
        for o in range(1, self.chips):
            self.cross_copy(t, o, False).start()

    def stage_cross(self, t):
        for o in range(1, self.chips):
            self.cross_copy(t, o, True).wait_recv()
        acc = self.sum[t, pl.ds(self.chip * self.part, self.part)].astype(F32)
        for o in range(1, self.chips):
            acc = acc + self.cross[t, self.peer(o)].astype(F32)
        self.out[t, self.rows(self.core, self.chip)] = acc.astype(BF16)
        for o in range(1, self.chips):
            self.back_copy(t, o, False).start()

    def stage_back(self, t):
        for o in range(1, self.chips):
            self.back_copy(t, o, True).wait_recv()
        self.fwd_copy(t, False).start()

    def stage_fwd(self, t):
        self.fwd_copy(t, True).wait_recv()
        self.store(t).start()

    def stages(self):
        return [self.stage_pair, self.stage_cross, self.stage_back, self.stage_fwd]

    def behind(self, step):
        for lag, stage in zip(LAGS, self.stages()):
            t = step - lag
            if isinstance(t, int):
                if 0 <= t < self.kinds:
                    stage(t)
            else:
                pl.when(t >= 0)(functools.partial(stage, t))

    def rest(self):
        stages = self.stages()
        done = [self.kinds - lag for lag in LAGS[: len(stages)]]
        while done[-1] < self.kinds:
            limit = [self.kinds] + done[:-1]
            for k, stage in enumerate(stages):
                for t in range(done[k], min(done[k] + 2, limit[k])):
                    stage(t)
                done[k] = max(done[k], min(done[k] + 2, limit[k]))
            yield

    def drain(self):
        def body(t, _):
            self.pair_copy(t).wait_send()
            for o in range(1, self.chips):
                self.cross_copy(t, o, False).wait_send()
                self.back_copy(t, o, False).wait_send()
            self.fwd_copy(t, False).wait_send()
            self.store(t).wait()
            return 0

        lax.fori_loop(0, self.kinds, body, 0)


class Square(Exchange):
    def __init__(self, n, kinds, bufs, sems):
        pair_bufs, one, sums, two = bufs[:3] + bufs[4:], bufs[3][0], bufs[3][1], bufs[3][2]
        gb, pair, total, out, hbm = pair_bufs
        super().__init__(n, kinds, (gb, pair, total, None, out, hbm), sems)
        self.one, self.sums, self.two = one, sums, two
        bits = (lax.rem(self.chip, 2), self.chip // 2)
        flip_x = self.chip + 1 - 2 * bits[0]
        flip_y = lax.rem(self.chip + 2, self.chips)
        self.first = (flip_x * 2 + self.core, flip_y * 2 + self.core)
        self.second = self.first[::-1]
        self.bit = bits
        self.other_bit = bits[::-1]
        self.plane = self.half // 2
        self.send_sem, self.step_sem = sems[0], sems[1]

    def coarse(self, p, bit):
        return pl.ds(p * self.plane + bit * (self.plane // 2), self.plane // 2)

    def fine(self, bit):
        return pl.ds(bit * (self.plane // 4), self.plane // 4)

    def placed(self, t, p, start, rows):
        at = self.core * self.half + p * self.plane + start
        return self.out.at[t, pl.ds(at, rows)]

    def pair_copy(self, t):
        src = self.gb.at[t, pl.ds(self.other * self.half, self.half)]
        return self.remote(
            src, self.pair.at[t], self.send_sem.at[0], self.step_sem.at[0, t], self.partner
        )

    def fwd_copy(self, t, arriving):
        core = self.other if arriving else self.core
        part = self.out.at[t, pl.ds(core * self.half, self.half)]
        return self.remote(
            part, part, self.send_sem.at[5], self.step_sem.at[5, t], self.partner
        )

    def copy(self, src, dst, k, t, device):
        return self.remote(src, dst, self.send_sem.at[k], self.step_sem.at[k, t], device)

    def one_copy(self, t, p):
        src = self.sum.at[t, self.coarse(p, 1 - self.bit[p])]
        return self.copy(src, self.one.at[t, p], 1, t, self.first[p])

    def two_copy(self, t, p):
        src = self.sums.at[t, p, self.fine(1 - self.other_bit[p])]
        return self.copy(src, self.two.at[t, p], 2, t, self.second[p])

    def three_copy(self, t, p):
        start = self.bit[p] * (self.plane // 2) + self.other_bit[p] * (self.plane // 4)
        part = self.placed(t, p, start, self.plane // 4)
        return self.copy(part, part, 3, t, self.second[p])

    def four_copy(self, t, p):
        part = self.placed(t, p, self.bit[p] * (self.plane // 2), self.plane // 2)
        return self.copy(part, part, 4, t, self.first[p])

    def both(self, buf, k, t):
        return self.copy(buf.at[t], buf.at[t], k, t, self.partner)

    def stage_pair(self, t):
        self.pair_copy(t).wait_recv()
        mine = self.gb[t, pl.ds(self.core * self.half, self.half)].astype(F32)
        self.sum[t] = (mine + self.pair[t].astype(F32)).astype(BF16)
        for p in range(2):
            self.one_copy(t, p).start()

    def stage_one(self, t):
        self.both(self.one, 1, t).wait_recv()
        for p in range(2):
            mine = self.sum[t, self.coarse(p, self.bit[p])].astype(F32)
            self.sums[t, p] = (mine + self.one[t, p].astype(F32)).astype(BF16)
        for p in range(2):
            self.two_copy(t, p).start()

    def stage_two(self, t):
        self.both(self.two, 2, t).wait_recv()
        for p in range(2):
            mine = self.sums[t, p, self.fine(self.other_bit[p])].astype(F32)
            total = (mine + self.two[t, p].astype(F32)).astype(BF16)
            start = self.bit[p] * (self.plane // 2) + self.other_bit[p] * (self.plane // 4)
            at = self.core * self.half + p * self.plane + start
            self.out[t, pl.ds(at, self.plane // 4)] = total
        for p in range(2):
            self.three_copy(t, p).start()

    def stage_three(self, t):
        self.both(self.two, 3, t).wait_recv()
        for p in range(2):
            self.four_copy(t, p).start()

    def stage_four(self, t):
        self.both(self.one, 4, t).wait_recv()
        self.fwd_copy(t, False).start()

    def store(self, t):
        return pltpu.make_async_copy(self.out.at[t], self.hbm.at[t], self.store_sem.at[0])

    def stages(self):
        return [
            self.stage_pair, self.stage_one, self.stage_two, self.stage_three,
            self.stage_four, self.stage_fwd,
        ]

    def drain(self):
        for k, buf in enumerate((self.pair, self.one, self.two, self.two, self.one, self.pair)):
            self.remote(
                buf, buf, self.send_sem.at[k], self.step_sem.at[k, 0], self.partner
            ).wait_send()
        pltpu.make_async_copy(self.out, self.hbm, self.store_sem.at[0]).wait()


class Halo:
    def __init__(self, n, lats, levels, level_windows, lat_windows, refs, sems):
        self.n, self.lats = n, lats
        self.levels, self.level_windows, self.lat_windows = levels, level_windows, lat_windows
        self.given, self.body, self.east, self.gl, self.gh, self.wh, self.nh, self.out = refs
        self.load_sem, self.east_sem, self.south_sem, self.wh_sem, self.nh_sem, self.out_sem = sems
        self.me, self.lat = lax.axis_index("lon"), lax.axis_index("lat")
        self.shift = WIN_LAT // 2
        self.height = lat_windows * WIN_LAT
        self.last = lat_windows - 1
        self.last_lat = self.lat == lats - 1
        self.strip = pl.ds(0, WIN_LON // 2)
        self.parts = ((1, WIN_Z), (1 + WIN_Z, levels - 1 - WIN_Z), (0, 1))

    def remote(self, src, dst, sems, at, lat, lon, send_at=None):
        device = {"lat": self.lat + lat, "lon": lax.rem(self.me + lon + self.n, self.n)}
        send = (0,) + (at if send_at is None else send_at)
        return pltpu.make_async_remote_copy(
            src_ref=src, dst_ref=dst, send_sem=sems.at[send], recv_sem=sems.at[(1,) + at],
            device_id=device, device_id_type=pl.DeviceIdType.MESH,
        )

    def count(self, bottom):
        return self.shift if bottom else WIN_LAT

    def load(self, i, b, bottom):
        rows = pl.ds(self.shift + b * WIN_LAT, self.count(bottom))
        return pltpu.make_async_copy(
            self.given[i].at[:, rows], self.body.at[i, :, rows], self.load_sem.at[i, b]
        )

    def east_copy(self, i, part, b, bottom):
        level = pl.ds(*self.parts[part])
        src = pl.ds(self.shift + b * WIN_LAT, self.count(bottom))
        dst = pl.ds(b * WIN_LAT, self.count(bottom))
        return self.remote(
            self.given[i].at[level, src, self.strip, :], self.east.at[i, level, dst, self.strip, :],
            self.east_sem, (i, b, part), 0, -1, (i, 0, 0),
        )

    def east_all(self, i):
        rows = pl.ds(self.shift, self.height - self.shift)
        src = self.given[i].at[:, rows, self.strip, :]
        dst = self.east.at[i, :, rows, self.strip, :]
        return self.remote(src, dst, self.east_sem, (i, 0, 0), 0, -1)

    def corner_copy(self, i):
        src, dst = pl.ds(0, self.shift), pl.ds(self.height - self.shift, self.shift)
        return self.remote(
            self.given[i].at[:, src, self.strip, :], self.east.at[i, :, dst, self.strip, :],
            self.east_sem, (i, self.lat_windows, 0), -1, -1,
        )

    def south_copy(self, i):
        src = self.given[i].at[:, pl.ds(0, self.shift)]
        dst = self.body.at[i, :, pl.ds(self.height, self.shift)]
        return self.remote(src, dst, self.south_sem, (i,), -1, 0)

    def begin(self):
        for b in range(self.lat_windows):
            for i in range(2):
                self.load(i, b, b == self.last).start()
        self.east[...] = jnp.zeros_like(self.east)
        self.wh[...] = jnp.zeros_like(self.wh)

        @pl.when(self.last_lat)
        def _():
            shape = self.body.shape
            blank = jnp.zeros(shape[:2] + (self.shift,) + shape[3:], BF16)
            self.body[:, :, pl.ds(self.height, self.shift)] = blank

        @pl.when(self.lat == 0)
        def _():
            self.nh[...] = jnp.zeros_like(self.nh)

    def send(self, b, bottom):
        for part in range(3):
            for i in range(2):
                self.east_copy(i, part, b, bottom).start()
        if bottom:
            @pl.when(self.lat > 0)
            def _():
                for i in range(2):
                    self.south_copy(i).start()
                    self.corner_copy(i).start()

    def send_next(self, b):
        pl.when(b + 1 < self.last)(lambda: self.send(b + 1, False))
        pl.when(b + 1 == self.last)(lambda: self.send(self.last, True))

    def pair(self, a):
        return [lax.rem(WIN_Z * a + 1 + u, self.levels) for u in range(WIN_Z)]

    def arrive_part(self, part, b, bottom):
        for i in range(2):
            if part == 0:
                self.load(i, b, bottom).wait()
            self.east_copy(i, part, b, bottom).wait_recv()
        if bottom and part == 0:
            @pl.when(jnp.logical_not(self.last_lat))
            def _():
                for i in range(2):
                    self.corner_copy(i).wait_recv()
                    self.south_copy(i).wait_recv()

    def arrive(self, a, b):
        at = (a == 0, a == 1, a == self.level_windows - 1)
        for part in range(3):
            pl.when(at[part] & (b < self.last))(
                functools.partial(self.arrive_part, part, b, False)
            )
            pl.when(at[part] & (b == self.last))(
                functools.partial(self.arrive_part, part, self.last, True)
            )

    def back_copy(self, b, bottom):
        src = pl.ds(b * WIN_LAT, self.count(bottom))
        dst = pl.ds(self.shift + b * WIN_LAT, self.count(bottom))
        return self.remote(
            self.gh.at[:, src, self.strip, :], self.wh.at[:, dst, self.strip, :],
            self.wh_sem, (b,), 0, 1,
        )

    def back_corner(self):
        src, dst = pl.ds(self.height - self.shift, self.shift), pl.ds(0, self.shift)
        return self.remote(
            self.gh.at[:, src, self.strip, :], self.wh.at[:, dst, self.strip, :],
            self.wh_sem, (self.lat_windows,), 1, 1,
        )

    def down_copy(self):
        src = self.gl.at[:, pl.ds(self.height, self.shift)]
        return self.remote(src, self.nh, self.nh_sem, (), 1, 0)

    def give_last(self):
        @pl.when(jnp.logical_not(self.last_lat))
        def _():
            self.back_corner().start()
            self.down_copy().start()

        self.back_copy(self.last, True).start()

    def store(self, b, bottom):
        rows = pl.ds(self.shift + b * WIN_LAT, self.count(bottom))
        return pltpu.make_async_copy(
            self.gl.at[:, rows], self.out.at[:, rows], self.out_sem.at[b]
        )

    def store_top(self):
        rows = pl.ds(0, self.shift)
        return pltpu.make_async_copy(
            self.nh, self.out.at[:, rows], self.out_sem.at[self.lat_windows]
        )

    def finish(self, b, bottom):
        self.back_copy(b, bottom).wait_recv()
        rows = pl.ds(self.shift + b * WIN_LAT, self.count(bottom))
        seam = self.gl[:, rows, :HALO].astype(F32) + self.wh[:, rows].astype(F32)
        self.gl[:, rows, :HALO] = seam.astype(BF16)
        self.store(b, bottom).start()

    def finish_top(self):
        @pl.when(self.lat > 0)
        def _():
            self.back_corner().wait_recv()
            self.down_copy().wait_recv()

        seam = self.nh[:, :, :HALO].astype(F32) + self.wh[:, : self.shift].astype(F32)
        self.nh[:, :, :HALO] = seam.astype(BF16)
        self.store_top().start()

    def end(self):
        for b in range(self.lat_windows):
            bottom = b == self.last
            self.back_copy(b, bottom).wait_send()
            self.store(b, bottom).wait()
        self.store_top().wait()
        for i in range(2):
            self.east_all(i).wait_send()

        @pl.when(self.lat > 0)
        def _():
            for i in range(2):
                self.south_copy(i).wait_send()
                self.corner_copy(i).wait_send()

        @pl.when(jnp.logical_not(self.last_lat))
        def _():
            self.back_corner().wait_send()
            self.down_copy().wait_send()


def enter(n, lats):
    me, lat = lax.axis_index("lon"), lax.axis_index("lat")
    barrier = pltpu.get_barrier_semaphore()
    for o in range(1, n):
        pl.semaphore_signal(
            barrier, inc=1, device_id={"lon": lax.rem(me + o, n)},
            device_id_type=pl.DeviceIdType.MESH,
        )
    for o in range(1, lats):
        pl.semaphore_signal(
            barrier, inc=1, device_id={"lat": lax.rem(lat + o, lats)},
            device_id_type=pl.DeviceIdType.MESH,
        )
    for o in (-1, 1):
        pl.semaphore_signal(
            barrier, inc=1,
            device_id={"lat": lax.rem(lat + o + lats, lats), "lon": lax.rem(me + o + n, n)},
            device_id_type=pl.DeviceIdType.MESH,
        )
    pl.semaphore_wait(barrier, n + lats)


class WeightSum:
    def __init__(self, n, lats, wg, w1, w2, wout, sems):
        self.n, self.lats = n, lats
        self.wg, self.w1, self.w2, self.wout = wg, w1, w2, wout
        self.sems = sems
        self.me, self.lat = lax.axis_index("lon"), lax.axis_index("lat")

    def remote(self, src, dst, k, device):
        return pltpu.make_async_remote_copy(
            src_ref=src, dst_ref=dst, send_sem=self.sems.at[0, k], recv_sem=self.sems.at[1, k],
            device_id=device, device_id_type=pl.DeviceIdType.MESH,
        )

    def every(self, buf, count, k):
        part = buf.at[pl.ds(0, count - 1)]
        return self.remote(part, part, k, {"lon": lax.rem(self.me + 1, self.n)})

    def start(self):
        for o in range(1, self.n):
            p = lax.rem(self.me + o, self.n)
            self.remote(self.wg.at[p], self.w1.at[self.me], 0, {"lon": p}).start()
        self.w1[pl.ds(self.me, 1)] = self.wg[pl.ds(self.me, 1)]

    def step_one(self):
        self.every(self.w1, self.n, 0).wait_recv()
        total = jnp.sum(self.w1[...].astype(F32), axis=0, keepdims=True)
        self.w2[pl.ds(self.lat, 1)] = total.astype(BF16)
        for o in range(1, self.lats):
            p = lax.rem(self.lat + o, self.lats)
            part = self.w2.at[self.lat]
            self.remote(part, part, 1, {"lat": p}).start()

    def step_two(self):
        self.every(self.w2, self.lats, 1).wait_recv()
        total = jnp.sum(self.w2[...].astype(F32), axis=0, keepdims=True)
        self.wout[pl.ds(self.me, 1)] = total.astype(BF16)
        for o in range(1, self.n):
            p = lax.rem(self.me + o, self.n)
            part = self.wout.at[self.me]
            self.remote(part, part, 2, {"lon": p}).start()

    def finish(self):
        self.every(self.wout, self.n, 2).wait_recv()
        self.every(self.w1, self.n, 0).wait_send()
        self.every(self.w2, self.lats, 1).wait_send()
        self.every(self.wout, self.n, 2).wait_send()


def flip(mains, under, right, corner):
    lane = lax.broadcasted_iota(jnp.int32, (TAIL, LANES), 1) // TAIL
    spare = jnp.zeros((LANES - HEADS * TAIL, LANES), F32)
    mains_t = [block.T for block in mains]
    right_t = jnp.concatenate(under + [spare], axis=0).T
    turned = right.T
    under_t = [turned[h * TAIL : (h + 1) * TAIL] for h in range(HEADS)]
    pad = jnp.zeros((LANES - TAIL, LANES), F32)
    turned = jnp.concatenate([corner, pad], axis=0).T
    corner_t = jnp.zeros((TAIL, LANES), F32)
    for h in range(HEADS):
        piece = turned[h * TAIL : (h + 1) * TAIL]
        if h:
            piece = pltpu.roll(piece, h * TAIL, 1)
        corner_t = jnp.where(lane == h, piece, corner_t)
    return mains_t, under_t, right_t, corner_t


def kernel(
    n,
    lats,
    kinds,
    lat_windows,
    level_windows,
    lon_windows,
    perm_ref,
    back_ref,
    x_hbm,
    c_hbm,
    wqkv_ref,
    wback_ref,
    wproj_ref,
    bias_ref,
    side_ref,
    gqkv_ref,
    gproj_ref,
    gbias_hbm,
    grad_hbm,
    q_s,
    m_s,
    qt_s,
    mt_s,
    kt_s,
    vt_s,
    p_s,
    ds_s,
    shift_s,
    mix_s,
    dqt_s,
    gqkv_s,
    gproj_s,
    gbias_s,
    pair_s,
    sum_s,
    cross_s,
    step_s,
    half_s,
    red_s,
    wg_s,
    w1_s,
    w2_s,
    w3_s,
    body_s,
    east_s,
    gl_s,
    gh_s,
    wh_s,
    nh_s,
    pair_sem,
    cross_sem,
    back_sem,
    fwd_sem,
    store_sem,
    w_sem,
    load_sem,
    east_sem,
    south_sem,
    wh_sem,
    nh_sem,
    out_sem,
):
    step = pl.program_id(0)
    a = lax.rem(step, level_windows)
    b = step // level_windows
    channels = wqkv_ref.shape[1]
    head_dim = channels // HEADS
    scale = head_dim ** -0.5
    levels = x_hbm.shape[0]
    shift = WIN_LAT // 2
    breadth = x_hbm.shape[2]
    tails = HEADS * LANES
    stack = HEADS * WTOK

    @pl.when(step == 0)
    def _():
        for ref in (gqkv_s, gproj_s, q_s, m_s, qt_s, mt_s):
            ref[...] = jnp.zeros_like(ref)
        gbias_s[:, stack + WTOK :, :] = jnp.zeros((kinds, PACKED - stack - WTOK, LANES), BF16)

    halo = Halo(
        n, lats, levels, level_windows, lat_windows,
        ((x_hbm, c_hbm), body_s, east_s, gl_s, gh_s, wh_s, nh_s, grad_hbm),
        (load_sem, east_sem, south_sem, wh_sem, nh_sem, out_sem),
    )

    @pl.when(step == 0)
    def _():
        halo.begin()
        enter(n, lats)
        halo.send(0, lat_windows == 1)

    halo.arrive(a, b)

    perm = perm_ref[...]
    bottom = b == lat_windows - 1

    def raw(which):
        flat = lambda t: t.reshape(-1, channels)
        zs = halo.pair(a)
        parts = [flat(body_s[which, z, pl.ds(shift + b * WIN_LAT, WIN_LAT)]) for z in zs]
        parts += [flat(east_s[which, z, pl.ds(b * WIN_LAT, WIN_LAT)]) for z in zs]
        return jnp.concatenate(parts, axis=0)

    x_raw, c_raw = raw(0), raw(1)
    x = mm(perm, x_raw).astype(BF16)
    c = mm(perm, c_raw).astype(BF16)
    q = (mm(x, wqkv_ref[0]) * (scale * LOG2E)).astype(BF16)
    k = mm(x, wqkv_ref[1]).astype(BF16)
    v = mm(x, wqkv_ref[2]).astype(BF16)
    m = mm(c, wproj_ref[...]).astype(BF16)

    wrap_here = a == level_windows - 1
    dead_here = bottom & (lax.axis_index("lat") == lats - 1)
    per_level = WTOK // WIN_Z

    def classes(token):
        upper = token >= per_level
        inner = jnp.where(upper, token - per_level, token)
        wrapped = jnp.where(upper & wrap_here, 2, 0)
        dead = jnp.where((inner >= per_level // 2) & dead_here, 1, 0)
        return wrapped + dead

    lane = lax.broadcasted_iota(jnp.int32, (1, LANES), 1)
    key_class = classes(lax.broadcasted_iota(jnp.int32, (WTOK, LANES), 0))
    mask_main = jnp.where(key_class == classes(lane), 0.0, -1e30)
    mask_tail = jnp.where(key_class == classes(LANES + lax.rem(lane, TAIL)), 0.0, -1e30)

    table = lambda lo, rows: bias_ref[0, lo : lo + rows, :].astype(F32) * LOG2E
    mains_t, under_t, right_t, corner_t = flip(
        [table(h * WTOK, LANES) for h in range(HEADS)],
        [table(h * WTOK + LANES, TAIL) for h in range(HEADS)],
        side_ref[0, :LANES, :].astype(F32) * LOG2E,
        side_ref[0, LANES:, :].astype(F32) * LOG2E,
    )
    for h in range(HEADS):
        cols = slice(h * LANES, (h + 1) * LANES)
        shift_s[:LANES, cols] = mains_t[h] + mask_main[:LANES]
        shift_s[LANES:, cols] = under_t[h] + mask_main[LANES:]
    shift_s[:LANES, tails:] = right_t + mask_tail[:LANES]
    shift_s[LANES:, tails:] = corner_t + mask_tail[LANES:]

    whole = lon_windows * LANES
    main = lambda w: slice(w * LANES, (w + 1) * LANES)
    tail = lambda w: slice(whole + w * TAIL, whole + (w + 1) * TAIL)
    window = lambda t, w: jnp.concatenate([t[main(w)], t[tail(w)]], axis=0)
    keys = [window(k, w) for w in range(lon_windows)]
    values = [window(v, w) for w in range(lon_windows)]
    for w in range(lon_windows):
        for flat, wide_s, turned_s in ((q, q_s, qt_s), (m, m_s, mt_s)):
            turned = flat[main(w)].T
            for h in range(HEADS):
                cs = slice(h * head_dim, (h + 1) * head_dim)
                wide_s[w, h * LANES : (h + 1) * LANES, cs] = flat[main(w), cs]
                wide_s[w, tails + h * TAIL : tails + (h + 1) * TAIL, cs] = flat[tail(w), cs]
                turned_s[w, cs, h * LANES : (h + 1) * LANES] = turned[cs]
            turned_s[w, :, tails:] = wide_s[w, tails:, :].T
        kt_s[w] = keys[w].T
        vt_s[w] = values[w].T

    tiles = HEADS + 1
    gb = []
    for j in range(0, tiles, 2):
        cols = slice(j * LANES, min(j + 2, tiles) * LANES)
        total = [None, None]
        for w in range(lon_windows):
            s2 = mm(keys[w], qt_s[w, :, cols])
            dp2 = mm(values[w], mt_s[w, :, cols])
            for i in range(min(2, tiles - j)):
                here = slice(i * LANES, (i + 1) * LANES)
                at = slice((j + i) * LANES, (j + i + 1) * LANES)
                s = s2[:, here] + shift_s[:, at]
                dp = dp2[:, here]
                e = jnp.exp2(s - jnp.max(s, axis=0, keepdims=True))
                r = 1.0 / jnp.sum(e, axis=0, keepdims=True)
                p = e * r
                delta = jnp.sum(p * dp, axis=0, keepdims=True)
                ds = p * (dp - delta)
                p_s[w, :, at] = p.astype(BF16)
                ds_s[w, :, at] = ds.astype(BF16)
                total[i] = ds if total[i] is None else total[i] + ds
        gb += total[: min(2, tiles - j)]

    tail_lane = lax.broadcasted_iota(jnp.int32, (head_dim, LANES), 1) // TAIL
    for turned_s, from_s, to_s, factor in ((vt_s, p_s, mix_s, None), (kt_s, ds_s, dqt_s, scale)):
        far = [None] * HEADS
        for w in range(lon_windows):
            for j in range(0, HEADS, 2):
                rows = slice(j * head_dim, (j + 2) * head_dim)
                out = mm(turned_s[w, rows, :], from_s[w, :, j * LANES : (j + 2) * LANES])
                if factor is not None:
                    out = out * factor
                for i in range(2):
                    cs = slice((j + i) * head_dim, (j + i + 1) * head_dim)
                    piece = out[i * head_dim : (i + 1) * head_dim, i * LANES : (i + 1) * LANES]
                    to_s[cs, main(w)] = piece.astype(BF16)
            out = mm(turned_s[w], from_s[w, :, tails:])
            if factor is not None:
                out = out * factor
            for h in range(HEADS):
                piece = out[h * head_dim : (h + 1) * head_dim]
                turn = (w - h) * TAIL % LANES
                if turn:
                    piece = pltpu.roll(piece, turn, 1)
                far[h] = jnp.where(tail_lane == w, piece, 0.0 if far[h] is None else far[h])
        for h in range(HEADS):
            cs = slice(h * head_dim, (h + 1) * head_dim)
            to_s[cs, whole:] = far[h].astype(BF16)

    dk, dv = [], []
    for w in range(lon_windows):
        dk.append((mm(ds_s[w], q_s[w]) * (1.0 / LOG2E)).astype(BF16))
        dv.append(mm(p_s[w], m_s[w]).astype(BF16))
    order = lambda ts: jnp.concatenate([t[:LANES] for t in ts] + [t[LANES:] for t in ts], axis=0)
    tokens = lon_windows * WTOK
    dq = dqt_s[...].T[:tokens]
    cols = [dq, order(dk), order(dv)]
    xt = x.T
    for i in range(3):
        gqkv_s[i] += mm(xt, cols[i])
    gproj_s[...] += mm(mix_s[:, :tokens], c)
    gin = mm(cols[0], wback_ref[0]) + mm(cols[1], wback_ref[1]) + mm(cols[2], wback_ref[2])
    gout = mm(back_ref[...], gin.astype(BF16)).astype(BF16)
    near, far = WIN_LAT * breadth, WIN_LAT * HALO
    for u, z in enumerate(halo.pair(a)):
        rows = pl.ds(shift + b * WIN_LAT, WIN_LAT)
        own = gout[u * near : (u + 1) * near]
        gl_s[z, rows] = own.reshape(WIN_LAT, breadth, channels)
        strip = gout[WIN_Z * near + u * far : WIN_Z * near + (u + 1) * far]
        gh_s[z, pl.ds(b * WIN_LAT, WIN_LAT)] = strip.reshape(WIN_LAT, HALO, channels)

    @pl.when((a == level_windows - 1) & (b < lat_windows - 1))
    def _():
        halo.back_copy(b, False).start()

    @pl.when(a == 0)
    def _():
        halo.send_next(b)

    @pl.when((a == GRAD_LAG - 1) & (b > 0))
    def _():
        halo.finish(b - 1, False)

    mains_t, under_t, right_t, corner_t = flip(
        [gb[h][:LANES] for h in range(HEADS)],
        [gb[h][LANES:] for h in range(HEADS)],
        gb[HEADS][:LANES],
        gb[HEADS][LANES:],
    )
    for h in range(HEADS):
        gbias_s[step, h * WTOK : h * WTOK + LANES, :] = mains_t[h].astype(BF16)
        gbias_s[step, h * WTOK + LANES : (h + 1) * WTOK, :] = under_t[h].astype(BF16)
    gbias_s[step, stack : stack + LANES, :] = right_t.astype(BF16)
    gbias_s[step, stack + LANES : stack + WTOK, :] = corner_t.astype(BF16)

    ex = (Square if n == 8 else Exchange)(
        n, kinds,
        (gbias_s, pair_s, sum_s, (cross_s, step_s, half_s) if n == 8 else cross_s, red_s, gbias_hbm),
        (pair_sem, cross_sem, back_sem, fwd_sem, store_sem),
    )
    ex.behind(step)
    ex.pair_copy(step).start()

    @pl.when(step == kinds - 1)
    def _():
        share = channels // n
        for i in range(n):
            rows = slice(i * share, (i + 1) * share)
            for j in range(3):
                wg_s[i, j * share : (j + 1) * share, :] = gqkv_s[j, rows].astype(BF16)
            wg_s[i, 3 * share :, :] = gproj_s[rows].astype(BF16)
        ws = WeightSum(n, lats, wg_s, w1_s, w2_s, w3_s, w_sem)
        ws.start()
        halo.give_last()
        for turn, _ in enumerate(ex.rest()):
            if turn == 1:
                ws.step_one()
            if turn == 2:
                halo.finish(lat_windows - 1, True)
                halo.finish_top()
            if turn == 3:
                ws.step_two()
        ws.finish()
        for p in range(n):
            rows = slice(p * share, (p + 1) * share)
            for j in range(3):
                cs = slice(j * channels, (j + 1) * channels)
                gqkv_ref[rows, cs] = w3_s[p, j * share : (j + 1) * share, :].astype(F32)
            gproj_ref[rows, :] = w3_s[p, 3 * share :, :].astype(F32)
        ex.drain()
        halo.end()


def pack_kernel(table_ref, main_ref, tail_ref, main_s, tail_s):
    h = pl.program_id(0)
    kinds = table_ref.shape[1]
    group = LANES // TAIL
    lane = lax.broadcasted_iota(jnp.int32, (kinds, LANES), 1)

    def body(m):
        tiles = []
        for r in range(group + 1):
            start = pl.multiple_of(m * (group * WTOK) + r * LANES, LANES)
            tiles.append(table_ref[0, :, pl.ds(start, LANES)].astype(F32))
        for r in range(group):
            turn = (LANES - TAIL * r) % LANES
            left = pltpu.roll(tiles[r], turn, 1) if r else tiles[r]
            right = pltpu.roll(tiles[r + 1], turn, 1) if r else tiles[r + 1]
            whole = jnp.where(lane < LANES - TAIL * r, left, right) if r else left
            at = pl.ds(m * group + r, kinds, stride=ODD)
            main_s[at, :] = whole
            tail_s[at, :] = right

    def several(i, _):
        for u in range(UNROLL):
            body(i * UNROLL + u)
        return 0

    lax.fori_loop(0, WTOK // group // UNROLL, several, 0)
    wide = lax.broadcasted_iota(jnp.int32, (WTOK, LANES), 1) // TAIL
    for t in range(kinds):
        at = slice(t * ODD, t * ODD + WTOK)
        main_ref[t, 0] = main_s[at, :].astype(BF16)
        turned = pltpu.roll(tail_s[at, :], h * TAIL, 1)
        before = jnp.where(h == 0, 0.0, tail_ref[t].astype(F32))
        tail_ref[t] = jnp.where(wide == h, turned, before).astype(BF16)


def pack(table):
    heads, kinds, flat = table.shape
    main, tail = pl.pallas_call(
        pack_kernel,
        grid=(heads,),
        in_specs=[pl.BlockSpec((1, kinds, flat), lambda i: (i, 0, 0))],
        out_specs=[
            pl.BlockSpec((kinds, 1, WTOK, LANES), lambda i: (0, i, 0, 0)),
            pl.BlockSpec((kinds, WTOK, LANES), lambda i: (0, 0, 0)),
        ],
        out_shape=[
            jax.ShapeDtypeStruct((kinds, heads, WTOK, LANES), BF16),
            jax.ShapeDtypeStruct((kinds, WTOK, LANES), BF16),
        ],
        scratch_shapes=[pltpu.VMEM((kinds * ODD, LANES), F32)] * 2,
        cost_estimate=pl.CostEstimate(
            flops=10_000_000_000, bytes_accessed=10_000_000, transcendentals=0
        ),
    )(table)
    return main, tail


def unpack_kernel(main_ref, tail_ref, out_ref, main_s, tail_s):
    h = pl.program_id(0)
    kinds = main_ref.shape[0]
    for t in range(kinds):
        at = slice(t * ODD, t * ODD + WTOK)
        main_s[at, :] = main_ref[t].astype(F32)
        tail_s[at, :] = pltpu.roll(tail_ref[t].astype(F32), (HEADS - h) * TAIL + LANES - HEADS * TAIL, 1)
    group = LANES // TAIL
    lane = lax.broadcasted_iota(jnp.int32, (kinds, LANES), 1)

    def body(m):
        before_main = before_tail = None
        for r in range(group + 1):
            tile = None
            if r < group:
                at = pl.ds(m * group + r, kinds, stride=ODD)
                here_main, here_tail = main_s[at, :], tail_s[at, :]
                if r:
                    here_main = pltpu.roll(here_main, TAIL * r, 1)
                    here_tail = pltpu.roll(here_tail, TAIL * r, 1)
                tile = here_main
            if r:
                ended = before_tail
                if r > 1:
                    ended = jnp.where(lane < TAIL * (r - 1), before_main, before_tail)
                tile = ended if r == group else jnp.where(lane < TAIL * r, ended, tile)
            start = pl.multiple_of(m * (group * WTOK) + r * LANES, LANES)
            out_ref[0, :, pl.ds(start, LANES)] = tile
            if r < group:
                before_main, before_tail = here_main, here_tail

    def several(i, _):
        for u in range(UNROLL):
            body(i * UNROLL + u)
        return 0

    lax.fori_loop(0, WTOK // group // UNROLL, several, 0)


def unpack(packed):
    kinds, _, lanes = packed.shape
    return pl.pallas_call(
        unpack_kernel,
        grid=(HEADS,),
        in_specs=[
            pl.BlockSpec((kinds, WTOK, lanes), lambda i: (0, i, 0)),
            pl.BlockSpec((kinds, WTOK, lanes), lambda i: (0, HEADS, 0)),
        ],
        out_specs=pl.BlockSpec((1, kinds, WTOK * WTOK), lambda i: (i, 0, 0)),
        out_shape=jax.ShapeDtypeStruct((HEADS, kinds, WTOK * WTOK), F32),
        scratch_shapes=[pltpu.VMEM((kinds * ODD, LANES), F32)] * 2,
        cost_estimate=pl.CostEstimate(
            flops=10_000_000_000, bytes_accessed=15_000_000, transcendentals=0
        ),
    )(packed, packed)


def window_call(perm, back, normed, cotangent, wqkv, wback, wproj, bias, side):
    levels, height, breadth, channels = normed.shape
    level_windows = levels // WIN_Z
    lat_windows = height // WIN_LAT
    lon_windows = perm.shape[0] // WTOK
    kinds = lat_windows * level_windows
    n, lats = lax.axis_size("lon"), lax.axis_size("lat")
    chips = n // 2
    shift = WIN_LAT // 2
    whole = lambda arr: pl.BlockSpec(arr.shape, lambda i: (0,) * arr.ndim)
    const = lambda shape: pl.BlockSpec(shape, lambda i: (0,) * len(shape))
    anywhere = pl.BlockSpec(memory_space=pl.ANY)
    stack = HEADS * WTOK
    padded = (HEADS + 1) * LANES
    turned = (lon_windows + 1) * LANES
    wgrad = (4 * channels // n, channels)
    sem = lambda *k: pltpu.SemaphoreType.DMA((2,) + k)
    dma = pltpu.SemaphoreType.DMA
    if n == 8:
        exchange_sems = [dma((6,)), dma((6, kinds)), dma((1,)), dma((1,)), dma((1,))]
    else:
        exchange_sems = [
            sem(kinds), sem(kinds, chips), sem(kinds, chips), sem(kinds), dma((kinds,))
        ]
    arriving = (2, PACKED // 8, LANES) if n == 8 else (chips, PACKED // n, LANES)
    return pl.pallas_call(
        functools.partial(kernel, n, lats, kinds, lat_windows, level_windows, lon_windows),
        grid=(kinds,),
        in_specs=[
            whole(perm),
            whole(back),
            anywhere,
            anywhere,
            whole(wqkv),
            whole(wback),
            whole(wproj),
            pl.BlockSpec((1, stack, LANES), lambda i: (i, 0, 0)),
            pl.BlockSpec((1, WTOK, LANES), lambda i: (i, 0, 0)),
        ],
        out_specs=[
            const((channels, 3 * channels)),
            const((channels, channels)),
            anywhere,
            anywhere,
        ],
        out_shape=[
            jax.ShapeDtypeStruct((channels, 3 * channels), F32),
            jax.ShapeDtypeStruct((channels, channels), F32),
            jax.ShapeDtypeStruct((kinds, PACKED, LANES), BF16),
            jax.ShapeDtypeStruct(normed.shape, BF16),
        ],
        scratch_shapes=[
            pltpu.VMEM((lon_windows, padded, channels), BF16),
            pltpu.VMEM((lon_windows, padded, channels), BF16),
            pltpu.VMEM((lon_windows, channels, padded), BF16),
            pltpu.VMEM((lon_windows, channels, padded), BF16),
            pltpu.VMEM((lon_windows, channels, WTOK), BF16),
            pltpu.VMEM((lon_windows, channels, WTOK), BF16),
            pltpu.VMEM((lon_windows, WTOK, padded), BF16),
            pltpu.VMEM((lon_windows, WTOK, padded), BF16),
            pltpu.VMEM((WTOK, padded), F32),
            pltpu.VMEM((channels, turned), BF16),
            pltpu.VMEM((channels, turned), BF16),
            pltpu.VMEM((3, channels, channels), F32),
            pltpu.VMEM((channels, channels), F32),
            pltpu.VMEM((kinds, PACKED, LANES), BF16),
            pltpu.VMEM((kinds, PACKED // 2, LANES), BF16),
            pltpu.VMEM((kinds, PACKED // 2, LANES), BF16),
            pltpu.VMEM((kinds,) + arriving, BF16),
            pltpu.VMEM((kinds, 2, PACKED // 8, LANES), BF16),
            pltpu.VMEM((kinds, 2, PACKED // 16, LANES), BF16),
            pltpu.VMEM((kinds, PACKED, LANES), BF16),
            pltpu.VMEM((n,) + wgrad, BF16),
            pltpu.VMEM((n,) + wgrad, BF16),
            pltpu.VMEM((lats,) + wgrad, BF16),
            pltpu.VMEM((n,) + wgrad, BF16),
            pltpu.VMEM((2, levels, height + shift, breadth, channels), BF16),
            pltpu.VMEM((2, levels, height, HALO, channels), BF16),
            pltpu.VMEM((levels, height + shift, breadth, channels), BF16),
            pltpu.VMEM((levels, height, HALO, channels), BF16),
            pltpu.VMEM((levels, height, HALO, channels), BF16),
            pltpu.VMEM((levels, shift, breadth, channels), BF16),
            *exchange_sems,
            sem(3),
            pltpu.SemaphoreType.DMA((2, lat_windows)),
            sem(2, lat_windows + 1, 3),
            sem(2),
            sem(lat_windows + 1),
            sem(),
            pltpu.SemaphoreType.DMA((lat_windows + 1,)),
        ],
        compiler_params=pltpu.CompilerParams(
            dimension_semantics=("arbitrary",),
            vmem_limit_bytes=56 * 2**20,
            collective_id=0,
            has_side_effects=True,
        ),
        cost_estimate=pl.CostEstimate(
            flops=kinds * 1_500_000_000, bytes_accessed=kinds * 2_000_000, transcendentals=0
        ),
    )(
        perm, back, normed, cotangent, wqkv, wback, wproj, bias, side
    )


def frame_order(breadth, lon_windows):
    rows = np.arange(lon_windows * WTOK)
    mains = lon_windows * LANES
    is_main = rows < mains
    window = np.where(is_main, rows // LANES, (rows - mains) // TAIL)
    token = np.where(is_main, rows % LANES, LANES + (rows - mains) % TAIL)
    per_level = WIN_LAT * WIN_LON
    level = token // per_level
    row = token % per_level // WIN_LON
    place = window * WIN_LON + token % WIN_LON + WIN_LON // 2
    near, far = WIN_LAT * breadth, WIN_LAT * HALO
    source = np.where(
        place < breadth,
        level * near + row * breadth + place,
        WIN_Z * near + level * far + row * HALO + place - breadth,
    )
    columns = np.arange(WIN_Z * (near + far))
    return (source[:, None] == columns[None, :]).astype(np.float32)


def local(normed, cotangent, weight_qkv, weight_proj, bias_table):
    breadth = normed.shape[2]
    lon_windows = breadth // WIN_LON
    bias, side = pack(jnp.swapaxes(bias_table, 0, 1))
    bias = bias.reshape(bias.shape[0], HEADS * WTOK, LANES)
    wqkv = jnp.stack(jnp.split(weight_qkv, 3, axis=1))
    wback = jnp.swapaxes(wqkv, 1, 2)
    wproj = weight_proj.T

    perm = frame_order(breadth, lon_windows)
    gqkv, gproj, packed, input_grad = window_call(
        jnp.asarray(perm, BF16), jnp.asarray(perm.T, BF16),
        normed, cotangent, wqkv, wback, wproj, bias, side,
    )
    bias_grad = jnp.swapaxes(unpack(packed), 0, 1)
    return input_grad, gqkv, gproj, bias_grad


def solution(mesh):
    in_specs = (
        P(None, "lat", "lon", None),
        P(None, "lat", "lon", None),
        P(),
        P(),
        P("lat", None, None),
    )
    out_specs = (P(None, "lat", "lon", None), P(), P(), P("lat", None, None))
    return jax.shard_map(local, mesh=mesh, in_specs=in_specs, out_specs=out_specs, check_vma=False)
```

time: 169 us -> 125 us (0.74)
  Pallas kernels: 146 us -> 116 us
  local copies, waits for them, and re-layouts: 17.7 us -> 6.82 us
  other arithmetic: 3.48 us -> 0.78 us
    pallas_call x1, Pallas kernels: 23.4 us -> 8.76 us  [pack(): pl.pallas_call(pack_kernel, grid=(heads,), in_specs=[pl.BlockSpec((1, kin...]
    pallas_call x1, Pallas kernels: 107 us -> 96.7 us  [window_call(): pl.pallas_call(functools.partial(kernel, n, lats, kinds, lat_windows, lev...]
    unnamed x8 -> x13, local copies, waits for them, and re-layouts: 13.3 us -> 4.81 us
    pallas_call x1, Pallas kernels: 15.9 us -> 10.7 us  [unpack(): pl.pallas_call(unpack_kernel, grid=(HEADS,), in_specs=[pl.BlockSpec((kind...]
where the time goes in v3:
time: 125 us; the launch traced here: 124 us
  Pallas kernels  116 us (93%)
  local copies, waits for them, and re-layouts  6.82 us (5%)
    pallas_call x1, Pallas kernels, window_call(): pl.pallas_call(functools.partial(kernel, n, lats, kinds, lat_windows, lev...  96.7 us
    pallas_call x1, Pallas kernels, unpack(): pl.pallas_call(unpack_kernel, grid=(HEADS,), in_specs=[pl.BlockSpec((kind...  10.7 us
    pallas_call x1, Pallas kernels, pack(): pl.pallas_call(pack_kernel, grid=(heads,), in_specs=[pl.BlockSpec((1, kin...  8.76 us
    unnamed x13, local copies, waits for them, and re-layouts  4.81 us

profile of v3, /device:TPU:0, one launch (start us, length us, event | category | flops | bytes accessed | tf_op | source)
XLA Modules:
  0.0 124.4 jit_solution(13790555562770581886)
XLA Ops:
  0.6 1.6 %copy.14 = bf16[192,192]{0,1:T(8,128)(2,1)} copy(bf16[192,192]{1,0:T(8,128)(2,1)} %param.10) | data formatting | bytes 147456 | tf_op args[3]
  2.3 1.1 fusion.1
  3.4 0.1 copy.16
  3.5 0.1 copy.17
  3.6 0.1 copy.18
  3.7 0.8 fusion
  4.5 0.9 copy.15.wqkv_ref
  5.4 8.8 %shard_map.102 = (bf16[16,6,144,128]{3,2,1,0:T(8,128)(2,1)}, bf16[16,144,128]{2,1,0:T(8,128)(2,1)}) custom-call(bf16[6,16,20736]{2,1,0:T(8,128)(2,1)} %bitcast.13), custom_call_target="tpu_custom_call" | custom-call | flops 10000000000 | bytes 10000000 | tf_op jit(solution)/shard_map/pallas_call | solution.py:883
  14.1 96.7 %shard_map.103 = (f32[192,576]{1,0:T(8,128)}, f32[192,192]{1,0:T(8,128)}, bf16[16,1024,128]{2,1,0:T(8,128)(2,1)}, bf16[8,24,24,192]{3,2,1,0:T(8,128)(2,1)}) custom-call(bf16[288,384]{1,0:T(8,128)(2,1)} %constant.4.clone.perm_ref, bf16[384,288]{1,0:T(8,128)(2,1)} %constant.5.clone.back_ref, bf16[8,24,24,192]{3,2,1,0:T(8,128)(2,1)} %x_hbm.1, ...), custom_call_target="tpu_custom_call" | custom-call | flops 24000000000 | bytes 32000000 | tf_op jit(solution)/shard_map/pallas_call | solution.py:985
  110.8 0.0 copy-start
  110.9 10.7 %shard_map.104 = f32[6,16,20736]{2,1,0:T(8,128)} custom-call(bf16[16,1024,128]{2,1,0:T(8,128)(2,1)} %get-tuple-element.15.main_ref.tail_ref, bf16[16,1024,128]{2,1,0:T(8,128)(2,1)} %get-tuple-element.15.main_ref.tail_ref), custom_call_target="tpu_custom_call" | custom-call | flops 10000000000 | bytes 15000000 | tf_op jit(solution)/shard_map/pallas_call | solution.py:944
  121.5 0.0 copy-start.1
  121.5 0.0 copy-start.2
  121.5 0.0 copy-done
  121.5 1.4 %copy.22 = bf16[8,24,24,192]{3,2,1,0:T(8,128)(2,1)} copy(bf16[8,24,24,192]{3,2,1,0:T(8,128)(2,1)S(1)} %copy-done) | data formatting | bytes 3538944
  122.9 0.0 copy-done.1
  122.9 0.8 copy.23
  123.7 0.0 copy-done.2
  123.7 0.7 copy.24
Async XLA Ops:
  110.8 10.7 %copy-start = (bf16[8,24,24,192]{3,2,1,0:T(8,128)(2,1)S(1)}, bf16[8,24,24,192]{3,2,1,0:T(8,128)(2,1)}, u32[]{:S(2)}) copy-start(bf16[8,24,24,192]{3,2,1,0:T(8,128)(2,1)} %get-tuple-element.25) | copy-start | bytes 5308420
  121.5 1.4 %copy-start.1 = (f32[192,576]{1,0:T(8,128)S(1)}, f32[192,576]{1,0:T(8,128)}, u32[]{:S(2)}) copy-start(f32[192,576]{1,0:T(8,128)} %get-tuple-element.26) | copy-start | bytes 1327108
  121.5 2.2 %copy-start.2 = (f32[192,192]{1,0:T(8,128)S(1)}, f32[192,192]{1,0:T(8,128)}, u32[]{:S(2)}) copy-start(f32[192,192]{1,0:T(8,128)} %get-tuple-element.27) | copy-start | bytes 442372

commit v4 on v3

--- a/solution.py
+++ b/solution.py
@@ -20,7 +20,7 @@
 PACKED = 1024
 GRAD_LAG = 2
 LAGS = (1, 3, 5, 7, 9, 10)
-UNROLL = 3
+UNROLL = 6
 ODD = WTOK + 1
 LOG2E = math.log2(math.e)
 F32 = jnp.float32
@@ -480,7 +480,7 @@
             device_id={"lat": lax.rem(lat + o + lats, lats), "lon": lax.rem(me + o + n, n)},
             device_id_type=pl.DeviceIdType.MESH,
         )
-    pl.semaphore_wait(barrier, n + lats)
+    return lambda: pl.semaphore_wait(barrier, n + lats)
 
 
 class WeightSum:
@@ -529,6 +529,58 @@
         self.every(self.w1, self.n, 0).wait_send()
         self.every(self.w2, self.lats, 1).wait_send()
         self.every(self.wout, self.n, 2).wait_send()
+
+
+class Pack:
+    def __init__(self, table, rows, sems, bias, side, main, tail):
+        self.table, self.rows, self.sems = table, rows, sems
+        self.bias, self.side, self.main, self.tail = bias, side, main, tail
+        self.kinds = bias.shape[0]
+
+    def load(self, h):
+        return pltpu.make_async_copy(self.table.at[h], self.rows.at[h], self.sems.at[h])
+
+    def begin(self):
+        for h in range(HEADS):
+            self.load(h).start()
+
+    def head(self, h, _):
+        self.load(h).wait()
+        group = LANES // TAIL
+        kinds = self.kinds
+        lane = lax.broadcasted_iota(jnp.int32, (kinds, LANES), 1)
+
+        def body(m):
+            tiles = []
+            for r in range(group + 1):
+                start = pl.multiple_of(m * (group * WTOK) + r * LANES, LANES)
+                tiles.append(self.rows[h, :, pl.ds(start, LANES)].astype(F32))
+            for r in range(group):
+                turn = (LANES - TAIL * r) % LANES
+                left = pltpu.roll(tiles[r], turn, 1) if r else tiles[r]
+                right = pltpu.roll(tiles[r + 1], turn, 1) if r else tiles[r + 1]
+                whole = jnp.where(lane < LANES - TAIL * r, left, right) if r else left
+                at = pl.ds(m * group + r, kinds, stride=ODD)
+                self.main[at, :] = whole
+                self.tail[at, :] = right
+
+        def several(i, _):
+            for u in range(UNROLL):
+                body(i * UNROLL + u)
+            return 0
+
+        lax.fori_loop(0, WTOK // group // UNROLL, several, 0)
+        wide = lax.broadcasted_iota(jnp.int32, (WTOK, LANES), 1) // TAIL
+        for t in range(kinds):
+            at = slice(t * ODD, t * ODD + WTOK)
+            self.bias[t, pl.ds(pl.multiple_of(h * WTOK, WTOK), WTOK)] = self.main[at, :].astype(BF16)
+            turned = pltpu.roll(self.tail[at, :], h * TAIL, 1)
+            before = jnp.where(h == 0, 0.0, self.side[t].astype(F32))
+            self.side[t] = jnp.where(wide == h, turned, before).astype(BF16)
+        return 0
+
+    def heads(self, lo, hi):
+        lax.fori_loop(lo, hi, self.head, 0)
 
 
 def flip(mains, under, right, corner):
@@ -561,10 +613,8 @@
     x_hbm,
     c_hbm,
     wqkv_ref,
-    wback_ref,
     wproj_ref,
-    bias_ref,
-    side_ref,
+    table_hbm,
     gqkv_ref,
     gproj_ref,
     gbias_hbm,
@@ -599,6 +649,15 @@
     gh_s,
     wh_s,
     nh_s,
+    rows_s,
+    bias_s,
+    side_s,
+    flat_s,
+    flat_tail_s,
+    wqkv_s,
+    wback_s,
+    wproj_s,
+    rows_sem,
     pair_sem,
     cross_sem,
     back_sem,
@@ -615,7 +674,7 @@
     step = pl.program_id(0)
     a = lax.rem(step, level_windows)
     b = step // level_windows
-    channels = wqkv_ref.shape[1]
+    channels = wqkv_ref.shape[0]
     head_dim = channels // HEADS
     scale = head_dim ** -0.5
     levels = x_hbm.shape[0]
@@ -638,9 +697,19 @@
 
     @pl.when(step == 0)
     def _():
+        table = Pack(table_hbm, rows_s, rows_sem, bias_s, side_s, flat_s, flat_tail_s)
+        table.begin()
         halo.begin()
-        enter(n, lats)
+        entered = enter(n, lats)
+        for i in range(3):
+            part = wqkv_ref[:, i * channels : (i + 1) * channels]
+            wqkv_s[i] = part
+            wback_s[i] = part.T
+        wproj_s[...] = wproj_ref[...].T
+        table.heads(0, HEADS // 3)
+        entered()
         halo.send(0, lat_windows == 1)
+        table.heads(HEADS // 3, HEADS)
 
     halo.arrive(a, b)
 
@@ -657,10 +726,10 @@
     x_raw, c_raw = raw(0), raw(1)
     x = mm(perm, x_raw).astype(BF16)
     c = mm(perm, c_raw).astype(BF16)
-    q = (mm(x, wqkv_ref[0]) * (scale * LOG2E)).astype(BF16)
-    k = mm(x, wqkv_ref[1]).astype(BF16)
-    v = mm(x, wqkv_ref[2]).astype(BF16)
-    m = mm(c, wproj_ref[...]).astype(BF16)
+    q = (mm(x, wqkv_s[0]) * (scale * LOG2E)).astype(BF16)
+    k = mm(x, wqkv_s[1]).astype(BF16)
+    v = mm(x, wqkv_s[2]).astype(BF16)
+    m = mm(c, wproj_s[...]).astype(BF16)
 
     wrap_here = a == level_windows - 1
     dead_here = bottom & (lax.axis_index("lat") == lats - 1)
@@ -678,12 +747,12 @@
     mask_main = jnp.where(key_class == classes(lane), 0.0, -1e30)
     mask_tail = jnp.where(key_class == classes(LANES + lax.rem(lane, TAIL)), 0.0, -1e30)
 
-    table = lambda lo, rows: bias_ref[0, lo : lo + rows, :].astype(F32) * LOG2E
+    table = lambda lo, rows: bias_s[step, lo : lo + rows, :].astype(F32) * LOG2E
     mains_t, under_t, right_t, corner_t = flip(
         [table(h * WTOK, LANES) for h in range(HEADS)],
         [table(h * WTOK + LANES, TAIL) for h in range(HEADS)],
-        side_ref[0, :LANES, :].astype(F32) * LOG2E,
-        side_ref[0, LANES:, :].astype(F32) * LOG2E,
+        side_s[step, :LANES, :].astype(F32) * LOG2E,
+        side_s[step, LANES:, :].astype(F32) * LOG2E,
     )
     for h in range(HEADS):
         cols = slice(h * LANES, (h + 1) * LANES)
@@ -771,7 +840,7 @@
     for i in range(3):
         gqkv_s[i] += mm(xt, cols[i])
     gproj_s[...] += mm(mix_s[:, :tokens], c)
-    gin = mm(cols[0], wback_ref[0]) + mm(cols[1], wback_ref[1]) + mm(cols[2], wback_ref[2])
+    gin = mm(cols[0], wback_s[0]) + mm(cols[1], wback_s[1]) + mm(cols[2], wback_s[2])
     gout = mm(back_ref[...], gin.astype(BF16)).astype(BF16)
     near, far = WIN_LAT * breadth, WIN_LAT * HALO
     for u, z in enumerate(halo.pair(a)):
@@ -780,6 +849,18 @@
         gl_s[z, rows] = own.reshape(WIN_LAT, breadth, channels)
         strip = gout[WIN_Z * near + u * far : WIN_Z * near + (u + 1) * far]
         gh_s[z, pl.ds(b * WIN_LAT, WIN_LAT)] = strip.reshape(WIN_LAT, HALO, channels)
+
+    ws = WeightSum(n, lats, wg_s, w1_s, w2_s, w3_s, w_sem)
+    share = channels // n
+
+    @pl.when(step == kinds - 1)
+    def _():
+        for i in range(n):
+            rows = slice(i * share, (i + 1) * share)
+            for j in range(3):
+                wg_s[i, j * share : (j + 1) * share, :] = gqkv_s[j, rows].astype(BF16)
+            wg_s[i, 3 * share :, :] = gproj_s[rows].astype(BF16)
+        ws.start()
 
     @pl.when((a == level_windows - 1) & (b < lat_windows - 1))
     def _():
@@ -815,14 +896,6 @@
 
     @pl.when(step == kinds - 1)
     def _():
-        share = channels // n
-        for i in range(n):
-            rows = slice(i * share, (i + 1) * share)
-            for j in range(3):
-                wg_s[i, j * share : (j + 1) * share, :] = gqkv_s[j, rows].astype(BF16)
-            wg_s[i, 3 * share :, :] = gproj_s[rows].astype(BF16)
-        ws = WeightSum(n, lats, wg_s, w1_s, w2_s, w3_s, w_sem)
-        ws.start()
         halo.give_last()
         for turn, _ in enumerate(ex.rest()):
             if turn == 1:
@@ -843,70 +916,18 @@
         halo.end()
 
 
-def pack_kernel(table_ref, main_ref, tail_ref, main_s, tail_s):
-    h = pl.program_id(0)
-    kinds = table_ref.shape[1]
-    group = LANES // TAIL
-    lane = lax.broadcasted_iota(jnp.int32, (kinds, LANES), 1)
-
-    def body(m):
-        tiles = []
-        for r in range(group + 1):
-            start = pl.multiple_of(m * (group * WTOK) + r * LANES, LANES)
-            tiles.append(table_ref[0, :, pl.ds(start, LANES)].astype(F32))
-        for r in range(group):
-            turn = (LANES - TAIL * r) % LANES
-            left = pltpu.roll(tiles[r], turn, 1) if r else tiles[r]
-            right = pltpu.roll(tiles[r + 1], turn, 1) if r else tiles[r + 1]
-            whole = jnp.where(lane < LANES - TAIL * r, left, right) if r else left
-            at = pl.ds(m * group + r, kinds, stride=ODD)
-            main_s[at, :] = whole
-            tail_s[at, :] = right
-
-    def several(i, _):
-        for u in range(UNROLL):
-            body(i * UNROLL + u)
-        return 0
-
-    lax.fori_loop(0, WTOK // group // UNROLL, several, 0)
-    wide = lax.broadcasted_iota(jnp.int32, (WTOK, LANES), 1) // TAIL
-    for t in range(kinds):
-        at = slice(t * ODD, t * ODD + WTOK)
-        main_ref[t, 0] = main_s[at, :].astype(BF16)
-        turned = pltpu.roll(tail_s[at, :], h * TAIL, 1)
-        before = jnp.where(h == 0, 0.0, tail_ref[t].astype(F32))
-        tail_ref[t] = jnp.where(wide == h, turned, before).astype(BF16)
-
-
-def pack(table):
-    heads, kinds, flat = table.shape
-    main, tail = pl.pallas_call(
-        pack_kernel,
-        grid=(heads,),
-        in_specs=[pl.BlockSpec((1, kinds, flat), lambda i: (i, 0, 0))],
-        out_specs=[
-            pl.BlockSpec((kinds, 1, WTOK, LANES), lambda i: (0, i, 0, 0)),
-            pl.BlockSpec((kinds, WTOK, LANES), lambda i: (0, 0, 0)),
-        ],
-        out_shape=[
-            jax.ShapeDtypeStruct((kinds, heads, WTOK, LANES), BF16),
-            jax.ShapeDtypeStruct((kinds, WTOK, LANES), BF16),
-        ],
-        scratch_shapes=[pltpu.VMEM((kinds * ODD, LANES), F32)] * 2,
-        cost_estimate=pl.CostEstimate(
-            flops=10_000_000_000, bytes_accessed=10_000_000, transcendentals=0
-        ),
-    )(table)
-    return main, tail
-
-
 def unpack_kernel(main_ref, tail_ref, out_ref, main_s, tail_s):
     h = pl.program_id(0)
     kinds = main_ref.shape[0]
     for t in range(kinds):
         at = slice(t * ODD, t * ODD + WTOK)
         main_s[at, :] = main_ref[t].astype(F32)
-        tail_s[at, :] = pltpu.roll(tail_ref[t].astype(F32), (HEADS - h) * TAIL + LANES - HEADS * TAIL, 1)
+
+    @pl.when(h == 0)
+    def _():
+        for t in range(kinds):
+            tail_s[t * ODD : t * ODD + WTOK, :] = tail_ref[t].astype(F32)
+
     group = LANES // TAIL
     lane = lax.broadcasted_iota(jnp.int32, (kinds, LANES), 1)
 
@@ -919,7 +940,7 @@
                 here_main, here_tail = main_s[at, :], tail_s[at, :]
                 if r:
                     here_main = pltpu.roll(here_main, TAIL * r, 1)
-                    here_tail = pltpu.roll(here_tail, TAIL * r, 1)
+                here_tail = pltpu.roll(here_tail, lax.rem(LANES + TAIL * (r - h), LANES), 1)
                 tile = here_main
             if r:
                 ended = before_tail
@@ -957,7 +978,7 @@
     )(packed, packed)
 
 
-def window_call(perm, back, normed, cotangent, wqkv, wback, wproj, bias, side):
+def window_call(perm, back, normed, cotangent, wqkv, wproj, table):
     levels, height, breadth, channels = normed.shape
     level_windows = levels // WIN_Z
     lat_windows = height // WIN_LAT
@@ -991,10 +1012,8 @@
             anywhere,
             anywhere,
             whole(wqkv),
-            whole(wback),
             whole(wproj),
-            pl.BlockSpec((1, stack, LANES), lambda i: (i, 0, 0)),
-            pl.BlockSpec((1, WTOK, LANES), lambda i: (i, 0, 0)),
+            anywhere,
         ],
         out_specs=[
             const((channels, 3 * channels)),
@@ -1039,6 +1058,15 @@
             pltpu.VMEM((levels, height, HALO, channels), BF16),
             pltpu.VMEM((levels, height, HALO, channels), BF16),
             pltpu.VMEM((levels, shift, breadth, channels), BF16),
+            pltpu.VMEM(table.shape, BF16),
+            pltpu.VMEM((kinds, stack, LANES), BF16),
+            pltpu.VMEM((kinds, WTOK, LANES), BF16),
+            pltpu.VMEM((kinds * ODD, LANES), F32),
+            pltpu.VMEM((kinds * ODD, LANES), F32),
+            pltpu.VMEM((3, channels, channels), BF16),
+            pltpu.VMEM((3, channels, channels), BF16),
+            pltpu.VMEM((channels, channels), BF16),
+            dma((HEADS,)),
             *exchange_sems,
             sem(3),
             pltpu.SemaphoreType.DMA((2, lat_windows)),
@@ -1050,7 +1078,7 @@
         ],
         compiler_params=pltpu.CompilerParams(
             dimension_semantics=("arbitrary",),
-            vmem_limit_bytes=56 * 2**20,
+            vmem_limit_bytes=62 * 2**20,
             collective_id=0,
             has_side_effects=True,
         ),
@@ -1058,7 +1086,7 @@
             flops=kinds * 1_500_000_000, bytes_accessed=kinds * 2_000_000, transcendentals=0
         ),
     )(
-        perm, back, normed, cotangent, wqkv, wback, wproj, bias, side
+        perm, back, normed, cotangent, wqkv, wproj, table
     )
 
 
@@ -1085,16 +1113,10 @@
 def local(normed, cotangent, weight_qkv, weight_proj, bias_table):
     breadth = normed.shape[2]
     lon_windows = breadth // WIN_LON
-    bias, side = pack(jnp.swapaxes(bias_table, 0, 1))
-    bias = bias.reshape(bias.shape[0], HEADS * WTOK, LANES)
-    wqkv = jnp.stack(jnp.split(weight_qkv, 3, axis=1))
-    wback = jnp.swapaxes(wqkv, 1, 2)
-    wproj = weight_proj.T
-
     perm = frame_order(breadth, lon_windows)
     gqkv, gproj, packed, input_grad = window_call(
         jnp.asarray(perm, BF16), jnp.asarray(perm.T, BF16),
-        normed, cotangent, wqkv, wback, wproj, bias, side,
+        normed, cotangent, weight_qkv, weight_proj, jnp.swapaxes(bias_table, 0, 1),
     )
     bias_grad = jnp.swapaxes(unpack(packed), 0, 1)
     return input_grad, gqkv, gproj, bias_grad

time: 125 us -> 112 us (0.90)
  Pallas kernels: 116 us -> 108 us
  local copies, waits for them, and re-layouts: 6.82 us -> 2.87 us
    pallas_call x1 -> x0, Pallas kernels: 8.76 us -> none  [pack(): pl.pallas_call(pack_kernel, grid=(heads,), in_specs=[pl.BlockSpec((1, kin...]
    unnamed x13 -> x9, local copies, waits for them, and re-layouts: 4.81 us -> 2.87 us
    pallas_call x1, Pallas kernels: 96.7 us -> 98.5 us  [window_call(): pl.pallas_call(functools.partial(kernel, n, lats, kinds, lat_windows, lev...]
    pallas_call x1, Pallas kernels: 10.7 us -> 9.25 us  [unpack(): pl.pallas_call(unpack_kernel, grid=(HEADS,), in_specs=[pl.BlockSpec((kind...]
where the time goes in v4:
time: 112 us; the launch traced here: 111 us
  Pallas kernels  108 us (96%)
  local copies, waits for them, and re-layouts  2.87 us (3%)
    pallas_call x1, Pallas kernels, window_call(): pl.pallas_call(functools.partial(kernel, n, lats, kinds, lat_windows, lev...  98.5 us
    pallas_call x1, Pallas kernels, unpack(): pl.pallas_call(unpack_kernel, grid=(HEADS,), in_specs=[pl.BlockSpec((kind...  9.25 us
    unnamed x9, local copies, waits for them, and re-layouts  2.87 us

profile of v4, /device:TPU:0, one launch (start us, length us, event | category | flops | bytes accessed | tf_op | source)
XLA Modules:
  0.0 111.3 jit_solution(16692208617380862551)
XLA Ops:
  0.6 98.5 %shard_map.102 = (f32[192,576]{1,0:T(8,128)}, f32[192,192]{1,0:T(8,128)}, bf16[16,1024,128]{2,1,0:T(8,128)(2,1)}, bf16[8,24,24,192]{3,2,1,0:T(8,128)(2,1)}) custom-call(bf16[288,384]{1,0:T(8,128)(2,1)} %constant.4.clone.perm_ref, bf16[384,288]{1,0:T(8,128)(2,1)} %constant.5.clone.back_ref, bf16[8,24,24,192]{3,2,1,0:T(8,128)(2,1)} %x_hbm.1, ...), custom_call_target="tpu_custom_call" | custom-call | flops 24000000000 | bytes 32000000 | tf_op jit(solution)/shard_map/pallas_call | solution.py:1006
  99.2 0.0 copy-start
  99.2 9.3 %shard_map.103 = f32[6,16,20736]{2,1,0:T(8,128)} custom-call(bf16[16,1024,128]{2,1,0:T(8,128)(2,1)} %get-tuple-element.11.main_ref.tail_ref, bf16[16,1024,128]{2,1,0:T(8,128)(2,1)} %get-tuple-element.11.main_ref.tail_ref), custom_call_target="tpu_custom_call" | custom-call | flops 10000000000 | bytes 15000000 | tf_op jit(solution)/shard_map/pallas_call | solution.py:965
  108.4 0.0 copy-done
  108.4 0.0 copy-start.1
  108.4 0.0 copy-start.2
  108.5 1.4 %copy.14 = bf16[8,24,24,192]{3,2,1,0:T(8,128)(2,1)} copy(bf16[8,24,24,192]{3,2,1,0:T(8,128)(2,1)S(1)} %copy-done) | data formatting | bytes 3538944
  109.9 0.0 copy-done.1
  109.9 0.8 copy.15
  110.6 0.0 copy-done.2
  110.6 0.7 copy.16
Async XLA Ops:
  99.2 9.3 %copy-start = (bf16[8,24,24,192]{3,2,1,0:T(8,128)(2,1)S(1)}, bf16[8,24,24,192]{3,2,1,0:T(8,128)(2,1)}, u32[]{:S(2)}) copy-start(bf16[8,24,24,192]{3,2,1,0:T(8,128)(2,1)} %get-tuple-element.16) | copy-start | bytes 5308420
  108.4 1.4 %copy-start.1 = (f32[192,576]{1,0:T(8,128)S(1)}, f32[192,576]{1,0:T(8,128)}, u32[]{:S(2)}) copy-start(f32[192,576]{1,0:T(8,128)} %get-tuple-element.17) | copy-start | bytes 1327108
  108.4 2.2 %copy-start.2 = (f32[192,192]{1,0:T(8,128)S(1)}, f32[192,192]{1,0:T(8,128)}, u32[]{:S(2)}) copy-start(f32[192,192]{1,0:T(8,128)} %get-tuple-element.18) | copy-start | bytes 442372

commit v5 on v4

--- a/solution.py
+++ b/solution.py
@@ -20,7 +20,7 @@
 PACKED = 1024
 GRAD_LAG = 2
 LAGS = (1, 3, 5, 7, 9, 10)
-UNROLL = 6
+UNROLL = 9
 ODD = WTOK + 1
 LOG2E = math.log2(math.e)
 F32 = jnp.float32
@@ -123,7 +123,7 @@
         return [self.stage_pair, self.stage_cross, self.stage_back, self.stage_fwd]
 
     def behind(self, step):
-        for lag, stage in zip(LAGS, self.stages()):
+        for lag, stage in reversed(list(zip(LAGS, self.stages()))):
             t = step - lag
             if isinstance(t, int):
                 if 0 <= t < self.kinds:
@@ -484,11 +484,16 @@
 
 
 class WeightSum:
-    def __init__(self, n, lats, wg, w1, w2, wout, sems):
-        self.n, self.lats = n, lats
-        self.wg, self.w1, self.w2, self.wout = wg, w1, w2, wout
+    def __init__(self, n, lats, wg, wp, wc, w1, w2, wout, sems):
+        self.n, self.lats, self.chips = n, lats, n // 2
+        self.wg, self.wp, self.wc = wg, wp, wc
+        self.w1, self.w2, self.wout = w1, w2, wout
         self.sems = sems
-        self.me, self.lat = lax.axis_index("lon"), lax.axis_index("lat")
+        me, self.lat = lax.axis_index("lon"), lax.axis_index("lat")
+        self.core, self.chip = lax.rem(me, 2), me // 2
+        self.partner = me + 1 - 2 * self.core
+        self.mine = pl.ds(self.core * self.chips, self.chips)
+        self.theirs = pl.ds((1 - self.core) * self.chips, self.chips)
 
     def remote(self, src, dst, k, device):
         return pltpu.make_async_remote_copy(
@@ -497,38 +502,54 @@
         )
 
     def every(self, buf, count, k):
-        part = buf.at[pl.ds(0, count - 1)]
-        return self.remote(part, part, k, {"lon": lax.rem(self.me + 1, self.n)})
+        part = buf.at[pl.ds(0, count)]
+        return self.remote(part, part, k, {"lon": self.partner})
+
+    def peers(self):
+        return [lax.rem(self.chip + o, self.chips) for o in range(1, self.chips)]
 
     def start(self):
-        for o in range(1, self.n):
-            p = lax.rem(self.me + o, self.n)
-            self.remote(self.wg.at[p], self.w1.at[self.me], 0, {"lon": p}).start()
-        self.w1[pl.ds(self.me, 1)] = self.wg[pl.ds(self.me, 1)]
+        self.remote(self.wg.at[self.theirs], self.wp, 0, {"lon": self.partner}).start()
+
+    def step_zero(self):
+        self.every(self.wp, self.chips, 0).wait_recv()
+        total = self.wg[self.mine].astype(F32) + self.wp[...].astype(F32)
+        self.wc[...] = total.astype(BF16)
+        self.w1[pl.ds(self.chip, 1)] = self.wc[pl.ds(self.chip, 1)]
+        for j in self.peers():
+            device = {"lon": j * 2 + self.core}
+            self.remote(self.wc.at[j], self.w1.at[self.chip], 1, device).start()
 
     def step_one(self):
-        self.every(self.w1, self.n, 0).wait_recv()
+        self.every(self.w1, self.chips - 1, 1).wait_recv()
         total = jnp.sum(self.w1[...].astype(F32), axis=0, keepdims=True)
         self.w2[pl.ds(self.lat, 1)] = total.astype(BF16)
         for o in range(1, self.lats):
             p = lax.rem(self.lat + o, self.lats)
             part = self.w2.at[self.lat]
-            self.remote(part, part, 1, {"lat": p}).start()
+            self.remote(part, part, 2, {"lat": p}).start()
 
     def step_two(self):
-        self.every(self.w2, self.lats, 1).wait_recv()
+        self.every(self.w2, self.lats - 1, 2).wait_recv()
         total = jnp.sum(self.w2[...].astype(F32), axis=0, keepdims=True)
-        self.wout[pl.ds(self.me, 1)] = total.astype(BF16)
-        for o in range(1, self.n):
-            p = lax.rem(self.me + o, self.n)
-            part = self.wout.at[self.me]
-            self.remote(part, part, 2, {"lon": p}).start()
+        at = self.core * self.chips + self.chip
+        self.wout[pl.ds(at, 1)] = total.astype(BF16)
+        for j in self.peers():
+            part = self.wout.at[at]
+            self.remote(part, part, 3, {"lon": j * 2 + self.core}).start()
+
+    def step_three(self):
+        self.every(self.w1, self.chips - 1, 3).wait_recv()
+        part = self.wout.at[self.mine]
+        self.remote(part, part, 4, {"lon": self.partner}).start()
 
     def finish(self):
-        self.every(self.wout, self.n, 2).wait_recv()
-        self.every(self.w1, self.n, 0).wait_send()
-        self.every(self.w2, self.lats, 1).wait_send()
-        self.every(self.wout, self.n, 2).wait_send()
+        self.every(self.wp, self.chips, 4).wait_recv()
+        self.every(self.wp, self.chips, 0).wait_send()
+        self.every(self.w1, self.chips - 1, 1).wait_send()
+        self.every(self.w2, self.lats - 1, 2).wait_send()
+        self.every(self.w1, self.chips - 1, 3).wait_send()
+        self.every(self.wp, self.chips, 4).wait_send()
 
 
 class Pack:
@@ -640,6 +661,8 @@
     half_s,
     red_s,
     wg_s,
+    wp_s,
+    wc_s,
     w1_s,
     w2_s,
     w3_s,
@@ -850,7 +873,7 @@
         strip = gout[WIN_Z * near + u * far : WIN_Z * near + (u + 1) * far]
         gh_s[z, pl.ds(b * WIN_LAT, WIN_LAT)] = strip.reshape(WIN_LAT, HALO, channels)
 
-    ws = WeightSum(n, lats, wg_s, w1_s, w2_s, w3_s, w_sem)
+    ws = WeightSum(n, lats, wg_s, wp_s, wc_s, w1_s, w2_s, w3_s, w_sem)
     share = channels // n
 
     @pl.when(step == kinds - 1)
@@ -897,14 +920,16 @@
     @pl.when(step == kinds - 1)
     def _():
         halo.give_last()
+        ws.step_zero()
         for turn, _ in enumerate(ex.rest()):
-            if turn == 1:
+            if turn == 0:
                 ws.step_one()
             if turn == 2:
+                ws.step_two()
                 halo.finish(lat_windows - 1, True)
                 halo.finish_top()
             if turn == 3:
-                ws.step_two()
+                ws.step_three()
         ws.finish()
         for p in range(n):
             rows = slice(p * share, (p + 1) * share)
@@ -1049,7 +1074,9 @@
             pltpu.VMEM((kinds, 2, PACKED // 16, LANES), BF16),
             pltpu.VMEM((kinds, PACKED, LANES), BF16),
             pltpu.VMEM((n,) + wgrad, BF16),
-            pltpu.VMEM((n,) + wgrad, BF16),
+            pltpu.VMEM((chips,) + wgrad, BF16),
+            pltpu.VMEM((chips,) + wgrad, BF16),
+            pltpu.VMEM((chips,) + wgrad, BF16),
             pltpu.VMEM((lats,) + wgrad, BF16),
             pltpu.VMEM((n,) + wgrad, BF16),
             pltpu.VMEM((2, levels, height + shift, breadth, channels), BF16),
@@ -1068,7 +1095,7 @@
             pltpu.VMEM((channels, channels), BF16),
             dma((HEADS,)),
             *exchange_sems,
-            sem(3),
+            sem(5),
             pltpu.SemaphoreType.DMA((2, lat_windows)),
             sem(2, lat_windows + 1, 3),
             sem(2),

time: 112 us -> 107 us (0.955)
  Pallas kernels: 108 us -> 103 us
    pallas_call x1, Pallas kernels: 98.5 us -> 94.2 us  [window_call(): pl.pallas_call(functools.partial(kernel, n, lats, kinds, lat_windows, lev...]
where the time goes in v5:
time: 107 us
  Pallas kernels  103 us (96%)
  local copies, waits for them, and re-layouts  2.87 us (3%)
    pallas_call x1, Pallas kernels, window_call(): pl.pallas_call(functools.partial(kernel, n, lats, kinds, lat_windows, lev...  94.2 us
    pallas_call x1, Pallas kernels, unpack(): pl.pallas_call(unpack_kernel, grid=(HEADS,), in_specs=[pl.BlockSpec((kind...  8.95 us
    unnamed x9, local copies, waits for them, and re-layouts  2.87 us

profile of v5, /device:TPU:0, one launch (start us, length us, event | category | flops | bytes accessed | tf_op | source)
XLA Modules:
  0.0 106.7 jit_solution(4085700282755698763)
XLA Ops:
  0.6 94.2 %shard_map.102 = (f32[192,576]{1,0:T(8,128)}, f32[192,192]{1,0:T(8,128)}, bf16[16,1024,128]{2,1,0:T(8,128)(2,1)}, bf16[8,24,24,192]{3,2,1,0:T(8,128)(2,1)}) custom-call(bf16[288,384]{1,0:T(8,128)(2,1)} %constant.4.clone.perm_ref, bf16[384,288]{1,0:T(8,128)(2,1)} %constant.5.clone.back_ref, bf16[8,24,24,192]{3,2,1,0:T(8,128)(2,1)} %x_hbm.1, ...), custom_call_target="tpu_custom_call" | custom-call | flops 24000000000 | bytes 32000000 | tf_op jit(solution)/shard_map/pallas_call | solution.py:1031
  94.8 0.0 copy-start
  94.8 9.0 %shard_map.103 = f32[6,16,20736]{2,1,0:T(8,128)} custom-call(bf16[16,1024,128]{2,1,0:T(8,128)(2,1)} %get-tuple-element.11.main_ref.tail_ref, bf16[16,1024,128]{2,1,0:T(8,128)(2,1)} %get-tuple-element.11.main_ref.tail_ref), custom_call_target="tpu_custom_call" | custom-call | flops 10000000000 | bytes 15000000 | tf_op jit(solution)/shard_map/pallas_call | solution.py:990
  103.8 0.0 copy-done
  103.8 0.0 copy-start.1
  103.8 0.0 copy-start.2
  103.8 1.4 %copy.14 = bf16[8,24,24,192]{3,2,1,0:T(8,128)(2,1)} copy(bf16[8,24,24,192]{3,2,1,0:T(8,128)(2,1)S(1)} %copy-done) | data formatting | bytes 3538944
  105.2 0.0 copy-done.1
  105.2 0.8 copy.15
  106.0 0.0 copy-done.2
  106.0 0.7 copy.16
Async XLA Ops:
  94.8 9.0 %copy-start = (bf16[8,24,24,192]{3,2,1,0:T(8,128)(2,1)S(1)}, bf16[8,24,24,192]{3,2,1,0:T(8,128)(2,1)}, u32[]{:S(2)}) copy-start(bf16[8,24,24,192]{3,2,1,0:T(8,128)(2,1)} %get-tuple-element.16) | copy-start | bytes 5308420
  103.8 1.4 %copy-start.1 = (f32[192,576]{1,0:T(8,128)S(1)}, f32[192,576]{1,0:T(8,128)}, u32[]{:S(2)}) copy-start(f32[192,576]{1,0:T(8,128)} %get-tuple-element.17) | copy-start | bytes 1327108
  103.8 2.2 %copy-start.2 = (f32[192,192]{1,0:T(8,128)S(1)}, f32[192,192]{1,0:T(8,128)}, u32[]{:S(2)}) copy-start(f32[192,192]{1,0:T(8,128)} %get-tuple-element.18) | copy-start | bytes 442372

commit v6 on v5

--- a/solution.py
+++ b/solution.py
@@ -606,7 +606,7 @@
 
 def flip(mains, under, right, corner):
     lane = lax.broadcasted_iota(jnp.int32, (TAIL, LANES), 1) // TAIL
-    spare = jnp.zeros((LANES - HEADS * TAIL, LANES), F32)
+    spare = jnp.zeros((LANES - HEADS * TAIL, LANES), right.dtype)
     mains_t = [block.T for block in mains]
     right_t = jnp.concatenate(under + [spare], axis=0).T
     turned = right.T
@@ -898,9 +898,9 @@
         halo.finish(b - 1, False)
 
     mains_t, under_t, right_t, corner_t = flip(
-        [gb[h][:LANES] for h in range(HEADS)],
-        [gb[h][LANES:] for h in range(HEADS)],
-        gb[HEADS][:LANES],
+        [gb[h][:LANES].astype(BF16) for h in range(HEADS)],
+        [gb[h][LANES:].astype(BF16) for h in range(HEADS)],
+        gb[HEADS][:LANES].astype(BF16),
         gb[HEADS][LANES:],
     )
     for h in range(HEADS):

time: 107 us -> 108 us (level)
  no operation moved by 1% of the time
where the time goes in v6:
time: 108 us; the launch traced here: 107 us
  Pallas kernels  103 us (95%)
  local copies, waits for them, and re-layouts  2.87 us (3%)
    pallas_call x1, Pallas kernels, window_call(): pl.pallas_call(functools.partial(kernel, n, lats, kinds, lat_windows, lev...  94.5 us
    pallas_call x1, Pallas kernels, unpack(): pl.pallas_call(unpack_kernel, grid=(HEADS,), in_specs=[pl.BlockSpec((kind...  8.95 us
    unnamed x9, local copies, waits for them, and re-layouts  2.87 us

profile of v6, /device:TPU:0, one launch (start us, length us, event | category | flops | bytes accessed | tf_op | source)
XLA Modules:
  0.0 107.0 jit_solution(16148583648741570626)
XLA Ops:
  0.6 94.5 %shard_map.102 = (f32[192,576]{1,0:T(8,128)}, f32[192,192]{1,0:T(8,128)}, bf16[16,1024,128]{2,1,0:T(8,128)(2,1)}, bf16[8,24,24,192]{3,2,1,0:T(8,128)(2,1)}) custom-call(bf16[288,384]{1,0:T(8,128)(2,1)} %constant.4.clone.perm_ref, bf16[384,288]{1,0:T(8,128)(2,1)} %constant.5.clone.back_ref, bf16[8,24,24,192]{3,2,1,0:T(8,128)(2,1)} %x_hbm.1, ...), custom_call_target="tpu_custom_call" | custom-call | flops 24000000000 | bytes 32000000 | tf_op jit(solution)/shard_map/pallas_call | solution.py:1031
  95.1 0.0 copy-start
  95.2 9.0 %shard_map.103 = f32[6,16,20736]{2,1,0:T(8,128)} custom-call(bf16[16,1024,128]{2,1,0:T(8,128)(2,1)} %get-tuple-element.11.main_ref.tail_ref, bf16[16,1024,128]{2,1,0:T(8,128)(2,1)} %get-tuple-element.11.main_ref.tail_ref), custom_call_target="tpu_custom_call" | custom-call | flops 10000000000 | bytes 15000000 | tf_op jit(solution)/shard_map/pallas_call | solution.py:990
  104.1 0.0 copy-done
  104.1 0.0 copy-start.1
  104.1 0.0 copy-start.2
  104.1 1.4 %copy.14 = bf16[8,24,24,192]{3,2,1,0:T(8,128)(2,1)} copy(bf16[8,24,24,192]{3,2,1,0:T(8,128)(2,1)S(1)} %copy-done) | data formatting | bytes 3538944
  105.5 0.0 copy-done.1
  105.5 0.8 copy.15
  106.3 0.0 copy-done.2
  106.3 0.7 copy.16
Async XLA Ops:
  95.1 9.0 %copy-start = (bf16[8,24,24,192]{3,2,1,0:T(8,128)(2,1)S(1)}, bf16[8,24,24,192]{3,2,1,0:T(8,128)(2,1)}, u32[]{:S(2)}) copy-start(bf16[8,24,24,192]{3,2,1,0:T(8,128)(2,1)} %get-tuple-element.16) | copy-start | bytes 5308420
  104.1 1.4 %copy-start.1 = (f32[192,576]{1,0:T(8,128)S(1)}, f32[192,576]{1,0:T(8,128)}, u32[]{:S(2)}) copy-start(f32[192,576]{1,0:T(8,128)} %get-tuple-element.17) | copy-start | bytes 1327108
  104.1 2.2 %copy-start.2 = (f32[192,192]{1,0:T(8,128)S(1)}, f32[192,192]{1,0:T(8,128)}, u32[]{:S(2)}) copy-start(f32[192,192]{1,0:T(8,128)} %get-tuple-element.18) | copy-start | bytes 442372
